TPU v7x, 128 devices: a whole 4x4x4 slice. The times are simulated.
128 devices in a mesh: ctx: 32 (over z, y, x_hi), dp: 4 (over x_lo, core).
Axes of the slice: x: 4 (x_hi: 2, x_lo: 2; x = x_hi * 2 + x_lo), y: 4, z: 4, core: 2. Of those that a mesh axis runs over, the one named last changes fastest.
Arguments:
- tokens: bfloat16 [8, 2048, 4096], P('dp', 'ctx'), may hold values from -6 to 6
- queries: bfloat16 [8, 2048, 2048], P('dp', 'ctx'), may hold values from -160 to 160
- d_attended: bfloat16 [8, 2048, 2048], P('dp', 'ctx'), may hold values from -6 to 6
- span_order: int32 [64], replicated, may hold values from 0 to 63, each once
- norm_gain: float32 [4096], replicated, may hold values from 0.1 to 1.9
- key_weight: bfloat16 [4096, 512], replicated, may hold values from -0.09375 to 0.09375
- value_weight: bfloat16 [4096, 512], replicated, may hold values from -0.09375 to 0.09375
Outputs:
- attended: bfloat16 [8, 2048, 2048], P('dp', 'ctx')
- grad_queries: bfloat16 [8, 2048, 2048], P('dp', 'ctx')
- grad_tokens: bfloat16 [8, 2048, 4096], P('dp', 'ctx')
- grad_key_weight: float32 [4096, 512], P(('ctx', 'dp'))
- grad_value_weight: float32 [4096, 512], P(('ctx', 'dp'))
- grad_gain: float32 [4096], P(('ctx', 'dp'))
All inputs are finite; a program needn't handle non-finite values.
Results may differ from a plain program's by a relative error of at most 0.025.
The roundings to bfloat16 on the way count: a program that leaves them out, or rounds other values in their place, can miss the bound.
Values may be sent and summed in bfloat16 or wider, within the bound.
A program may use at most 192 MiB of HBM per device.

v0:
```python
import math

import jax
import jax.numpy as jnp
from jax import lax
from jax.sharding import PartitionSpec as P

KV_HEADS = 4
HEAD_DIM = 128


ROPE_BASE = 500000.0
EPSILON = 1e-05


def side_by_side(arrays, axis, dim, along):
    both = jnp.concatenate(arrays, axis=along)
    out, at, done = (lax.all_gather(both, axis, axis=dim, tiled=True), 0, [])
    for a in arrays:
        done.append(lax.slice_in_dim(out, at, at + a.shape[along], axis=along))
        at += a.shape[along]
    return tuple(done)


def in_blocks(array, dim, count):
    lengths = array.shape
    blocks = array.reshape(*lengths[:dim], count, lengths[dim] // count, *lengths[dim + 1 :])
    return jnp.moveaxis(blocks, dim, 0)


def sent_and_summed(array, axis, dim):
    blocks = in_blocks(array, dim, lax.axis_size(axis))
    arrived = lax.all_to_all(blocks, axis, split_axis=0, concat_axis=0, tiled=True)
    return arrived.astype(jnp.float32).sum(axis=0)


def in_one_piece(arrays, axis, dim, along):
    widths = [a.shape[along] for a in arrays]
    both = jnp.concatenate(arrays, axis=along)
    out = sent_and_summed(both, axis, dim)
    return tuple(jnp.split(out, [sum(widths[:k]) for k in range(1, len(widths))], axis=along))


def sent_together(arrays, axis, dim, along):
    widths = [math.prod(a.shape[along:]) for a in arrays]
    both = jnp.concatenate(
        [a.reshape(*a.shape[:along], w) for a, w in zip(arrays, widths)], axis=along
    )
    out = lax.psum_scatter(both, axis, scatter_dimension=dim, tiled=True)
    blocks = jnp.split(out, [sum(widths[:k]) for k in range(1, len(widths))], axis=along)
    return tuple((b.reshape(*out.shape[:along], *a.shape[along:]) for a, b in zip(arrays, blocks)))


def positions(span_order, span_len):
    offsets = jnp.arange(span_len, dtype=jnp.int32)
    return (span_order[:, None] * span_len + offsets[None, :]).reshape(-1)


def rotation(token_pos, head_size):
    half_dim = head_size // 2
    frequency = ROPE_BASE ** (-2.0 * jnp.arange(half_dim, dtype=jnp.float32) / head_size)
    angles = token_pos.astype(jnp.float32)[:, None] * frequency[None, :]
    angles = jnp.concatenate([angles, angles], axis=1)
    return (jnp.cos(angles), jnp.sin(angles))


def rotate_half(values):
    half_dim = values.shape[-1] // 2
    return jnp.concatenate([-values[..., half_dim:], values[..., :half_dim]], axis=-1)


def rotate_back(values):
    half_dim = values.shape[-1] // 2
    return jnp.concatenate([values[..., half_dim:], -values[..., :half_dim]], axis=-1)


def normalize(tokens, norm_gain):
    widened = tokens.astype(jnp.float32)
    rms_scale = lax.rsqrt(jnp.mean(widened * widened, axis=-1, keepdims=True) + EPSILON)
    return ((widened * rms_scale * norm_gain).astype(jnp.bfloat16), rms_scale)


def project_keys(normed, key_weight, value_weight, cosine, sine_table, kv_heads, head_size):
    row_count = normed.shape[0]
    key_pre = jnp.dot(normed, key_weight, preferred_element_type=jnp.float32).reshape(
        row_count, kv_heads, head_size
    )
    rotated = key_pre * cosine[:, None, :] + rotate_half(key_pre) * sine_table[:, None, :]
    value_rows = jnp.dot(normed, value_weight, preferred_element_type=jnp.float32)
    return (
        rotated.reshape(row_count, kv_heads * head_size).astype(jnp.bfloat16),
        value_rows.astype(jnp.bfloat16),
    )


def attend_group(query_group, grad_group, key_group, value_group, causal_mask, score_scale):
    scores = (
        jnp.einsum("tgd,sd->gts", query_group, key_group, preferred_element_type=jnp.float32)
        * score_scale
    )
    scores = jnp.where(causal_mask[None], scores, -1e30)
    row_max = jnp.max(scores, axis=-1, keepdims=True)
    exponent = jnp.exp(scores - row_max)
    probability = exponent / jnp.sum(exponent, axis=-1, keepdims=True)
    probability_b = probability.astype(jnp.bfloat16)
    attended = jnp.einsum(
        "gts,sd->tgd", probability_b, value_group, preferred_element_type=jnp.float32
    ).astype(jnp.bfloat16)
    dprob = jnp.einsum("tgd,sd->gts", grad_group, value_group, preferred_element_type=jnp.float32)
    delta = jnp.sum(grad_group.astype(jnp.float32) * attended.astype(jnp.float32), axis=-1)
    dscores = (probability * (dprob - jnp.transpose(delta)[:, :, None])).astype(jnp.bfloat16)
    dquery = (
        jnp.einsum("gts,sd->tgd", dscores, key_group, preferred_element_type=jnp.float32)
        * score_scale
    ).astype(jnp.bfloat16)
    key_term = (
        jnp.einsum("gts,tgd->sd", dscores, query_group, preferred_element_type=jnp.float32)
        * score_scale
    )
    value_term = jnp.einsum(
        "gts,tgd->sd", probability_b, grad_group, preferred_element_type=jnp.float32
    )
    return (attended, dquery, key_term, value_term)


def attend_device(queries, grads, all_keys, all_values, query_pos, key_pos, kv_heads, head_size):
    row_count = queries.shape[0]
    group_size = queries.shape[1] // (kv_heads * head_size)
    group_width = group_size * head_size
    causal_mask = key_pos[None, :] <= query_pos[:, None]
    score_scale = head_size ** (-0.5)
    outputs = []
    for head_group in range(kv_heads):
        query_group = queries[:, head_group * group_width : (head_group + 1) * group_width].reshape(
            row_count, group_size, head_size
        )
        grad_group = grads[:, head_group * group_width : (head_group + 1) * group_width].reshape(
            row_count, group_size, head_size
        )
        key_group = all_keys[:, head_group * head_size : (head_group + 1) * head_size]
        value_group = all_values[:, head_group * head_size : (head_group + 1) * head_size]
        outputs.append(
            attend_group(query_group, grad_group, key_group, value_group, causal_mask, score_scale)
        )
    attended = jnp.concatenate(
        [item[0].reshape(row_count, group_width) for item in outputs], axis=1
    )
    dquery = jnp.concatenate([item[1].reshape(row_count, group_width) for item in outputs], axis=1)
    key_terms = jnp.concatenate([item[2] for item in outputs], axis=1)
    value_terms = jnp.concatenate([item[3] for item in outputs], axis=1)
    return (attended, dquery, key_terms, value_terms)


def finish_backward(
    tokens,
    normed,
    rms_scale,
    key_grad,
    value_grad,
    cosine,
    sine_table,
    norm_gain,
    key_weight,
    value_weight,
    kv_heads,
    head_size,
):
    row_count = tokens.shape[0]
    shaped = key_grad.reshape(row_count, kv_heads, head_size)
    key_pre_grad = (
        (shaped * cosine[:, None, :] + rotate_back(shaped * sine_table[:, None, :]))
        .reshape(row_count, kv_heads * head_size)
        .astype(jnp.bfloat16)
    )
    value_pre_grad = value_grad.astype(jnp.bfloat16)
    weight_key = jnp.dot(normed.T, key_pre_grad, preferred_element_type=jnp.float32)
    weight_value = jnp.dot(normed.T, value_pre_grad, preferred_element_type=jnp.float32)
    normed_grad = jnp.dot(key_pre_grad, key_weight.T, preferred_element_type=jnp.float32) + jnp.dot(
        value_pre_grad, value_weight.T, preferred_element_type=jnp.float32
    )
    widened = tokens.astype(jnp.float32)
    gain_part = jnp.sum(normed_grad * widened * rms_scale, axis=0)
    inner_mean = jnp.mean(normed_grad * norm_gain * widened, axis=-1, keepdims=True)
    grad_rows = (
        rms_scale * norm_gain * normed_grad - widened * rms_scale**3 * inner_mean
    ).astype(jnp.bfloat16)
    return (grad_rows, weight_key, weight_value, gain_part)


def body(tokens, queries, d_attended, span_order, norm_gain, key_weight, value_weight):
    local_seqs = tokens.shape[0]
    row_count = tokens.shape[1]
    model_width = tokens.shape[2]
    kv_width = key_weight.shape[1]
    shard_index = lax.axis_index("ctx")
    token_pos = positions(span_order, row_count // 2)
    query_pos = lax.dynamic_slice_in_dim(token_pos, shard_index * row_count, row_count, 0)
    cosine, sine_table = rotation(query_pos, HEAD_DIM)
    cosine_all = jnp.tile(cosine, (local_seqs, 1))
    sine_all = jnp.tile(sine_table, (local_seqs, 1))
    flat_tokens = tokens.reshape(local_seqs * row_count, model_width)
    normed, rms_scale = normalize(flat_tokens, norm_gain)
    rotated_keys, value_rows = project_keys(
        normed, key_weight, value_weight, cosine_all, sine_all, KV_HEADS, HEAD_DIM
    )
    rotated_keys = rotated_keys.reshape(local_seqs, row_count, kv_width)
    value_rows = value_rows.reshape(local_seqs, row_count, kv_width)
    all_keys, all_values = side_by_side((rotated_keys, value_rows), "ctx", 1, 0)
    attended_list, dquery_list, key_list, value_list = ([], [], [], [])
    for sequence in range(local_seqs):
        attended, dquery, key_terms, value_terms = attend_device(
            queries[sequence],
            d_attended[sequence],
            all_keys[sequence],
            all_values[sequence],
            query_pos,
            token_pos,
            KV_HEADS,
            HEAD_DIM,
        )
        attended_list.append(attended)
        dquery_list.append(dquery)
        key_list.append(key_terms)
        value_list.append(value_terms)
    key_stack = jnp.stack(key_list)
    value_stack = jnp.stack(value_list)
    key_grad, value_grad = in_one_piece(
        (key_stack.astype(jnp.bfloat16), value_stack.astype(jnp.bfloat16)), "ctx", 1, 0
    )
    key_grad = key_grad.reshape(local_seqs * row_count, kv_width)
    value_grad = value_grad.reshape(local_seqs * row_count, kv_width)
    grad_rows, weight_key, weight_value, gain_part = finish_backward(
        flat_tokens,
        normed,
        rms_scale,
        key_grad,
        value_grad,
        cosine_all,
        sine_all,
        norm_gain,
        key_weight,
        value_weight,
        KV_HEADS,
        HEAD_DIM,
    )
    weight_key, weight_value, gain_part = tuple(
        (
            part.astype(jnp.float32)
            for part in sent_together(
                (
                    weight_key.astype(jnp.bfloat16),
                    weight_value.astype(jnp.bfloat16),
                    gain_part.astype(jnp.bfloat16),
                ),
                ("ctx", "dp"),
                0,
                1,
            )
        )
    )
    return (
        jnp.stack(attended_list),
        jnp.stack(dquery_list),
        grad_rows.reshape(local_seqs, row_count, model_width),
        weight_key,
        weight_value,
        gain_part,
    )


def solution(mesh):
    placed = (P("dp", "ctx", None), P("dp", "ctx", None), P("dp", "ctx", None), P(), P(), P(), P())
    return jax.shard_map(
        body,
        mesh=mesh,
        in_specs=placed,
        out_specs=(
            P("dp", "ctx", None),
            P("dp", "ctx", None),
            P("dp", "ctx", None),
            P(("ctx", "dp"), None),
            P(("ctx", "dp"), None),
            P(("ctx", "dp")),
        ),
        check_vma=False,
    )
```

profile of v0, /device:TPU:1, one launch (start us, length us, event | category | flops | bytes accessed | tf_op | source)
XLA Modules:
  0.0 627.1 jit_solution(16988463766735147621)
XLA Ops:
  12.3 6.4 %copy.158 = bf16[512,4096]{1,0:T(8,128)(2,1)} copy(bf16[512,4096]{0,1:T(8,128)(2,1)} %bitcast.762) | data formatting | bytes 8388608 | tf_op jit(solution)/shard_map/dot_general | solution.py:85
  18.7 3.4 fusion.292
  22.4 2.9 convolution_convert_fusion.1
  28.9 102.6 %all-gather.2.cloned.1.call-done = bf16[4,2048,512]{2,1,0:T(8,128)(2,1)} async-done(((bf16[4,64,512]{2,1,0:T(8,128)(2,1)}), bf16[4,2048,512]{2,1,0:T(8,128)(2,1)}) %all-gather.2.cloned.1.call-update) | async-done | bytes 8388624 | tf_op jit(solution)/shard_map/all_gather | solution.py:18
  131.5 6.2 slice_bitcast_fusion.3
  137.7 3.3 fusion.276
  146.5 3.2 fusion.273
  151.6 2.7 multiply_reduce_fusion.2
  155.4 3.3 fusion.270
  160.6 2.7 multiply_reduce_fusion.1
  164.4 3.2 fusion.267
  169.5 2.7 multiply_reduce_fusion
  173.4 3.2 fusion.288
  178.9 2.7 multiply_reduce_fusion.7
  181.5 3.8 fusion.285
  187.3 2.6 multiply_reduce_fusion.6
  191.1 3.8 fusion.282
  200.6 4.1 fusion.279
  206.7 2.8 multiply_reduce_fusion.4
  219.1 4.0 copy.151
  228.4 4.0 copy.141
  241.6 3.9 copy.146
  250.7 3.9 copy.136
  254.6 7.2 %maximum_bitcast_fusion = bf16[32,4,64,512]{3,2,0,1:T(8,128)(2,1)} fusion(bf16[1,32,64,512]{3,2,1,0:T(8,128)(2,1)} %bitcast.764, bf16[1,32,64,512]{3,2,1,0:T(8,128)(2,1)} %bitcast.766, bf16[1,32,64,512]{3,2,1,0:T(8,128)(2,1)} %bitcast.765, bf16[1,32,64,512]{3,2,1,0:T(8,128)(2,1)} %bitcast.767), kind=kLoop, calls=%fused_computation.10 | loop fusion | flops 12582912 | bytes 16777216 | tf_op jit(solution)/shard_map/transpose | solution.py:28
  261.8 7.8 %copy.152 = bf16[32,4,64,512]{3,2,1,0:T(8,128)(2,1)} copy(bf16[32,4,64,512]{3,2,0,1:T(8,128)(2,1)} %maximum_bitcast_fusion) | data formatting | bytes 16777216 | tf_op jit(solution)/shard_map/transpose | solution.py:28
  269.6 101.9 %all_to_all.5 = bf16[32,4,64,512]{3,2,1,0:T(8,128)(2,1)S(1)} all-to-all(bf16[32,4,64,512]{3,2,1,0:T(8,128)(2,1)} %copy.152), channel_id=1, replica_groups=mesh['ctx'=32,'dp'=4] {'ctx'}, dimensions={0} | all-to-all | bytes 16777216 | tf_op jit(solution)/shard_map/all_to_all | solution.py:33
  373.3 3.3 bitcast_convert_fusion
  377.1 3.8 fusion.293
  381.0 3.4 fusion.98
  386.7 3.9 pad_maximum_fusion
  390.6 11.7 %copy.159 = bf16[4096,1025]{1,0:T(8,128)(2,1)} copy(bf16[4096,1025]{0,1:T(8,128)(2,1)} %pad_maximum_fusion) | data formatting | bytes 16793600
  415.1 200.9 %reduce-scatter.4.cloned.1.call-done = bf16[32,1025]{1,0:T(8,128)(2,1)} async-done(((bf16[4096,1025]{1,0:T(8,128)(2,1)}), bf16[32,1025]{1,0:T(8,128)(2,1)}) %reduce-scatter.4.cloned.1.call-update) | async-done | bytes 65616
  (323 shorter events, 85.6 us)
Async XLA Ops:
  7.2 3.7 copy-start.1
  7.2 4.7 copy-start.39
  7.2 124.3 %all-gather.2.cloned.1.call-start = ((), (), s32[]{:S(2)}) async-start(), calls=%async_computation.2 | async-start | bytes 8650752 | tf_op jit(solution)/shard_map/all_gather | solution.py:18
  26.1 589.9 %reduce-scatter.4.cloned.1.call-start = ((), (), s32[]{:S(2)}) async-start(), calls=%async_computation.3 | async-start | bytes 9510912
  28.0 109.7 %copy-start.56 = (bf16[8,4,8,128]{3,2,1,0:T(8,128)(2,1)}, bf16[8,4,8,128]{3,2,1,0:T(8,128)(2,1)S(1)}, u32[]{:S(2)}) copy-start(bf16[8,4,8,128]{3,2,1,0:T(8,128)(2,1)S(1)} %get-tuple-element.52) | copy-start | bytes 196612
  28.8 115.1 %copy-start.62 = (bf16[8,4,8,128]{3,2,1,0:T(8,128)(2,1)}, bf16[8,4,8,128]{3,2,1,0:T(8,128)(2,1)S(1)}, u32[]{:S(2)}) copy-start(bf16[8,4,8,128]{3,2,1,0:T(8,128)(2,1)S(1)} %get-tuple-element.44) | copy-start | bytes 196612
  28.8 125.5 %copy-start.60 = (bf16[8,4,8,128]{3,2,1,0:T(8,128)(2,1)}, bf16[8,4,8,128]{3,2,1,0:T(8,128)(2,1)S(1)}, u32[]{:S(2)}) copy-start(bf16[8,4,8,128]{3,2,1,0:T(8,128)(2,1)S(1)} %get-tuple-element.47) | copy-start | bytes 196612
  28.8 134.5 %copy-start.58 = (bf16[8,4,8,128]{3,2,1,0:T(8,128)(2,1)}, bf16[8,4,8,128]{3,2,1,0:T(8,128)(2,1)S(1)}, u32[]{:S(2)}) copy-start(bf16[8,4,8,128]{3,2,1,0:T(8,128)(2,1)S(1)} %get-tuple-element.46) | copy-start | bytes 196612
  28.8 143.5 %copy-start.54 = (bf16[8,4,8,128]{3,2,1,0:T(8,128)(2,1)}, bf16[8,4,8,128]{3,2,1,0:T(8,128)(2,1)S(1)}, u32[]{:S(2)}) copy-start(bf16[8,4,8,128]{3,2,1,0:T(8,128)(2,1)S(1)} %get-tuple-element.45) | copy-start | bytes 196612
  28.9 144.5 %copy-start.64 = (pred[64,2048]{1,0:T(8,128)(4,1)}, pred[64,2048]{1,0:T(8,128)(4,1)S(1)}, u32[]{:S(2)}) copy-start(pred[64,2048]{1,0:T(8,128)(4,1)S(1)} %broadcast_compare_fusion) | copy-start | bytes 393220
  149.7 4.6 copy-start.87
  151.5 3.9 copy-start.50
  158.7 4.6 copy-start.90
  160.6 3.9 copy-start.44
  167.7 4.6 copy-start.84
  169.5 3.9 copy-start.40
  204.7 6.1 copy-start.37
  206.7 4.1 copy-start.20
  206.7 4.0 copy-start.63
  206.7 4.0 copy-start.82
  206.7 4.0 copy-start.94
  219.1 4.0 copy-start.55
  219.1 4.0 copy-start.85
  219.1 4.0 copy-start.95
  228.4 4.0 copy-start.49
  228.4 4.0 copy-start.80
  228.4 4.0 copy-start.93
  241.6 3.9 copy-start.83
  241.6 3.9 copy-start.97
  377.1 3.9 copy-start.2
  377.1 3.9 copy-start.76
  402.3 5.1 copy-start.9
  (71 other events, 145.5 us)
Sparse Core Ops, SparseCore 0:
  26.2 105.2 all-gather.1
  402.4 213.5 reduce-scatter.3
where the time goes:
time: 634 us; the launch traced here: 627 us
  waiting for transfers between devices  304 us (48%)
  blocking collectives  102 us (16%)
  matrix products  97.4 us (15%)
  local copies, waits for them, and re-layouts  64.4 us (10%)
  other arithmetic  43.8 us (7%)
  between operations  16 us (3%)
    unnamed x3, waiting for transfers between devices  201 us
    all_gather x1, waiting for transfers between devices, side_by_side(): out, at, done = (lax.all_gather(both, axis, axis=dim, tiled=True), 0, [])  103 us
    all_to_all x1, blocking collectives, sent_and_summed(): lax.all_to_all(blocks, axis, split_axis=0, concat_axis=0, tiled=True)  102 us
    sub x8, matrix products, attend_group(): exponent = jnp.exp(scores - row_max)  27.9 us
    unnamed x210, local copies, waits for them, and re-layouts  24.5 us
    dot_general x8, matrix products, attend_group(): jnp.einsum('gts,sd->tgd', probability_b, value_group, preferred_element_t...  21.6 us
    convert_element_type x8, other arithmetic, attend_group(): probability_b = probability.astype(jnp.bfloat16)  15 us
  transfers between devices with their start and end apart: 2, of which 2 were waited for; matrix products, arithmetic and copies ran while one was open for 2% of the time, Pallas kernels for 0%

commit v1 on v0

v1 whole, which is shorter than its diff:
```python
import functools
import math

import jax
import jax.numpy as jnp
from jax import lax
from jax.experimental import pallas as pl
from jax.experimental.pallas import tpu as pltpu
from jax.sharding import PartitionSpec as P

KV_HEADS = 4
HEAD_DIM = 128
ROPE_BASE = 500000.0
EPSILON = 1e-05
BF = jnp.bfloat16
F32 = jnp.float32
VM = pltpu.VMEM
MESH = pl.DeviceIdType.MESH


def flip1(a):
    return a + 1 - 2 * (a % 2)


def flip3(a):
    return 3 - a


def flip2(a):
    return (a + 2) % 4


class Here:
    def __init__(self):
        ctx = lax.axis_index("ctx")
        dp = lax.axis_index("dp")
        self.z = ctx // 8
        self.y = (ctx // 2) % 4
        self.xh = ctx % 2
        self.xl = dp // 2
        self.core = dp % 2
        self.x = self.xh * 2 + self.xl

    def at(self, z=None, y=None, x=None, core=None):
        z = self.z if z is None else z
        y = self.y if y is None else y
        core = self.core if core is None else core
        if x is None:
            xh, xl = self.xh, self.xl
        else:
            xh, xl = x // 2, x % 2
        return {"ctx": z * 8 + y * 2 + xh, "dp": xl * 2 + core}


class Net:
    def __init__(self, send_sems, recv_sems):
        self.send_sems = send_sems
        self.recv_sems = recv_sems
        self.made = []

    def start(self, src, dst, device):
        k = len(self.made)
        copy = pltpu.make_async_remote_copy(
            src_ref=src,
            dst_ref=dst,
            send_sem=self.send_sems.at[k],
            recv_sem=self.recv_sems.at[k],
            device_id=device,
            device_id_type=MESH,
        )
        copy.start()
        self.made.append(copy)
        return copy

    def finish(self):
        for copy in self.made:
            copy.wait_send()


def greet(devices):
    barrier = pltpu.get_barrier_semaphore()
    for device in devices:
        pl.semaphore_signal(barrier, inc=1, device_id=device, device_id_type=MESH)
    pl.semaphore_wait(barrier, len(devices))


def cols(index, width):
    return pl.ds(pl.multiple_of(index * width, width), width)


N_FRONT = 2 * 3 * 3 + 2 * (1 + 2 * (2 + 4)) + 1


def front_kernel(q, do, kv, nrm, qr, dr, kvr, nrm2, send_sems, recv_sems, local_sems):
    here = Here()
    z, y, xh = here.z, here.y, here.xh
    x2 = flip2(here.x)
    greet(
        [here.at(z=f(z)) for f in (flip1, flip3, flip2)]
        + [here.at(y=f(y)) for f in (flip1, flip3, flip2)]
        + [here.at(x=x2), here.at(core=1 - here.core)]
    )
    net = Net(send_sems, recv_sems)

    def along(s, value):
        return here.at(z=value) if s == 0 else here.at(y=value)

    def across(s, value):
        return here.at(y=value) if s == 0 else here.at(z=value)

    head = [z, y]
    ring = [y, z]
    local = []

    def keep(src, dst):
        copy = pltpu.make_async_copy(src, dst, local_sems.at[len(local)])
        copy.start()
        local.append(copy)

    mine = [ring[s] * 2 + xh for s in range(2)]
    kv_copies = [[], []]
    for s in range(2):
        keep(kv.at[s, :, cols(head[s], 256)], kvr.at[s, mine[s], head[s]])
    for f in (flip1, flip3, flip2):
        for s in range(2):
            to = f(head[s])
            kv_copies[s].append(
                net.start(kv.at[s, :, cols(to, 256)], kvr.at[s, mine[s], head[s]], along(s, to))
            )
    rest = []
    for f in (flip1, flip3, flip2):
        for s in range(2):
            to = f(head[s])
            for src, dst in ((q, qr), (do, dr)):
                rest.append(net.start(src.at[s, :, cols(to, 512)], dst.at[s, head[s]], along(s, to)))
    for s in range(2):
        keep(q.at[s, :, cols(head[s], 512)], qr.at[s, head[s]])
        keep(do.at[s, :, cols(head[s], 512)], dr.at[s, head[s]])
    for s in range(2):
        local[s].wait()
        for copy in kv_copies[s]:
            copy.wait_recv()

    first = [[], []]
    second = [[], []]
    last = []

    def spread(s, xh_of):
        slot = ring[s] * 2 + xh_of
        for half, f in ((0, flip1), (1, flip3)):
            block = kvr.at[s, slot, 2 * half : 2 * half + 2]
            first[s].append(net.start(block, block, across(s, f(ring[s]))))

    def spread_on(s, xh_of):
        for half, f, g in ((0, flip1, flip3), (1, flip3, flip1)):
            first[s].pop(0).wait_recv()
            for value in (ring[s], f(ring[s])):
                block = kvr.at[s, value * 2 + xh_of, 2 * half : 2 * half + 2]
                last.append(net.start(block, block, across(s, g(ring[s]))))

    swapped = []
    for s in range(2):
        block = kvr.at[s, mine[s]]
        swapped.append(net.start(block, block, here.at(x=x2)))
        spread(s, xh)
    rest.append(net.start(nrm, nrm2, here.at(core=1 - here.core)))
    for s in range(2):
        spread_on(s, xh)
    for s in range(2):
        swapped[s].wait_recv()
        spread(s, 1 - xh)
    for s in range(2):
        spread_on(s, 1 - xh)
    for copy in last + rest:
        copy.wait_recv()
    for copy in local[2:]:
        copy.wait()
    net.finish()


def front(q, do, kv, nrm):
    vm = pl.BlockSpec(memory_space=VM)
    return pl.pallas_call(
        front_kernel,
        name="front",
        out_shape=(
            jax.ShapeDtypeStruct((2, 4, 64, 512), BF),
            jax.ShapeDtypeStruct((2, 4, 64, 512), BF),
            jax.ShapeDtypeStruct((2, 8, 4, 64, 256), BF),
            jax.ShapeDtypeStruct(nrm.shape, BF),
        ),
        in_specs=[vm] * 4,
        out_specs=(vm,) * 4,
        scratch_shapes=[
            pltpu.SemaphoreType.DMA((N_FRONT,)),
            pltpu.SemaphoreType.DMA((N_FRONT,)),
            pltpu.SemaphoreType.DMA((6,)),
        ],
        compiler_params=pltpu.CompilerParams(collective_id=1, has_side_effects=True),
    )(q, do, kv, nrm)


CHUNK = 256
KEYS = 2048


def attend_kernel(
    q_ref, do_ref, kv_ref, qpos_ref, kpos_ref, att_ref, dq_ref, term_ref,
    score, prob, key_t, value_t, acc_k, acc_v,
):
    block = pl.program_id(1)
    chunks = KEYS // CHUNK
    scale = HEAD_DIM ** (-0.5)
    to_two = scale * math.log2(math.e)

    @pl.when(block == 0)
    def _():
        key_t[...] = kv_ref[0, :, :128].T
        value_t[...] = kv_ref[0, :, 128:].T
        acc_k[...] = jnp.zeros_like(acc_k)
        acc_v[...] = jnp.zeros_like(acc_v)

    q = jnp.concatenate([q_ref[0, 0, :, h * 128 : (h + 1) * 128] for h in range(4)], axis=0)
    do = jnp.concatenate([do_ref[0, 0, :, h * 128 : (h + 1) * 128] for h in range(4)], axis=0)
    q_t = q.T
    do_t = do.T
    q_pos = qpos_ref[0, 0]

    def rows(c):
        return pl.ds(pl.multiple_of(c * CHUNK, CHUNK), CHUNK)

    def scores_of(c, top):
        s = jnp.dot(kv_ref[0, rows(c), :128], q_t, preferred_element_type=F32)
        k_pos = kpos_ref[0, rows(c), :]
        k_pos = jnp.concatenate([k_pos, k_pos], axis=1)
        s = jnp.where(k_pos <= q_pos, s, -1e30)
        score[rows(c), :] = s
        return jnp.maximum(top, jnp.max(s.reshape(CHUNK // 8, 8, 256), axis=0))

    top = lax.fori_loop(0, chunks, scores_of, jnp.full((8, 256), -1e30, F32), unroll=True)
    top = jnp.max(top, axis=0, keepdims=True)

    def exps_of(c, total):
        e = jnp.exp2((score[rows(c), :] - top) * to_two)
        score[rows(c), :] = e
        return total + jnp.sum(e.reshape(CHUNK // 8, 8, 256), axis=0)

    total = lax.fori_loop(0, chunks, exps_of, jnp.zeros((8, 256), F32), unroll=True)
    inverse = 1.0 / jnp.sum(total, axis=0, keepdims=True)

    def attended_of(c, out):
        p = (score[rows(c), :] * inverse).astype(BF)
        prob[rows(c), :] = p
        return out + jnp.dot(value_t[:, rows(c)], p, preferred_element_type=F32)

    out_t = lax.fori_loop(0, chunks, attended_of, jnp.zeros((128, 256), F32), unroll=True)
    out_t = out_t.astype(BF)
    delta = jnp.sum(out_t.astype(F32) * do_t.astype(F32), axis=0, keepdims=True)

    def grads_of(c, dq_t):
        dp = jnp.dot(kv_ref[0, rows(c), 128:], do_t, preferred_element_type=F32)
        ds = (score[rows(c), :] * inverse * (dp - delta)).astype(BF)
        acc_k[rows(c), :] += jnp.dot(ds, q, preferred_element_type=F32)
        acc_v[rows(c), :] += jnp.dot(prob[rows(c), :], do, preferred_element_type=F32)
        return dq_t + jnp.dot(key_t[:, rows(c)], ds, preferred_element_type=F32)

    dq_t = lax.fori_loop(0, chunks, grads_of, jnp.zeros((128, 256), F32), unroll=True)
    out = out_t.T
    dq = (dq_t * scale).astype(BF).T
    for h in range(4):
        att_ref[0, 0, :, h * 128 : (h + 1) * 128] = out[h * 64 : (h + 1) * 64]
        dq_ref[0, 0, :, h * 128 : (h + 1) * 128] = dq[h * 64 : (h + 1) * 64]

    @pl.when(block == 3)
    def _():
        term_ref[0, :, :128] = (acc_k[...] * scale).astype(BF)
        term_ref[0, :, 128:] = acc_v[...].astype(BF)


def attend(qr, dr, kvr, q_pos, k_pos):
    rows = pl.BlockSpec((1, 1, 64, 512), lambda s, b: (s, b, 0, 0))
    whole = pl.BlockSpec((1, KEYS, 256), lambda s, b: (s, 0, 0))
    return pl.pallas_call(
        attend_kernel,
        name="attend",
        grid=(2, 4),
        out_shape=(
            jax.ShapeDtypeStruct((2, 4, 64, 512), BF),
            jax.ShapeDtypeStruct((2, 4, 64, 512), BF),
            jax.ShapeDtypeStruct((2, KEYS, 256), BF),
        ),
        in_specs=[
            rows,
            rows,
            whole,
            pl.BlockSpec((1, 1, 1, 256), lambda s, b: (s, b, 0, 0)),
            pl.BlockSpec((1, KEYS, 128), lambda s, b: (s, 0, 0)),
        ],
        out_specs=(rows, rows, whole),
        scratch_shapes=[
            VM((KEYS, 256), F32),
            VM((KEYS, 256), BF),
            VM((128, KEYS), BF),
            VM((128, KEYS), BF),
            VM((KEYS, 128), F32),
            VM((KEYS, 128), F32),
        ],
        compiler_params=pltpu.CompilerParams(
            dimension_semantics=("arbitrary", "arbitrary"), vmem_limit_bytes=48 * 2**20
        ),
        cost_estimate=pl.CostEstimate(
            flops=6_500_000_000, bytes_accessed=12_000_000, transcendentals=4_200_000
        ),
    )(qr, dr, kvr, q_pos, k_pos)


N_BACK = 2 * (2 * 3 + 4 + 2 + 1 + 3)


def back_kernel(
    att, dq, term, att_out, dq_out, dkv_out,
    got1, sum1, got2, part, got3, final, send_sems, recv_sems, local_sems,
):
    here = Here()
    z, y, xh = here.z, here.y, here.xh
    x2 = flip2(here.x)
    greet(
        [here.at(z=f(z)) for f in (flip1, flip3, flip2)]
        + [here.at(y=f(y)) for f in (flip1, flip3, flip2)]
        + [here.at(x=x2)]
    )
    net = Net(send_sems, recv_sems)

    def along(s, value):
        return here.at(z=value) if s == 0 else here.at(y=value)

    def across(s, value):
        return here.at(y=value) if s == 0 else here.at(z=value)

    head = [z, y]
    ring = [y, z]
    flips = ((flip3, flip1), (flip1, flip3))

    def slots(value):
        return pl.ds(value * 2, 2)

    one = {}
    for j in (1, 0):
        for s in range(2):
            for half in range(2):
                f, g = flips[half]
                target = f(ring[s])
                slot = target if j == 0 else g(target)
                one[s, half, j] = net.start(
                    term.at[s, slots(slot), 2 * half : 2 * half + 2],
                    got1.at[s, half, j],
                    across(s, target),
                )
    rest = []
    local = []
    for f in (flip1, flip3, flip2):
        for s in range(2):
            to = f(head[s])
            for src, dst in ((att, att_out), (dq, dq_out)):
                rest.append(net.start(src.at[s, to], dst.at[s, :, cols(head[s], 512)], along(s, to)))
    for s in range(2):
        for src, dst in ((att, att_out), (dq, dq_out)):
            copy = pltpu.make_async_copy(
                src.at[s, head[s]], dst.at[s, :, cols(head[s], 512)], local_sems.at[len(local)]
            )
            copy.start()
            local.append(copy)

    two = {}
    for s in range(2):
        for half in range(2):
            f, g = flips[half]
            one[s, half, 1].wait_recv()
            sum1[s, half] = (
                term[s, slots(g(ring[s])), 2 * half : 2 * half + 2].astype(F32)
                + got1[s, half, 1].astype(F32)
            ).astype(BF)
            two[s, half] = net.start(sum1.at[s, half], got2.at[s, half], across(s, g(ring[s])))
    three = []
    for s in range(2):
        for half in range(2):
            one[s, half, 0].wait_recv()
            two[s, half].wait_recv()
            part[s, :, 2 * half : 2 * half + 2] = (
                term[s, slots(ring[s]), 2 * half : 2 * half + 2].astype(F32)
                + got1[s, half, 0].astype(F32)
                + got2[s, half].astype(F32)
            ).astype(BF)
        three.append(net.start(part.at[s, 1 - xh], got3.at[s], here.at(x=x2)))
    for s in range(2):
        three[s].wait_recv()
        final[s] = (part[s, xh].astype(F32) + got3[s].astype(F32)).astype(BF)
        for f in (flip1, flip3, flip2):
            to = f(head[s])
            rest.append(net.start(final.at[s, to], dkv_out.at[s, :, cols(head[s], 256)], along(s, to)))
        copy = pltpu.make_async_copy(
            final.at[s, head[s]], dkv_out.at[s, :, cols(head[s], 256)], local_sems.at[len(local)]
        )
        copy.start()
        local.append(copy)
    for copy in rest:
        copy.wait_recv()
    for copy in local:
        copy.wait()
    net.finish()


def back(att, dq, term):
    vm = pl.BlockSpec(memory_space=VM)
    return pl.pallas_call(
        back_kernel,
        name="back",
        out_shape=(
            jax.ShapeDtypeStruct((2, 64, 2048), BF),
            jax.ShapeDtypeStruct((2, 64, 2048), BF),
            jax.ShapeDtypeStruct((2, 64, 1024), BF),
        ),
        in_specs=[vm] * 3,
        out_specs=(vm,) * 3,
        scratch_shapes=[
            VM((2, 2, 2, 2, 2, 64, 256), BF),
            VM((2, 2, 2, 2, 64, 256), BF),
            VM((2, 2, 2, 2, 64, 256), BF),
            VM((2, 2, 4, 64, 256), BF),
            VM((2, 4, 64, 256), BF),
            VM((2, 4, 64, 256), BF),
            pltpu.SemaphoreType.DMA((N_BACK,)),
            pltpu.SemaphoreType.DMA((N_BACK,)),
            pltpu.SemaphoreType.DMA((6,)),
        ],
        compiler_params=pltpu.CompilerParams(collective_id=2, has_side_effects=True),
    )(att, dq, term)


def outer_kernel(n0_ref, n1_ref, g0_ref, g1_ref, out_ref):
    n = jnp.concatenate([n0_ref[...], n1_ref[...]], axis=0)
    g = jnp.concatenate([g0_ref[...], g1_ref[...]], axis=0)
    w = lax.dot_general(n, g, (((0,), (0,)), ((), ())), preferred_element_type=F32).astype(BF)
    for x in range(4):
        for u in range(4):
            at = x * 64 + u * 16
            out_ref[u, 0, x] = w[at : at + 16]


def outer(n0, n1, g0, g1):
    n_spec = pl.BlockSpec((128, 256), lambda i: (0, i))
    g_spec = pl.BlockSpec((128, 512), lambda i: (0, 0))
    return pl.pallas_call(
        outer_kernel,
        name="outer",
        grid=(16,),
        out_shape=jax.ShapeDtypeStruct((4, 16, 4, 16, 512), BF),
        in_specs=[n_spec, n_spec, g_spec, g_spec],
        out_specs=pl.BlockSpec((4, 1, 4, 16, 512), lambda i: (0, i, 0, 0, 0)),
        compiler_params=pltpu.CompilerParams(dimension_semantics=("arbitrary",)),
        cost_estimate=pl.CostEstimate(
            flops=1_080_000_000, bytes_accessed=6_500_000, transcendentals=0
        ),
    )(n0, n1, g0, g1)


PARTS = (
    (0, 0, 128, "zyx", True),
    (1, 0, 128, "yxz", True),
    (2, 0, 256, "xzy", True),
    (0, 128, 384, "zyx", False),
    (1, 128, 384, "yxz", False),
    (2, 256, 256, "xzy", False),
    (3, 0, 256, "zyx", True),
    (3, 256, 256, "yxz", True),
)
N_SUM = 9 * len(PARTS) + 8 + 1


def sum_kernel(
    g, gain, out, gain_out,
    r0, s0, r1, s1, r2, s2, r3, s3, r4, s4, r5, full, gain_got, gain_sent, send_sems, recv_sems,
):
    here = Here()
    place = {"z": here.z, "y": here.y, "x": here.x}
    greet(
        [here.at(**{a: f(place[a])}) for a in "zyx" for f in (flip1, flip3)]
        + [here.at(core=1 - here.core)]
    )
    net = Net(send_sems, recv_sems)

    def device(axis, value):
        return here.at(**{axis: value})

    plans = []
    for u, lo, width, order, up in PARTS:
        f, f2 = (flip1, flip3) if up else (flip3, flip1)
        a0, a1, a2 = order
        left = [a for a in "zyx" if a != a0]
        plans.append((u, pl.ds(lo, width), f, f2, a0, a1, a2, left.index(a1) == 0))

    def slab(ref, u, axis, value, lanes):
        if axis == "z":
            return ref.at[u, value, :, :, :, lanes]
        if axis == "y":
            return ref.at[u, :, value, :, :, lanes]
        return ref.at[u, :, :, value, :, lanes]

    def slab1(u, value, lanes, leading):
        return s1.at[u, value, :, :, lanes] if leading else s1.at[u, :, value, :, lanes]

    def wide(ref):
        return ref[...].astype(F32)

    waits = {}

    zf, yf, xf = place["z"], place["y"], place["x"]
    gain_routes = (
        [device("z", flip3(zf))]
        + [device("y", flip1(yf)), device("y", flip3(yf)), device("x", flip1(xf)), device("x", flip3(xf))]
        + [here.at(core=1 - here.core)]
    )
    gain_now = []

    def gain_step(step):
        if step == 0:
            gain_now.append(
                [
                    net.start(gain.at[flip1(zf)], gain_got.at[0], device("z", flip1(zf))),
                    net.start(gain.at[flip2(zf)], gain_got.at[1], device("z", flip1(zf))),
                ]
            )
            return
        for copy in gain_now[-1]:
            copy.wait_recv()
        if step == 1:
            gain_sent[0] = gain[flip3(zf)] + gain_got[1]
            gain_sent[1] = gain[zf] + gain_got[0]
            gain_now.append([net.start(gain_sent.at[0], gain_got.at[2], gain_routes[0])])
            return
        if step == 2:
            gain_sent[2] = gain_sent[1] + gain_got[2]
        else:
            gain_sent[step] = gain_sent[step - 1] + gain_got[step]
        if step < 7:
            gain_now.append(
                [net.start(gain_sent.at[step], gain_got.at[step + 1], gain_routes[step - 1])]
            )

    for step in range(6):
        for p, (u, lanes, f, f2, a0, a1, a2, leading) in enumerate(plans):
            m0, m1, m2 = place[a0], place[a1], place[a2]
            if step == 0:
                to = device(a0, f(m0))
                waits[p, 0, 1] = net.start(
                    slab(g, u, a0, flip2(m0), lanes), r0.at[u, 1, :, :, :, lanes], to
                )
                waits[p, 0, 0] = net.start(
                    slab(g, u, a0, f(m0), lanes), r0.at[u, 0, :, :, :, lanes], to
                )
            elif step == 1:
                waits[p, 0, 1].wait_recv()
                s0[u, :, :, :, lanes] = (
                    wide(slab(g, u, a0, f2(m0), lanes)) + r0[u, 1, :, :, :, lanes].astype(F32)
                ).astype(BF)
                waits[p, 1] = net.start(
                    s0.at[u, :, :, :, lanes], r1.at[u, :, :, :, lanes], device(a0, f2(m0))
                )
            elif step == 2:
                waits[p, 0, 0].wait_recv()
                waits[p, 1].wait_recv()
                s1[u, :, :, :, lanes] = (
                    wide(slab(g, u, a0, m0, lanes))
                    + r0[u, 0, :, :, :, lanes].astype(F32)
                    + r1[u, :, :, :, lanes].astype(F32)
                ).astype(BF)
                to = device(a1, f(m1))
                waits[p, 2, 1] = net.start(
                    slab1(u, flip2(m1), lanes, leading), r2.at[u, 1, :, :, lanes], to
                )
                waits[p, 2, 0] = net.start(
                    slab1(u, f(m1), lanes, leading), r2.at[u, 0, :, :, lanes], to
                )
            elif step == 3:
                waits[p, 2, 1].wait_recv()
                s2[u, :, :, lanes] = (
                    wide(slab1(u, f2(m1), lanes, leading)) + r2[u, 1, :, :, lanes].astype(F32)
                ).astype(BF)
                waits[p, 3] = net.start(
                    s2.at[u, :, :, lanes], r3.at[u, :, :, lanes], device(a1, f2(m1))
                )
            elif step == 4:
                waits[p, 2, 0].wait_recv()
                waits[p, 3].wait_recv()
                s3[u, :, :, lanes] = (
                    wide(slab1(u, m1, lanes, leading))
                    + r2[u, 0, :, :, lanes].astype(F32)
                    + r3[u, :, :, lanes].astype(F32)
                ).astype(BF)
                to = device(a2, f(m2))
                waits[p, 4, 1] = net.start(
                    s3.at[u, flip2(m2), :, lanes], r4.at[u, 1, :, lanes], to
                )
                waits[p, 4, 0] = net.start(s3.at[u, f(m2), :, lanes], r4.at[u, 0, :, lanes], to)
            else:
                waits[p, 4, 1].wait_recv()
                s4[u, :, lanes] = (
                    s3[u, f2(m2), :, lanes].astype(F32) + r4[u, 1, :, lanes].astype(F32)
                ).astype(BF)
                waits[p, 5] = net.start(
                    s4.at[u, :, lanes], r5.at[u, :, lanes], device(a2, f2(m2))
                )
        gain_step(step)
    for p, (u, lanes, f, f2, a0, a1, a2, leading) in enumerate(plans):
        waits[p, 4, 0].wait_recv()
        waits[p, 5].wait_recv()
        full[u // 2, u % 2, :, lanes] = (
            s3[u, place[a2], :, lanes].astype(F32)
            + r4[u, 0, :, lanes].astype(F32)
            + r5[u, :, lanes].astype(F32)
        )
    gain_step(6)
    swap = net.start(full.at[1 - here.core], out.at[here.core], here.at(core=1 - here.core))
    out[here.core] = full[here.core]
    gain_step(7)
    gain_out[...] = gain_sent[7]
    swap.wait_recv()
    net.finish()


def sum_everywhere(g, gain):
    vm = pl.BlockSpec(memory_space=VM)
    tail = (16, 512)
    return pl.pallas_call(
        sum_kernel,
        name="sum_everywhere",
        out_shape=(
            jax.ShapeDtypeStruct((2, 2, *tail), F32),
            jax.ShapeDtypeStruct((8, 128), F32),
        ),
        in_specs=[vm] * 2,
        out_specs=(vm,) * 2,
        scratch_shapes=[
            VM((4, 2, 4, 4, *tail), BF),
            VM((4, 4, 4, *tail), BF),
            VM((4, 4, 4, *tail), BF),
            VM((4, 4, 4, *tail), BF),
            VM((4, 2, 4, *tail), BF),
            VM((4, 4, *tail), BF),
            VM((4, 4, *tail), BF),
            VM((4, 4, *tail), BF),
            VM((4, 2, *tail), BF),
            VM((4, *tail), BF),
            VM((4, *tail), BF),
            VM((2, 2, *tail), F32),
            VM((8, 8, 128), F32),
            VM((8, 8, 128), F32),
            pltpu.SemaphoreType.DMA((N_SUM,)),
            pltpu.SemaphoreType.DMA((N_SUM,)),
        ],
        compiler_params=pltpu.CompilerParams(collective_id=3, has_side_effects=True),
    )(g, gain)


def rotation(token_pos, head_size):
    half_dim = head_size // 2
    frequency = ROPE_BASE ** (-2.0 * jnp.arange(half_dim, dtype=F32) / head_size)
    angles = token_pos.astype(F32)[:, None] * frequency[None, :]
    angles = jnp.concatenate([angles, angles], axis=1)
    return (jnp.cos(angles), jnp.sin(angles))


def rotate_half(values):
    half_dim = values.shape[-1] // 2
    return jnp.concatenate([-values[..., half_dim:], values[..., :half_dim]], axis=-1)


def rotate_back(values):
    half_dim = values.shape[-1] // 2
    return jnp.concatenate([values[..., half_dim:], -values[..., :half_dim]], axis=-1)


def body(tokens, queries, d_attended, span_order, norm_gain, key_weight, value_weight):
    seqs, rows, width = tokens.shape
    count = seqs * rows
    ctx = lax.axis_index("ctx")
    core = lax.axis_index("dp") % 2
    z, y, xh = ctx // 8, (ctx // 2) % 4, ctx % 2
    offsets = jnp.arange(rows // 2, dtype=jnp.int32)
    token_pos = (span_order[:, None] * (rows // 2) + offsets[None, :]).reshape(-1)
    own_pos = lax.dynamic_slice_in_dim(token_pos, ctx * rows, rows, 0)
    cosine, sine = rotation(own_pos, HEAD_DIM)
    cosine = jnp.tile(cosine, (seqs, 1))[:, None, :]
    sine = jnp.tile(sine, (seqs, 1))[:, None, :]

    placed = token_pos.reshape(4, 4, 2, rows)
    q_pos = jnp.stack([placed[:, y, xh], placed[z, :, xh]])
    q_pos = jnp.tile(q_pos, (1, 1, 4))[:, :, None, :]
    k_pos = jnp.stack(
        [placed.transpose(1, 2, 0, 3).reshape(-1), placed.transpose(0, 2, 1, 3).reshape(-1)]
    )
    k_pos = jnp.broadcast_to(k_pos[:, :, None], (*k_pos.shape, 128))

    flat = tokens.reshape(count, width)
    wide = flat.astype(F32)
    rms = lax.rsqrt(jnp.mean(wide * wide, axis=-1, keepdims=True) + EPSILON)
    normed = (wide * rms * norm_gain).astype(BF)
    key_pre = jnp.dot(normed, key_weight, preferred_element_type=F32).reshape(count, KV_HEADS, -1)
    keys = (key_pre * cosine + rotate_half(key_pre) * sine).astype(BF)
    values = jnp.dot(normed, value_weight, preferred_element_type=F32).astype(BF)
    kv = jnp.stack([keys, values.reshape(count, KV_HEADS, HEAD_DIM)], axis=2)
    kv = kv.reshape(seqs, rows, 2 * KV_HEADS * HEAD_DIM)

    qr, dr, kvr, other = front(queries, d_attended, kv, normed)
    att, dq, term = attend(qr, dr, kvr.reshape(seqs, -1, 256), q_pos, k_pos)
    attended, grad_queries, dkv = back(att, dq, term.reshape(seqs, 8, 4, rows, 256))

    dkv = dkv.reshape(count, KV_HEADS, 2, HEAD_DIM).astype(F32)
    shaped = dkv[:, :, 0]
    key_grad = (shaped * cosine + rotate_back(shaped * sine)).reshape(count, -1).astype(BF)
    value_grad = dkv[:, :, 1].reshape(count, -1).astype(BF)
    own = jnp.where(core == 0, key_grad, value_grad)
    sent = jnp.where(core == 0, value_grad, key_grad)
    got = lax.ppermute(sent, "dp", [(0, 1), (1, 0), (2, 3), (3, 2)])
    normed_grad = jnp.dot(key_grad, key_weight.T, preferred_element_type=F32) + jnp.dot(
        value_grad, value_weight.T, preferred_element_type=F32
    )
    gain_part = jnp.sum(normed_grad * wide * rms, axis=0)
    inner = jnp.mean(normed_grad * norm_gain * wide, axis=-1, keepdims=True)
    grad_rows = (rms * norm_gain * normed_grad - wide * rms**3 * inner).astype(BF)

    g = outer(normed, other, own, got).reshape(4, 4, 4, 4, 16, 512)
    weights, gain = sum_everywhere(g, gain_part.reshape(4, 8, 128))
    weights = weights.reshape(2, 32, 512)
    gain = lax.dynamic_slice(gain, (ctx % 8, lax.axis_index("dp") * 32), (1, 32))
    return (
        attended,
        grad_queries,
        grad_rows.reshape(seqs, rows, width),
        weights[0],
        weights[1],
        gain.reshape(32),
    )


def solution(mesh):
    placed = (P("dp", "ctx", None), P("dp", "ctx", None), P("dp", "ctx", None), P(), P(), P(), P())
    return jax.shard_map(
        body,
        mesh=mesh,
        in_specs=placed,
        out_specs=(
            P("dp", "ctx", None),
            P("dp", "ctx", None),
            P("dp", "ctx", None),
            P(("ctx", "dp"), None),
            P(("ctx", "dp"), None),
            P(("ctx", "dp")),
        ),
        check_vma=False,
    )
```

time: 634 us -> 178 us (0.28)
  waiting for transfers between devices: 304 us -> 0.01 us
  Pallas kernels: 0 us -> 130 us
  blocking collectives: 102 us -> 0 us
  matrix products: 97.4 us -> 10.4 us
  local copies, waits for them, and re-layouts: 64.4 us -> 21.7 us
  other arithmetic: 43.8 us -> 8.46 us
  between operations: 16 us -> 1.11 us
    unnamed x3 -> x0, waiting for transfers between devices: 201 us -> none
    pallas_call x0 -> x5, Pallas kernels: none -> 130 us  [the longest x1 35.6 us: sum_everywhere(): pl.pallas_call(sum_kernel, name='sum_everywhere', out_shape=(jax.ShapeDty...]
    all_gather x1 -> x0, waiting for transfers between devices: 103 us -> none  [side_by_side(): out, at, done = (lax.all_gather(both, axis, axis=dim, tiled=True), 0, [])]
    all_to_all x1 -> x0, blocking collectives: 102 us -> none  [sent_and_summed(): lax.all_to_all(blocks, axis, split_axis=0, concat_axis=0, tiled=True)]
    dot_general x46 -> x4, matrix products: 69.4 us -> 10.4 us  [the longest x1 3.81 us: body(): jnp.dot(key_grad, key_weight.T, preferred_element_type=F32)]
    sub x8 -> x0, matrix products: 27.9 us -> none  [attend_group(): exponent = jnp.exp(scores - row_max)]
    unnamed x210 -> x33, local copies, waits for them, and re-layouts: 24.5 us -> 5.53 us
    convert_element_type x16 -> x4, other arithmetic: 19.3 us -> 3.02 us  [the longest x1 2.29 us: body(): (rms * norm_gain * normed_grad - wide * rms ** 3 * inner).astype(BF)]
  transfers between devices with their start and end apart: 2 -> 1, of which waited for: 2 -> 0; matrix products, arithmetic and copies ran while one was open for 2% -> 6% of each run, Pallas kernels for 0% -> 0%
where the time goes in v1:
time: 178 us; the launch traced here: 177 us
  Pallas kernels  130 us (73%)
  local copies, waits for them, and re-layouts  21.7 us (12%)
  matrix products  10.4 us (6%)
  other arithmetic  8.46 us (5%)
  starting transfers between devices  5.4 us (3%)
    pallas_call x1, Pallas kernels, sum_everywhere(): pl.pallas_call(sum_kernel, name='sum_everywhere', out_shape=(jax.ShapeDty...  35.6 us
    pallas_call x1, Pallas kernels, front(): pl.pallas_call(front_kernel, name='front', out_shape=(jax.ShapeDtypeStruc...  30 us
    pallas_call x1, Pallas kernels, back(): pl.pallas_call(back_kernel, name='back', out_shape=(jax.ShapeDtypeStruct(...  27.5 us
    pallas_call x1, Pallas kernels, attend(): pl.pallas_call(attend_kernel, name='attend', grid=(2, 4), out_shape=(jax....  25.2 us
    pallas_call x1, Pallas kernels, outer(): pl.pallas_call(outer_kernel, name='outer', grid=(16,), out_shape=jax.Shap...  11.3 us
    dot_general x1, local copies, waits for them, and re-layouts, body(): jnp.dot(normed, key_weight, preferred_element_type=F32)  6.45 us
    unnamed x33, local copies, waits for them, and re-layouts  5.53 us
    ppermute x1, starting transfers between devices, body(): got = lax.ppermute(sent, 'dp', [(0, 1), (1, 0), (2, 3), (3, 2)])  5.4 us
  transfers between devices with their start and end apart: 1, of which 0 were waited for; matrix products, arithmetic and copies ran while one was open for 6% of the time, Pallas kernels for 0%

profile of v1, /device:TPU:1, one launch (start us, length us, event | category | flops | bytes accessed | tf_op | source)
XLA Modules:
  0.0 176.9 jit_solution(12993285929975192540)
XLA Ops:
  0.7 0.7 broadcast_multiply_fusion.2
  2.4 0.2 fusion.17
  2.8 1.5 fusion
  4.4 0.3 fusion.2
  4.8 6.5 %copy.35 = bf16[512,4096]{1,0:T(8,128)(2,1)} copy(bf16[512,4096]{0,1:T(8,128)(2,1)} %bitcast.71) | data formatting | bytes 8388608 | tf_op jit(solution)/shard_map/dot_general | solution.py:708
  11.2 3.6 %fusion.21 = f32[128,4,128]{0,2,1:T(8,128)S(1)} fusion(bf16[128,4096,1]{1,0,2:T(8,128)(2,1)S(1)} %bitcast.74, bf16[4,128,4096]{2,1,0:T(8,128)(2,1)} %bitcast.73), kind=kOutput, calls=%fused_computation.54 | convolution fusion | flops 536870912 | bytes 5505024 | tf_op jit(solution)/shard_map/dot_general | solution.py:708
  14.9 0.3 fusion.4.nrm.n0_ref
  15.2 0.8 convolution_convert_fusion
  16.6 0.9 reshape.176.kv
  17.7 30.0 %front.1 = (bf16[2,4,64,512]{3,2,1,0:T(8,128)(2,1)}, bf16[2,4,64,512]{3,2,1,0:T(8,128)(2,1)}, bf16[2,8,4,64,256]{4,3,2,1,0:T(8,128)(2,1)}, bf16[128,4096]{1,0:T(8,128)(2,1)}) custom-call(bf16[2,64,2048]{2,1,0:T(8,128)(2,1)} %q.1, bf16[2,64,2048]{2,1,0:T(8,128)(2,1)} %do.1, bf16[2,64,1024]{2,1,0:T(8,128)(2,1)} %reshape.176.kv, bf16[128,4096]{1,0:T(8,128)(2,1)} %copy-done.8), custom_call_target="tpu_custom_call" | custom-call | tf_op jit(solution)/shard_map/front/pallas_call | solution.py:183
  47.7 2.3 %broadcast_in_dim.2.kpos_ref = s32[2,2048,128]{2,1,0:T(8,128)} broadcast(s32[2,2048]{1,0:T(2,128)S(1)} %pad_add_fusion), dimensions={0,1} | broadcast | bytes 2113536 | tf_op jit(solution)/shard_map/broadcast_in_dim | solution.py:702
  50.0 25.2 %attend.1 = (bf16[2,4,64,512]{3,2,1,0:T(8,128)(2,1)S(1)}, bf16[2,4,64,512]{3,2,1,0:T(8,128)(2,1)S(1)}, bf16[2,2048,256]{2,1,0:T(8,128)(2,1)S(1)}) custom-call(bf16[2,4,64,512]{3,2,1,0:T(8,128)(2,1)S(1)} %copy-done.3, bf16[2,4,64,512]{3,2,1,0:T(8,128)(2,1)S(1)} %copy-done.4, bf16[2,2048,256]{2,1,0:T(8,128)(2,1)} %bitcast.89, ...), custom_call_target="tpu_custom_call" | custom-call | flops 6499999744 | bytes 12000000 | tf_op jit(solution)/shard_map/attend/pallas_call | solution.py:283
  75.3 1.3 copy-done
  76.6 0.8 copy-done.1
  77.4 0.8 copy-done.2
  78.2 27.5 %back.1 = (bf16[2,64,2048]{2,1,0:T(8,128)(2,1)}, bf16[2,64,2048]{2,1,0:T(8,128)(2,1)}, bf16[2,64,1024]{2,1,0:T(8,128)(2,1)}) custom-call(bf16[2,4,64,512]{3,2,1,0:T(8,128)(2,1)} %copy-done.1, bf16[2,4,64,512]{3,2,1,0:T(8,128)(2,1)} %copy-done.2, bf16[2,8,4,64,256]{4,3,2,1,0:T(8,128)(2,1)} %bitcast.70), custom_call_target="tpu_custom_call" | custom-call | tf_op jit(solution)/shard_map/back/pallas_call | solution.py:415
  105.7 1.1 convert_element_type.49
  106.8 0.9 fusion.19
  108.4 0.7 bitcast_select_fusion
  109.2 5.4 %collective-permute-start = (bf16[128,512]{1,0:T(8,128)(2,1)}, bf16[128,512]{1,0:T(8,128)(2,1)S(1)}, u32[]{:S(2)}, u32[]{:S(2)}) collective-permute-start(bf16[128,512]{1,0:T(8,128)(2,1)} %get-tuple-element.32), channel_id=1, source_target_pairs={{0,1},{1,0},{2,3},{3,2},{4,5},{5,4},{6,7},{7,6},{8,9},{9,8},{10,11... | collective-permute-start | bytes 393224 | tf_op jit(solution)/shard_map/ppermute | solution.py:724
  114.6 3.8 %fusion.22 = f32[128,4096]{1,0:T(8,128)S(1)} fusion(bf16[128,512]{1,0:T(8,128)(2,1)S(1)} %get-tuple-element.33, bf16[4096,512]{1,0:T(8,128)(2,1)} %param.12), kind=kOutput, calls=%fused_computation.55 | convolution fusion | flops 536870912 | bytes 6422528 | tf_op jit(solution)/shard_map/dot_general | solution.py:725
  118.4 2.3 %fusion.10 = (f32[4096]{0:T(1024)}, f32[128]{0:T(128)}, f32[128,4096]{1,0:T(8,128)S(1)}) fusion(bf16[2,64,4096]{2,1,0:T(8,128)(2,1)S(1)} %copy-done.5, f32[128]{0:T(128)S(1)} %copy-done.14, f32[4096]{0:T(1024)S(1)} %copy-done.11, f32[128,4096]{1,0:T(8,128)S(1)} %fusion.22, bf16[4096,512]{1,0:T(8,128)(2,1)S(1)} %copy-done.7, ...), kind=kOutput, calls=%fused_computation.17 | convolution fusion | flops 541060992 | bytes 9602048 | tf_op jit(solution)/shard_map/dot_general | solution.py:725
  120.7 1.2 multiply_multiply_fusion
  121.8 2.3 %fusion.7 = bf16[128,4096]{1,0:T(8,128)(2,1)} fusion(bf16[2,64,4096]{2,1,0:T(8,128)(2,1)S(1)} %copy-done.5, f32[128,4096]{1,0:T(8,128)S(1)} %get-tuple-element.44, f32[128]{0:T(128)} %get-tuple-element.46, f32[128]{0:T(128)} %get-tuple-element.45, f32[4096]{0:T(1024)S(1)} %copy-done.11, f32[128]{0:T(128)} %copy-done.13), kind=kLoop, calls=%fused_computation.14 | loop fusion | flops 3670016 | bytes 4212224 | tf_op jit(solution)/shard_map/convert_element_type | solution.py:730
  124.1 0.7 bitcast_select_fusion.1.g0_ref
  124.8 0.7 copy-done.12
  125.5 11.3 %outer.1 = bf16[4,16,4,16,512]{4,3,2,1,0:T(8,128)(2,1)} custom-call(bf16[128,4096]{1,0:T(8,128)(2,1)} %copy-done.8, bf16[128,4096]{1,0:T(8,128)(2,1)} %get-tuple-element.27.n1_ref, bf16[128,512]{1,0:T(8,128)(2,1)} %bitcast_select_fusion.1.g0_ref, bf16[128,512]{1,0:T(8,128)(2,1)} %copy-done.12), custom_call_target="tpu_custom_call" | custom-call | flops 1080000000 | bytes 6500000 | tf_op jit(solution)/shard_map/outer/pallas_call | solution.py:453
  136.8 35.6 %sum_everywhere.1 = (f32[2,2,16,512]{3,2,1,0:T(8,128)}, f32[8,128]{1,0:T(8,128)}) custom-call(bf16[4,4,4,4,16,512]{5,4,3,2,1,0:T(8,128)(2,1)} %bitcast.72, f32[4,8,128]{2,1,0:T(8,128)} %bitcast.85), custom_call_target="tpu_custom_call" | custom-call | tf_op jit(solution)/shard_map/sum_everywhere/pallas_call | solution.py:634
  172.5 1.5 fusion.20
  174.0 1.3 dynamic-slice_bitcast_fusion.1
  175.3 0.8 copy.52
  176.1 0.8 copy.53
  (69 shorter events, 2.5 us)
Async XLA Ops:
  0.6 3.8 %copy-start.5 = (bf16[2,64,4096]{2,1,0:T(8,128)(2,1)S(1)}, bf16[2,64,4096]{2,1,0:T(8,128)(2,1)}, u32[]{:S(2)}) copy-start(bf16[2,64,4096]{2,1,0:T(8,128)(2,1)} %param.7) | copy-start | bytes 3145732
  0.6 3.8 %copy-start.11 = (f32[4096]{0:T(1024)S(1)}, f32[4096]{0:T(1024)}, u32[]{:S(2)}) copy-start(f32[4096]{0:T(1024)} %param.11) | copy-start | bytes 49156
  4.4 10.4 %copy-start.13 = (f32[128]{0:T(128)}, f32[128]{0:T(128)S(1)}, u32[]{:S(2)}) copy-start(f32[128]{0:T(128)S(1)} %rsqrt.16) | copy-start | bytes 1540
  11.2 4.0 %copy-start.6 = (bf16[4096,512]{1,0:T(8,128)(2,1)S(1)}, bf16[4096,512]{1,0:T(8,128)(2,1)}, u32[]{:S(2)}) copy-start(bf16[4096,512]{1,0:T(8,128)(2,1)} %param.13) | copy-start | bytes 12582916
  15.2 1.0 copy-start.8
  47.7 2.4 %copy-start.3 = (bf16[2,4,64,512]{3,2,1,0:T(8,128)(2,1)S(1)}, bf16[2,4,64,512]{3,2,1,0:T(8,128)(2,1)}, u32[]{:S(2)}) copy-start(bf16[2,4,64,512]{3,2,1,0:T(8,128)(2,1)} %get-tuple-element.18.q_ref) | copy-start | bytes 1572868
  47.7 2.3 %copy-start.4 = (bf16[2,4,64,512]{3,2,1,0:T(8,128)(2,1)S(1)}, bf16[2,4,64,512]{3,2,1,0:T(8,128)(2,1)}, u32[]{:S(2)}) copy-start(bf16[2,4,64,512]{3,2,1,0:T(8,128)(2,1)} %get-tuple-element.19.do_ref) | copy-start | bytes 1572868
  75.2 1.3 copy-start
  76.6 0.8 copy-start.1
  77.4 0.8 copy-start.2
  109.2 15.7 %collective-permute-start = (bf16[128,512]{1,0:T(8,128)(2,1)}, bf16[128,512]{1,0:T(8,128)(2,1)S(1)}, u32[]{:S(2)}, u32[]{:S(2)}) collective-permute-start(bf16[128,512]{1,0:T(8,128)(2,1)} %get-tuple-element.32), channel_id=1, source_target_pairs={{0,1},{1,0},{2,3},{3,2},{4,5},{5,4},{6,7},{7,6},{8,9},{9,8},{10,11... | collective-permute-start | bytes 393224 | tf_op jit(solution)/shard_map/ppermute | solution.py:724
  114.6 3.8 %copy-start.7 = (bf16[4096,512]{1,0:T(8,128)(2,1)S(1)}, bf16[4096,512]{1,0:T(8,128)(2,1)}, u32[]{:S(2)}) copy-start(bf16[4096,512]{1,0:T(8,128)(2,1)} %param.13) | copy-start | bytes 12582916
  114.6 3.8 %copy-start.14 = (f32[128]{0:T(128)S(1)}, f32[128]{0:T(128)}, u32[]{:S(2)}) copy-start(f32[128]{0:T(128)} %copy-done.13) | copy-start | bytes 1540
  124.8 0.7 copy-start.12
  136.8 38.4 %copy-start.10 = (bf16[2,64,2048]{2,1,0:T(8,128)(2,1)S(1)}, bf16[2,64,2048]{2,1,0:T(8,128)(2,1)}, u32[]{:S(2)}) copy-start(bf16[2,64,2048]{2,1,0:T(8,128)(2,1)} %get-tuple-element.53) | copy-start | bytes 1572868
  136.8 39.2 %copy-start.9 = (bf16[2,64,2048]{2,1,0:T(8,128)(2,1)S(1)}, bf16[2,64,2048]{2,1,0:T(8,128)(2,1)}, u32[]{:S(2)}) copy-start(bf16[2,64,2048]{2,1,0:T(8,128)(2,1)} %get-tuple-element.54) | copy-start | bytes 1572868

commit v2 on v1

--- a/solution.py
+++ b/solution.py
@@ -89,12 +89,25 @@
 
 
 N_FRONT = 2 * 3 * 3 + 2 * (1 + 2 * (2 + 4)) + 1
-
-
-def front_kernel(q, do, kv, nrm, qr, dr, kvr, nrm2, send_sems, recv_sems, local_sems):
+PIECES = 8
+
+
+def front_kernel(
+    q, do, tokens, gain, key_w, value_w, cos, sin,
+    qr, dr, kvr, norm_t, rms_out,
+    kw, vw, normed, acc, kv, send_sems, recv_sems, local_sems, weight_sems,
+):
     here = Here()
     z, y, xh = here.z, here.y, here.xh
     x2 = flip2(here.x)
+    piece = 4096 // PIECES
+    loads = []
+    for c in range(PIECES):
+        for w, (src, dst) in enumerate(((key_w, kw), (value_w, vw))):
+            at = pl.ds(c * piece, piece)
+            copy = pltpu.make_async_copy(src.at[at], dst.at[at], weight_sems.at[2 * c + w])
+            copy.start()
+            loads.append(copy)
     greet(
         [here.at(z=f(z)) for f in (flip1, flip3, flip2)]
         + [here.at(y=f(y)) for f in (flip1, flip3, flip2)]
@@ -117,32 +130,66 @@
         copy.start()
         local.append(copy)
 
+    rest = []
+    for f in (flip1, flip3, flip2):
+        for s in range(2):
+            to = f(head[s])
+            for src, dst in ((q, qr), (do, dr)):
+                rest.append(net.start(src.at[s, :, cols(to, 512)], dst.at[s, head[s]], along(s, to)))
+    for s in range(2):
+        keep(q.at[s, :, cols(head[s], 512)], qr.at[s, head[s]])
+        keep(do.at[s, :, cols(head[s], 512)], dr.at[s, head[s]])
+
+    squares = jnp.zeros((128, 128), F32)
+    for c in range(32):
+        t = tokens[:, c * 128 : (c + 1) * 128].astype(F32)
+        squares = squares + t * t
+    rms = lax.rsqrt(jnp.sum(squares, axis=1, keepdims=True) / 4096.0 + EPSILON)
+    rms_out[...] = jnp.broadcast_to(rms, (128, 128))
+    for c in range(PIECES):
+        at = slice(c * piece, (c + 1) * piece)
+        normed[:, at] = (tokens[:, at].astype(F32) * rms * gain[:, at]).astype(BF)
+    for c in range(PIECES):
+        at = slice(c * piece, (c + 1) * piece)
+        n = normed[:, at]
+        for w, ref in enumerate((kw, vw)):
+            loads[2 * c + w].wait()
+            term = jnp.dot(n, ref[at, :], preferred_element_type=F32)
+            if c == 0:
+                acc[w] = term
+            else:
+                acc[w] += term
+    both_cos = jnp.concatenate([cos[...], cos[...]], axis=0)
+    both_sin = jnp.concatenate([sin[...], sin[...]], axis=0)
+    for h in range(KV_HEADS):
+        at = slice(h * 128, (h + 1) * 128)
+        u = acc[0, :, at]
+        k = (u * both_cos + pltpu.roll(u, 64, 1) * both_sin).astype(BF)
+        v = acc[1, :, at].astype(BF)
+        for s in range(2):
+            kv[s, :, h * 256 : h * 256 + 128] = k[s * 64 : (s + 1) * 64]
+            kv[s, :, h * 256 + 128 : (h + 1) * 256] = v[s * 64 : (s + 1) * 64]
+
     mine = [ring[s] * 2 + xh for s in range(2)]
     kv_copies = [[], []]
-    for s in range(2):
-        keep(kv.at[s, :, cols(head[s], 256)], kvr.at[s, mine[s], head[s]])
     for f in (flip1, flip3, flip2):
         for s in range(2):
             to = f(head[s])
             kv_copies[s].append(
                 net.start(kv.at[s, :, cols(to, 256)], kvr.at[s, mine[s], head[s]], along(s, to))
             )
-    rest = []
-    for f in (flip1, flip3, flip2):
-        for s in range(2):
-            to = f(head[s])
-            for src, dst in ((q, qr), (do, dr)):
-                rest.append(net.start(src.at[s, :, cols(to, 512)], dst.at[s, head[s]], along(s, to)))
-    for s in range(2):
-        keep(q.at[s, :, cols(head[s], 512)], qr.at[s, head[s]])
-        keep(do.at[s, :, cols(head[s], 512)], dr.at[s, head[s]])
-    for s in range(2):
-        local[s].wait()
+    for s in range(2):
+        keep(kv.at[s, :, cols(head[s], 256)], kvr.at[s, mine[s], head[s]])
+    for c in range(32):
+        at = slice(c * 128, (c + 1) * 128)
+        norm_t[0, at, :] = normed[:, at].T
+    rest.append(net.start(norm_t.at[0], norm_t.at[1], here.at(core=1 - here.core)))
+    for s in range(2):
+        local[4 + s].wait()
         for copy in kv_copies[s]:
             copy.wait_recv()
 
     first = [[], []]
-    second = [[], []]
     last = []
 
     def spread(s, xh_of):
@@ -163,7 +210,6 @@
         block = kvr.at[s, mine[s]]
         swapped.append(net.start(block, block, here.at(x=x2)))
         spread(s, xh)
-    rest.append(net.start(nrm, nrm2, here.at(core=1 - here.core)))
     for s in range(2):
         spread_on(s, xh)
     for s in range(2):
@@ -173,13 +219,14 @@
         spread_on(s, 1 - xh)
     for copy in last + rest:
         copy.wait_recv()
-    for copy in local[2:]:
+    for copy in local[:4]:
         copy.wait()
     net.finish()
 
 
-def front(q, do, kv, nrm):
+def front(q, do, tokens, gain, key_w, value_w, cos, sin):
     vm = pl.BlockSpec(memory_space=VM)
+    any_ = pl.BlockSpec(memory_space=pl.ANY)
     return pl.pallas_call(
         front_kernel,
         name="front",
@@ -187,17 +234,26 @@
             jax.ShapeDtypeStruct((2, 4, 64, 512), BF),
             jax.ShapeDtypeStruct((2, 4, 64, 512), BF),
             jax.ShapeDtypeStruct((2, 8, 4, 64, 256), BF),
-            jax.ShapeDtypeStruct(nrm.shape, BF),
+            jax.ShapeDtypeStruct((2, 4096, 128), BF),
+            jax.ShapeDtypeStruct((128, 128), F32),
         ),
-        in_specs=[vm] * 4,
-        out_specs=(vm,) * 4,
+        in_specs=[any_, any_, vm, vm, any_, any_, vm, vm],
+        out_specs=(vm,) * 5,
         scratch_shapes=[
+            VM((4096, 512), BF),
+            VM((4096, 512), BF),
+            VM((128, 4096), BF),
+            VM((2, 128, 512), F32),
+            VM((2, 64, 1024), BF),
             pltpu.SemaphoreType.DMA((N_FRONT,)),
             pltpu.SemaphoreType.DMA((N_FRONT,)),
             pltpu.SemaphoreType.DMA((6,)),
+            pltpu.SemaphoreType.DMA((2 * PIECES,)),
         ],
-        compiler_params=pltpu.CompilerParams(collective_id=1, has_side_effects=True),
-    )(q, do, kv, nrm)
+        compiler_params=pltpu.CompilerParams(
+            collective_id=1, has_side_effects=True, vmem_limit_bytes=56 * 2**20
+        ),
+    )(q, do, tokens, gain, key_w, value_w, cos, sin)
 
 
 CHUNK = 256
@@ -314,156 +370,6 @@
     )(qr, dr, kvr, q_pos, k_pos)
 
 
-N_BACK = 2 * (2 * 3 + 4 + 2 + 1 + 3)
-
-
-def back_kernel(
-    att, dq, term, att_out, dq_out, dkv_out,
-    got1, sum1, got2, part, got3, final, send_sems, recv_sems, local_sems,
-):
-    here = Here()
-    z, y, xh = here.z, here.y, here.xh
-    x2 = flip2(here.x)
-    greet(
-        [here.at(z=f(z)) for f in (flip1, flip3, flip2)]
-        + [here.at(y=f(y)) for f in (flip1, flip3, flip2)]
-        + [here.at(x=x2)]
-    )
-    net = Net(send_sems, recv_sems)
-
-    def along(s, value):
-        return here.at(z=value) if s == 0 else here.at(y=value)
-
-    def across(s, value):
-        return here.at(y=value) if s == 0 else here.at(z=value)
-
-    head = [z, y]
-    ring = [y, z]
-    flips = ((flip3, flip1), (flip1, flip3))
-
-    def slots(value):
-        return pl.ds(value * 2, 2)
-
-    one = {}
-    for j in (1, 0):
-        for s in range(2):
-            for half in range(2):
-                f, g = flips[half]
-                target = f(ring[s])
-                slot = target if j == 0 else g(target)
-                one[s, half, j] = net.start(
-                    term.at[s, slots(slot), 2 * half : 2 * half + 2],
-                    got1.at[s, half, j],
-                    across(s, target),
-                )
-    rest = []
-    local = []
-    for f in (flip1, flip3, flip2):
-        for s in range(2):
-            to = f(head[s])
-            for src, dst in ((att, att_out), (dq, dq_out)):
-                rest.append(net.start(src.at[s, to], dst.at[s, :, cols(head[s], 512)], along(s, to)))
-    for s in range(2):
-        for src, dst in ((att, att_out), (dq, dq_out)):
-            copy = pltpu.make_async_copy(
-                src.at[s, head[s]], dst.at[s, :, cols(head[s], 512)], local_sems.at[len(local)]
-            )
-            copy.start()
-            local.append(copy)
-
-    two = {}
-    for s in range(2):
-        for half in range(2):
-            f, g = flips[half]
-            one[s, half, 1].wait_recv()
-            sum1[s, half] = (
-                term[s, slots(g(ring[s])), 2 * half : 2 * half + 2].astype(F32)
-                + got1[s, half, 1].astype(F32)
-            ).astype(BF)
-            two[s, half] = net.start(sum1.at[s, half], got2.at[s, half], across(s, g(ring[s])))
-    three = []
-    for s in range(2):
-        for half in range(2):
-            one[s, half, 0].wait_recv()
-            two[s, half].wait_recv()
-            part[s, :, 2 * half : 2 * half + 2] = (
-                term[s, slots(ring[s]), 2 * half : 2 * half + 2].astype(F32)
-                + got1[s, half, 0].astype(F32)
-                + got2[s, half].astype(F32)
-            ).astype(BF)
-        three.append(net.start(part.at[s, 1 - xh], got3.at[s], here.at(x=x2)))
-    for s in range(2):
-        three[s].wait_recv()
-        final[s] = (part[s, xh].astype(F32) + got3[s].astype(F32)).astype(BF)
-        for f in (flip1, flip3, flip2):
-            to = f(head[s])
-            rest.append(net.start(final.at[s, to], dkv_out.at[s, :, cols(head[s], 256)], along(s, to)))
-        copy = pltpu.make_async_copy(
-            final.at[s, head[s]], dkv_out.at[s, :, cols(head[s], 256)], local_sems.at[len(local)]
-        )
-        copy.start()
-        local.append(copy)
-    for copy in rest:
-        copy.wait_recv()
-    for copy in local:
-        copy.wait()
-    net.finish()
-
-
-def back(att, dq, term):
-    vm = pl.BlockSpec(memory_space=VM)
-    return pl.pallas_call(
-        back_kernel,
-        name="back",
-        out_shape=(
-            jax.ShapeDtypeStruct((2, 64, 2048), BF),
-            jax.ShapeDtypeStruct((2, 64, 2048), BF),
-            jax.ShapeDtypeStruct((2, 64, 1024), BF),
-        ),
-        in_specs=[vm] * 3,
-        out_specs=(vm,) * 3,
-        scratch_shapes=[
-            VM((2, 2, 2, 2, 2, 64, 256), BF),
-            VM((2, 2, 2, 2, 64, 256), BF),
-            VM((2, 2, 2, 2, 64, 256), BF),
-            VM((2, 2, 4, 64, 256), BF),
-            VM((2, 4, 64, 256), BF),
-            VM((2, 4, 64, 256), BF),
-            pltpu.SemaphoreType.DMA((N_BACK,)),
-            pltpu.SemaphoreType.DMA((N_BACK,)),
-            pltpu.SemaphoreType.DMA((6,)),
-        ],
-        compiler_params=pltpu.CompilerParams(collective_id=2, has_side_effects=True),
-    )(att, dq, term)
-
-
-def outer_kernel(n0_ref, n1_ref, g0_ref, g1_ref, out_ref):
-    n = jnp.concatenate([n0_ref[...], n1_ref[...]], axis=0)
-    g = jnp.concatenate([g0_ref[...], g1_ref[...]], axis=0)
-    w = lax.dot_general(n, g, (((0,), (0,)), ((), ())), preferred_element_type=F32).astype(BF)
-    for x in range(4):
-        for u in range(4):
-            at = x * 64 + u * 16
-            out_ref[u, 0, x] = w[at : at + 16]
-
-
-def outer(n0, n1, g0, g1):
-    n_spec = pl.BlockSpec((128, 256), lambda i: (0, i))
-    g_spec = pl.BlockSpec((128, 512), lambda i: (0, 0))
-    return pl.pallas_call(
-        outer_kernel,
-        name="outer",
-        grid=(16,),
-        out_shape=jax.ShapeDtypeStruct((4, 16, 4, 16, 512), BF),
-        in_specs=[n_spec, n_spec, g_spec, g_spec],
-        out_specs=pl.BlockSpec((4, 1, 4, 16, 512), lambda i: (0, i, 0, 0, 0)),
-        compiler_params=pltpu.CompilerParams(dimension_semantics=("arbitrary",)),
-        cost_estimate=pl.CostEstimate(
-            flops=1_080_000_000, bytes_accessed=6_500_000, transcendentals=0
-        ),
-    )(n0, n1, g0, g1)
-
-
 PARTS = (
     (0, 0, 128, "zyx", True),
     (1, 0, 128, "yxz", True),
@@ -474,20 +380,166 @@
     (3, 0, 256, "zyx", True),
     (3, 256, 256, "yxz", True),
 )
+N_BACK = 2 * (2 * 3 + 4 + 2 + 1 + 3)
 N_SUM = 9 * len(PARTS) + 8 + 1
-
-
-def sum_kernel(
-    g, gain, out, gain_out,
-    r0, s0, r1, s1, r2, s2, r3, s3, r4, s4, r5, full, gain_got, gain_sent, send_sems, recv_sems,
+N_TAIL = N_BACK + N_SUM + 1
+
+
+def tail_kernel(
+    att, dq, term_hbm, tokens_hbm, norm_hbm, rms_in, norm_gain, key_w, value_w, cos, sin,
+    att_out, dq_out, rows_out, out, gain_out,
+    term, tokens, norm_t, kw, vw, got1, sum1, got2, part, got3, final, dkv_out,
+    grads, got_grad, big, wide_grad, gain,
+    r0, s0, r1, s1, r2, s2, r3, s3, r4, s4, r5, full, gain_got, gain_sent,
+    send_sems, recv_sems, local_sems, load_sems,
 ):
     here = Here()
     place = {"z": here.z, "y": here.y, "x": here.x}
+    z, y, xh = here.z, here.y, here.xh
+    x2 = flip2(here.x)
     greet(
-        [here.at(**{a: f(place[a])}) for a in "zyx" for f in (flip1, flip3)]
+        [here.at(**{a: f(place[a])}) for a in "zy" for f in (flip1, flip3, flip2)]
+        + [here.at(x=f(here.x)) for f in (flip1, flip3, flip2)]
         + [here.at(core=1 - here.core)]
     )
     net = Net(send_sems, recv_sems)
+    loads = []
+    for k, (src, dst) in enumerate(
+        ((term_hbm, term), (norm_hbm, norm_t), (tokens_hbm, tokens), (key_w, kw), (value_w, vw))
+    ):
+        loads.append(pltpu.make_async_copy(src, dst, load_sems.at[k]))
+
+    def along(s, value):
+        return here.at(z=value) if s == 0 else here.at(y=value)
+
+    def across(s, value):
+        return here.at(y=value) if s == 0 else here.at(z=value)
+
+    head = [z, y]
+    ring = [y, z]
+    flips = ((flip3, flip1), (flip1, flip3))
+
+    def slots(value):
+        return pl.ds(value * 2, 2)
+
+    one = {}
+    for j in (1, 0):
+        for s in range(2):
+            for half in range(2):
+                f, g = flips[half]
+                target = f(ring[s])
+                slot = target if j == 0 else g(target)
+                one[s, half, j] = net.start(
+                    term_hbm.at[s, slots(slot), 2 * half : 2 * half + 2],
+                    got1.at[s, half, j],
+                    across(s, target),
+                )
+    for copy in loads:
+        copy.start()
+    rest = []
+    local = []
+    for f in (flip1, flip3, flip2):
+        for s in range(2):
+            to = f(head[s])
+            for src, dst in ((att, att_out), (dq, dq_out)):
+                rest.append(net.start(src.at[s, to], dst.at[s, :, cols(head[s], 512)], along(s, to)))
+    for s in range(2):
+        for src, dst in ((att, att_out), (dq, dq_out)):
+            copy = pltpu.make_async_copy(
+                src.at[s, head[s]], dst.at[s, :, cols(head[s], 512)], local_sems.at[len(local)]
+            )
+            copy.start()
+            local.append(copy)
+
+    loads[0].wait()
+    two = {}
+    for s in range(2):
+        for half in range(2):
+            f, g = flips[half]
+            one[s, half, 1].wait_recv()
+            sum1[s, half] = (
+                term[s, slots(g(ring[s])), 2 * half : 2 * half + 2].astype(F32)
+                + got1[s, half, 1].astype(F32)
+            ).astype(BF)
+            two[s, half] = net.start(sum1.at[s, half], got2.at[s, half], across(s, g(ring[s])))
+    three = []
+    for s in range(2):
+        for half in range(2):
+            one[s, half, 0].wait_recv()
+            two[s, half].wait_recv()
+            part[s, :, 2 * half : 2 * half + 2] = (
+                term[s, slots(ring[s]), 2 * half : 2 * half + 2].astype(F32)
+                + got1[s, half, 0].astype(F32)
+                + got2[s, half].astype(F32)
+            ).astype(BF)
+        three.append(net.start(part.at[s, 1 - xh], got3.at[s], here.at(x=x2)))
+    four = []
+    for s in range(2):
+        three[s].wait_recv()
+        final[s] = (part[s, xh].astype(F32) + got3[s].astype(F32)).astype(BF)
+        for f in (flip1, flip3, flip2):
+            to = f(head[s])
+            four.append(net.start(final.at[s, to], dkv_out.at[s, :, cols(head[s], 256)], along(s, to)))
+        copy = pltpu.make_async_copy(
+            final.at[s, head[s]], dkv_out.at[s, :, cols(head[s], 256)], local_sems.at[len(local)]
+        )
+        copy.start()
+        local.append(copy)
+    for copy in four:
+        copy.wait_recv()
+    for copy in local[4:]:
+        copy.wait()
+
+    both_cos = jnp.concatenate([cos[...], cos[...]], axis=0)
+    both_sin = jnp.concatenate([sin[...], sin[...]], axis=0)
+    for h in range(KV_HEADS):
+        at = slice(h * 128, (h + 1) * 128)
+        u = jnp.concatenate([dkv_out[s, :, h * 256 : h * 256 + 128] for s in range(2)], axis=0)
+        v = jnp.concatenate([dkv_out[s, :, h * 256 + 128 : (h + 1) * 256] for s in range(2)], axis=0)
+        u = u.astype(F32)
+        grads[0, :, at] = (u * both_cos - pltpu.roll(u, 64, 1) * both_sin).astype(BF)
+        grads[1, :, at] = v
+    swap_grad = net.start(grads.at[1 - here.core], got_grad, here.at(core=1 - here.core))
+    loads[1].wait()
+    swap_grad.wait_recv()
+    pair = jnp.concatenate([grads[here.core], got_grad[...]], axis=0)
+
+    @pl.loop(0, 16)
+    def _(i):
+        at = pl.ds(pl.multiple_of(i * 256, 256), 256)
+        n = jnp.concatenate([norm_t[0, at, :], norm_t[1, at, :]], axis=1)
+        w = jnp.dot(n, pair, preferred_element_type=F32).astype(BF)
+        for x in range(4):
+            for u in range(4):
+                row = x * 64 + u * 16
+                big[u, i // 4, i % 4, x] = w[row : row + 16]
+
+    def backward_rows():
+        for copy in loads[2:]:
+            copy.wait()
+        rms = rms_in[:, :1]
+        key_grad, value_grad = grads[0], grads[1]
+        nt = (((1,), (1,)), ((), ()))
+        inner = jnp.zeros((128, 128), F32)
+        for c in range(16):
+            at = slice(c * 256, (c + 1) * 256)
+            ng = lax.dot_general(key_grad, kw[at, :], nt, preferred_element_type=F32)
+            ng = ng + lax.dot_general(value_grad, vw[at, :], nt, preferred_element_type=F32)
+            t = tokens[:, at].astype(F32)
+            wide_grad[:, at] = ng
+            across_rows = jnp.sum(ng * t * rms, axis=0, keepdims=True)
+            weighted = ng * norm_gain[:, at] * t
+            inner = inner + weighted[:, :128] + weighted[:, 128:]
+            for k in range(2):
+                row = c * 2 + k
+                gain[row // 8, row % 8 : row % 8 + 1, :] = across_rows[:, k * 128 : (k + 1) * 128]
+        mean = jnp.sum(inner, axis=1, keepdims=True) / 4096.0
+        cube = rms**3 * mean
+        for c in range(16):
+            at = slice(c * 256, (c + 1) * 256)
+            rows_out[:, at] = (
+                rms * norm_gain[:, at] * wide_grad[:, at] - tokens[:, at].astype(F32) * cube
+            ).astype(BF)
 
     def device(axis, value):
         return here.at(**{axis: value})
@@ -553,15 +605,15 @@
             if step == 0:
                 to = device(a0, f(m0))
                 waits[p, 0, 1] = net.start(
-                    slab(g, u, a0, flip2(m0), lanes), r0.at[u, 1, :, :, :, lanes], to
+                    slab(big, u, a0, flip2(m0), lanes), r0.at[u, 1, :, :, :, lanes], to
                 )
                 waits[p, 0, 0] = net.start(
-                    slab(g, u, a0, f(m0), lanes), r0.at[u, 0, :, :, :, lanes], to
+                    slab(big, u, a0, f(m0), lanes), r0.at[u, 0, :, :, :, lanes], to
                 )
             elif step == 1:
                 waits[p, 0, 1].wait_recv()
                 s0[u, :, :, :, lanes] = (
-                    wide(slab(g, u, a0, f2(m0), lanes)) + r0[u, 1, :, :, :, lanes].astype(F32)
+                    wide(slab(big, u, a0, f2(m0), lanes)) + r0[u, 1, :, :, :, lanes].astype(F32)
                 ).astype(BF)
                 waits[p, 1] = net.start(
                     s0.at[u, :, :, :, lanes], r1.at[u, :, :, :, lanes], device(a0, f2(m0))
@@ -570,7 +622,7 @@
                 waits[p, 0, 0].wait_recv()
                 waits[p, 1].wait_recv()
                 s1[u, :, :, :, lanes] = (
-                    wide(slab(g, u, a0, m0, lanes))
+                    wide(slab(big, u, a0, m0, lanes))
                     + r0[u, 0, :, :, :, lanes].astype(F32)
                     + r1[u, :, :, :, lanes].astype(F32)
                 ).astype(BF)
@@ -610,6 +662,8 @@
                 waits[p, 5] = net.start(
                     s4.at[u, :, lanes], r5.at[u, :, lanes], device(a2, f2(m2))
                 )
+        if step == 0:
+            backward_rows()
         gain_step(step)
     for p, (u, lanes, f, f2, a0, a1, a2, leading) in enumerate(plans):
         waits[p, 4, 0].wait_recv()
@@ -625,41 +679,70 @@
     gain_step(7)
     gain_out[...] = gain_sent[7]
     swap.wait_recv()
+    for copy in rest:
+        copy.wait_recv()
+    for copy in local[:4]:
+        copy.wait()
     net.finish()
 
 
-def sum_everywhere(g, gain):
+def tail(att, dq, term, tokens, norm_t, rms, norm_gain, key_w, value_w, cos, sin):
     vm = pl.BlockSpec(memory_space=VM)
-    tail = (16, 512)
+    any_ = pl.BlockSpec(memory_space=pl.ANY)
+    end = (16, 512)
     return pl.pallas_call(
-        sum_kernel,
-        name="sum_everywhere",
+        tail_kernel,
+        name="tail",
         out_shape=(
-            jax.ShapeDtypeStruct((2, 2, *tail), F32),
+            jax.ShapeDtypeStruct((2, 64, 2048), BF),
+            jax.ShapeDtypeStruct((2, 64, 2048), BF),
+            jax.ShapeDtypeStruct((128, 4096), BF),
+            jax.ShapeDtypeStruct((2, 2, *end), F32),
             jax.ShapeDtypeStruct((8, 128), F32),
         ),
-        in_specs=[vm] * 2,
-        out_specs=(vm,) * 2,
+        in_specs=[any_] * 5 + [vm] * 2 + [any_] * 2 + [vm] * 2,
+        out_specs=(vm,) * 5,
         scratch_shapes=[
-            VM((4, 2, 4, 4, *tail), BF),
-            VM((4, 4, 4, *tail), BF),
-            VM((4, 4, 4, *tail), BF),
-            VM((4, 4, 4, *tail), BF),
-            VM((4, 2, 4, *tail), BF),
-            VM((4, 4, *tail), BF),
-            VM((4, 4, *tail), BF),
-            VM((4, 4, *tail), BF),
-            VM((4, 2, *tail), BF),
-            VM((4, *tail), BF),
-            VM((4, *tail), BF),
-            VM((2, 2, *tail), F32),
+            VM((2, 8, 4, 64, 256), BF),
+            VM((128, 4096), BF),
+            VM((2, 4096, 128), BF),
+            VM((4096, 512), BF),
+            VM((4096, 512), BF),
+            VM((2, 2, 2, 2, 2, 64, 256), BF),
+            VM((2, 2, 2, 2, 64, 256), BF),
+            VM((2, 2, 2, 2, 64, 256), BF),
+            VM((2, 2, 4, 64, 256), BF),
+            VM((2, 4, 64, 256), BF),
+            VM((2, 4, 64, 256), BF),
+            VM((2, 64, 1024), BF),
+            VM((2, 128, 512), BF),
+            VM((128, 512), BF),
+            VM((4, 4, 4, 4, *end), BF),
+            VM((128, 4096), F32),
+            VM((4, 8, 128), F32),
+            VM((4, 2, 4, 4, *end), BF),
+            VM((4, 4, 4, *end), BF),
+            VM((4, 4, 4, *end), BF),
+            VM((4, 4, 4, *end), BF),
+            VM((4, 2, 4, *end), BF),
+            VM((4, 4, *end), BF),
+            VM((4, 4, *end), BF),
+            VM((4, 4, *end), BF),
+            VM((4, 2, *end), BF),
+            VM((4, *end), BF),
+            VM((4, *end), BF),
+            VM((2, 2, *end), F32),
             VM((8, 8, 128), F32),
             VM((8, 8, 128), F32),
-            pltpu.SemaphoreType.DMA((N_SUM,)),
-            pltpu.SemaphoreType.DMA((N_SUM,)),
+            pltpu.SemaphoreType.DMA((N_TAIL,)),
+            pltpu.SemaphoreType.DMA((N_TAIL,)),
+            pltpu.SemaphoreType.DMA((6,)),
+            pltpu.SemaphoreType.DMA((5,)),
         ],
-        compiler_params=pltpu.CompilerParams(collective_id=3, has_side_effects=True),
-    )(g, gain)
+        compiler_params=pltpu.CompilerParams(
+            collective_id=2, has_side_effects=True, vmem_limit_bytes=60 * 2**20
+        ),
+    )(att, dq, term, tokens, norm_t, rms, norm_gain, key_w, value_w, cos, sin)
 
 
 def rotation(token_pos, head_size):
@@ -670,28 +753,16 @@
     return (jnp.cos(angles), jnp.sin(angles))
 
 
-def rotate_half(values):
-    half_dim = values.shape[-1] // 2
-    return jnp.concatenate([-values[..., half_dim:], values[..., :half_dim]], axis=-1)
-
-
-def rotate_back(values):
-    half_dim = values.shape[-1] // 2
-    return jnp.concatenate([values[..., half_dim:], -values[..., :half_dim]], axis=-1)
-
-
 def body(tokens, queries, d_attended, span_order, norm_gain, key_weight, value_weight):
     seqs, rows, width = tokens.shape
     count = seqs * rows
     ctx = lax.axis_index("ctx")
-    core = lax.axis_index("dp") % 2
     z, y, xh = ctx // 8, (ctx // 2) % 4, ctx % 2
     offsets = jnp.arange(rows // 2, dtype=jnp.int32)
     token_pos = (span_order[:, None] * (rows // 2) + offsets[None, :]).reshape(-1)
     own_pos = lax.dynamic_slice_in_dim(token_pos, ctx * rows, rows, 0)
     cosine, sine = rotation(own_pos, HEAD_DIM)
-    cosine = jnp.tile(cosine, (seqs, 1))[:, None, :]
-    sine = jnp.tile(sine, (seqs, 1))[:, None, :]
+    sine = jnp.concatenate([-sine[:, : HEAD_DIM // 2], sine[:, HEAD_DIM // 2 :]], axis=1)
 
     placed = token_pos.reshape(4, 4, 2, rows)
     q_pos = jnp.stack([placed[:, y, xh], placed[z, :, xh]])
@@ -702,35 +773,15 @@
     k_pos = jnp.broadcast_to(k_pos[:, :, None], (*k_pos.shape, 128))
 
     flat = tokens.reshape(count, width)
-    wide = flat.astype(F32)
-    rms = lax.rsqrt(jnp.mean(wide * wide, axis=-1, keepdims=True) + EPSILON)
-    normed = (wide * rms * norm_gain).astype(BF)
-    key_pre = jnp.dot(normed, key_weight, preferred_element_type=F32).reshape(count, KV_HEADS, -1)
-    keys = (key_pre * cosine + rotate_half(key_pre) * sine).astype(BF)
-    values = jnp.dot(normed, value_weight, preferred_element_type=F32).astype(BF)
-    kv = jnp.stack([keys, values.reshape(count, KV_HEADS, HEAD_DIM)], axis=2)
-    kv = kv.reshape(seqs, rows, 2 * KV_HEADS * HEAD_DIM)
-
-    qr, dr, kvr, other = front(queries, d_attended, kv, normed)
+    gain_row = norm_gain.reshape(1, width)
+    qr, dr, kvr, norm_t, rms = front(
+        queries, d_attended, flat, gain_row, key_weight, value_weight, cosine, sine
+    )
     att, dq, term = attend(qr, dr, kvr.reshape(seqs, -1, 256), q_pos, k_pos)
-    attended, grad_queries, dkv = back(att, dq, term.reshape(seqs, 8, 4, rows, 256))
-
-    dkv = dkv.reshape(count, KV_HEADS, 2, HEAD_DIM).astype(F32)
-    shaped = dkv[:, :, 0]
-    key_grad = (shaped * cosine + rotate_back(shaped * sine)).reshape(count, -1).astype(BF)
-    value_grad = dkv[:, :, 1].reshape(count, -1).astype(BF)
-    own = jnp.where(core == 0, key_grad, value_grad)
-    sent = jnp.where(core == 0, value_grad, key_grad)
-    got = lax.ppermute(sent, "dp", [(0, 1), (1, 0), (2, 3), (3, 2)])
-    normed_grad = jnp.dot(key_grad, key_weight.T, preferred_element_type=F32) + jnp.dot(
-        value_grad, value_weight.T, preferred_element_type=F32
+    attended, grad_queries, grad_rows, weights, gain = tail(
+        att, dq, term.reshape(seqs, 8, 4, rows, 256), flat, norm_t, rms, gain_row,
+        key_weight, value_weight, cosine, sine,
     )
-    gain_part = jnp.sum(normed_grad * wide * rms, axis=0)
-    inner = jnp.mean(normed_grad * norm_gain * wide, axis=-1, keepdims=True)
-    grad_rows = (rms * norm_gain * normed_grad - wide * rms**3 * inner).astype(BF)
-
-    g = outer(normed, other, own, got).reshape(4, 4, 4, 4, 16, 512)
-    weights, gain = sum_everywhere(g, gain_part.reshape(4, 8, 128))
     weights = weights.reshape(2, 32, 512)
     gain = lax.dynamic_slice(gain, (ctx % 8, lax.axis_index("dp") * 32), (1, 32))
     return (

time: 178 us -> 148 us (0.83)
  matrix products: 10.4 us -> 0 us
  local copies, waits for them, and re-layouts: 21.7 us -> 15.6 us
  other arithmetic: 8.46 us -> 2.53 us
  starting transfers between devices: 5.4 us -> 0 us
    dot_general x4 -> x0, matrix products: 10.4 us -> none  [the longest x1 3.81 us: body(): jnp.dot(key_grad, key_weight.T, preferred_element_type=F32)]
    dot_general x1 -> x0, local copies, waits for them, and re-layouts: 6.45 us -> none  [body(): jnp.dot(normed, key_weight, preferred_element_type=F32)]
    ppermute x1 -> x0, starting transfers between devices: 5.4 us -> none  [body(): got = lax.ppermute(sent, 'dp', [(0, 1), (1, 0), (2, 3), (3, 2)])]
    pallas_call x3 -> x1, Pallas kernels: 74.5 us -> 69.7 us  [tail(): pl.pallas_call(tail_kernel, name='tail', out_shape=(jax.ShapeDtypeStruct(...]
    unnamed x33 -> x15, local copies, waits for them, and re-layouts: 5.53 us -> 9.7 us
    pallas_call x1, Pallas kernels: 30 us -> 33.8 us  [front(): pl.pallas_call(front_kernel, name='front', out_shape=(jax.ShapeDtypeStruc...]
    convert_element_type x3 -> x0, other arithmetic: 2.94 us -> none  [the longest x1 2.29 us: body(): (rms * norm_gain * normed_grad - wide * rms ** 3 * inner).astype(BF)]
  transfers between devices with their start and end apart: 1 -> 0, of which waited for: 0 -> 0; matrix products, arithmetic and copies ran while one was open for 6% -> 0% of each run, Pallas kernels for 0% -> 0%
where the time goes in v2:
time: 148 us
  Pallas kernels  129 us (87%)
  local copies, waits for them, and re-layouts  15.6 us (11%)
  other arithmetic  2.53 us (2%)
    pallas_call x1, Pallas kernels, tail(): pl.pallas_call(tail_kernel, name='tail', out_shape=(jax.ShapeDtypeStruct(...  69.7 us
    pallas_call x1, Pallas kernels, front(): pl.pallas_call(front_kernel, name='front', out_shape=(jax.ShapeDtypeStruc...  33.8 us
    pallas_call x1, Pallas kernels, attend(): pl.pallas_call(attend_kernel, name='attend', grid=(2, 4), out_shape=(jax....  25.2 us
    unnamed x15, local copies, waits for them, and re-layouts  9.7 us

profile of v2, /device:TPU:1, one launch (start us, length us, event | category | flops | bytes accessed | tf_op | source)
XLA Modules:
  0.0 147.7 jit_solution(1828019743983229622)
XLA Ops:
  0.7 0.7 broadcast_multiply_fusion.1
  1.4 0.1 add.72
  1.5 0.1 add.68
  1.6 0.1 add.69
  1.7 0.1 add.70
  1.9 0.1 tile.9.qpos_ref
  2.0 0.1 stack_reshape.7
  2.1 0.1 stack_reshape.6
  2.2 0.1 iota_add_fusion
  2.3 0.1 add.66
  2.3 0.1 dynamic-slice_convert_fusion
  2.4 0.1 broadcast_multiply_fusion
  2.5 0.8 fusion
  3.3 0.1 slice_negate_fusion
  3.4 0.7 pad_maximum_fusion.1.sin
  4.1 2.3 %broadcast_in_dim.2.kpos_ref = s32[2,2048,128]{2,1,0:T(8,128)} broadcast(s32[2,2048]{1,0:T(2,128)S(1)} %pad_add_fusion), dimensions={0,1} | broadcast | bytes 2113536 | tf_op jit(solution)/shard_map/broadcast_in_dim | solution.py:773
  6.4 33.8 %front.1 = (bf16[2,4,64,512]{3,2,1,0:T(8,128)(2,1)}, bf16[2,4,64,512]{3,2,1,0:T(8,128)(2,1)}, bf16[2,8,4,64,256]{4,3,2,1,0:T(8,128)(2,1)}, bf16[2,4096,128]{2,1,0:T(8,128)(2,1)}, f32[128,128]{1,0:T(8,128)}) custom-call(bf16[2,64,2048]{2,1,0:T(8,128)(2,1)} %q.1, bf16[2,64,2048]{2,1,0:T(8,128)(2,1)} %do.1, bf16[128,4096]{1,0:T(8,128)(2,1)} %bitcast.19, ...), custom_call_target="tpu_custom_call" | custom-call | tf_op jit(solution)/shard_map/front/pallas_call | solution.py:230
  40.2 0.0 copy-start.3
  40.2 1.0 copy-done.3
  41.2 1.0 copy-done.4
  42.3 25.2 %attend.1 = (bf16[2,4,64,512]{3,2,1,0:T(8,128)(2,1)S(1)}, bf16[2,4,64,512]{3,2,1,0:T(8,128)(2,1)S(1)}, bf16[2,2048,256]{2,1,0:T(8,128)(2,1)S(1)}) custom-call(bf16[2,4,64,512]{3,2,1,0:T(8,128)(2,1)S(1)} %copy-done.3, bf16[2,4,64,512]{3,2,1,0:T(8,128)(2,1)S(1)} %copy-done.4, bf16[2,2048,256]{2,1,0:T(8,128)(2,1)} %bitcast.27, ...), custom_call_target="tpu_custom_call" | custom-call | flops 6499999744 | bytes 12000000 | tf_op jit(solution)/shard_map/attend/pallas_call | solution.py:339
  67.5 0.0 copy-start
  67.5 1.3 copy-done
  68.8 0.8 copy-done.1
  69.6 0.8 copy-done.2
  70.4 69.7 %tail.1 = (bf16[2,64,2048]{2,1,0:T(8,128)(2,1)}, bf16[2,64,2048]{2,1,0:T(8,128)(2,1)}, bf16[128,4096]{1,0:T(8,128)(2,1)}, f32[2,2,16,512]{3,2,1,0:T(8,128)}, f32[8,128]{1,0:T(8,128)}) custom-call(bf16[2,4,64,512]{3,2,1,0:T(8,128)(2,1)} %copy-done.1, bf16[2,4,64,512]{3,2,1,0:T(8,128)(2,1)} %copy-done.2, bf16[2,8,4,64,256]{4,3,2,1,0:T(8,128)(2,1)} %bitcast.18, ...), custom_call_target="tpu_custom_call" | custom-call | tf_op jit(solution)/shard_map/tail/pallas_call | solution.py:693
  140.0 0.0 copy-start.5
  140.0 1.4 dynamic-slice_bitcast_fusion.1
  141.4 1.5 %fusion.2 = (f32[1,2,16,512]{3,2,1,0:T(8,128)}, f32[1,2,16,512]{3,2,1,0:T(8,128)}) fusion(f32[2,2,16,512]{3,2,1,0:T(8,128)} %get-tuple-element.30), kind=kLoop, calls=%fused_computation.16 | loop fusion | bytes 262144 | tf_op jit(solution)/shard_map/slice | solution.py:792
  142.9 1.9 %copy.20 = bf16[2,64,2048]{2,1,0:T(8,128)(2,1)} copy(bf16[2,64,2048]{2,1,0:T(8,128)(2,1)} %get-tuple-element.44) | data formatting | bytes 1048576
  144.8 1.9 %copy.21 = bf16[2,64,2048]{2,1,0:T(8,128)(2,1)} copy(bf16[2,64,2048]{2,1,0:T(8,128)(2,1)} %get-tuple-element.45) | data formatting | bytes 1048576
  146.7 1.0 copy.22
  (16 shorter events, 0.1 us)
Async XLA Ops:
  40.2 1.0 copy-start.3
  41.2 1.0 copy-start.4
  67.5 1.3 copy-start
  68.8 0.8 copy-start.1
  69.6 0.8 copy-start.2
  140.0 6.7 %copy-start.5 = (bf16[128,4096]{1,0:T(8,128)(2,1)S(1)}, bf16[128,4096]{1,0:T(8,128)(2,1)}, u32[]{:S(2)}) copy-start(bf16[128,4096]{1,0:T(8,128)(2,1)} %get-tuple-element.29) | copy-start | bytes 3145732

commit v3 on v2

--- a/solution.py
+++ b/solution.py
@@ -88,7 +88,7 @@
     return pl.ds(pl.multiple_of(index * width, width), width)
 
 
-N_FRONT = 2 * 3 * 3 + 2 * (1 + 2 * (2 + 4)) + 1
+N_FRONT = 2 * 3 * 3 + 2 * (2 + 2 * (2 + 4)) + 1
 PIECES = 8
 
 
@@ -192,11 +192,10 @@
     first = [[], []]
     last = []
 
-    def spread(s, xh_of):
-        slot = ring[s] * 2 + xh_of
-        for half, f in ((0, flip1), (1, flip3)):
-            block = kvr.at[s, slot, 2 * half : 2 * half + 2]
-            first[s].append(net.start(block, block, across(s, f(ring[s]))))
+    def spread(s, xh_of, half):
+        f = (flip1, flip3)[half]
+        block = kvr.at[s, ring[s] * 2 + xh_of, 2 * half : 2 * half + 2]
+        first[s].append(net.start(block, block, across(s, f(ring[s]))))
 
     def spread_on(s, xh_of):
         for half, f, g in ((0, flip1, flip3), (1, flip3, flip1)):
@@ -205,16 +204,20 @@
                 block = kvr.at[s, value * 2 + xh_of, 2 * half : 2 * half + 2]
                 last.append(net.start(block, block, across(s, g(ring[s]))))
 
-    swapped = []
-    for s in range(2):
-        block = kvr.at[s, mine[s]]
-        swapped.append(net.start(block, block, here.at(x=x2)))
-        spread(s, xh)
+    swapped = {}
+    for half in range(2):
+        for s in range(2):
+            block = kvr.at[s, mine[s], 2 * half : 2 * half + 2]
+            swapped[s, half] = net.start(block, block, here.at(x=x2))
+    for half in range(2):
+        for s in range(2):
+            spread(s, xh, half)
     for s in range(2):
         spread_on(s, xh)
-    for s in range(2):
-        swapped[s].wait_recv()
-        spread(s, 1 - xh)
+    for half in range(2):
+        for s in range(2):
+            swapped[s, half].wait_recv()
+            spread(s, 1 - xh, half)
     for s in range(2):
         spread_on(s, 1 - xh)
     for copy in last + rest:
@@ -251,7 +254,7 @@
             pltpu.SemaphoreType.DMA((2 * PIECES,)),
         ],
         compiler_params=pltpu.CompilerParams(
-            collective_id=1, has_side_effects=True, vmem_limit_bytes=56 * 2**20
+            collective_id=1, has_side_effects=True, vmem_limit_bytes=60 * 1024 * 1024
         ),
     )(q, do, tokens, gain, key_w, value_w, cos, sin)
 
@@ -261,113 +264,207 @@
 
 
 def attend_kernel(
-    q_ref, do_ref, kv_ref, qpos_ref, kpos_ref, att_ref, dq_ref, term_ref,
-    score, prob, key_t, value_t, acc_k, acc_v,
+    spans, q_ref, do_ref, kv_ref, att_ref, dq_ref, term_ref,
+    score, prob, kv_s, key_t, value_t, acc_k, acc_v, picked,
 ):
-    block = pl.program_id(1)
+    seq = pl.program_id(0)
+    pair = pl.program_id(1)
     chunks = KEYS // CHUNK
     scale = HEAD_DIM ** (-0.5)
     to_two = scale * math.log2(math.e)
 
-    @pl.when(block == 0)
+    def key_span(i):
+        a, xh, b, half = i // 16, (i // 8) % 2, (i // 2) % 4, i % 2
+        along_z = ((b * 4 + a) * 2 + xh) * 2 + half
+        along_y = ((a * 4 + b) * 2 + xh) * 2 + half
+        return spans[jnp.where(seq == 0, along_z, along_y)]
+
+    def span_rows(span):
+        return pl.ds(pl.multiple_of(span * 32, 32), 32)
+
+    @pl.when(pair == 0)
     def _():
-        key_t[...] = kv_ref[0, :, :128].T
-        value_t[...] = kv_ref[0, :, 128:].T
+        for i in range(64):
+            kv_s[span_rows(key_span(i)), :] = kv_ref[0, i * 32 : (i + 1) * 32, :]
+
+        key_t[...] = kv_s[:, :128].T
+        value_t[...] = kv_s[:, 128:].T
         acc_k[...] = jnp.zeros_like(acc_k)
         acc_v[...] = jnp.zeros_like(acc_v)
-
-    q = jnp.concatenate([q_ref[0, 0, :, h * 128 : (h + 1) * 128] for h in range(4)], axis=0)
-    do = jnp.concatenate([do_ref[0, 0, :, h * 128 : (h + 1) * 128] for h in range(4)], axis=0)
+        here = Here()
+        start = jnp.where(seq == 0, here.y * 4, here.z * 16) + here.xh * 2
+        stride = jnp.where(seq == 0, 16, 4)
+        own = [spans[start + stride * (i // 2) + i % 2] for i in range(8)]
+        for i in range(8):
+            rank = jnp.int32(0)
+            for j in range(8):
+                if j != i:
+                    rank = rank + (own[j] < own[i]).astype(jnp.int32)
+            picked[rank] = i
+            picked[8 + rank] = own[i]
+
+    first, second = picked[2 * pair], picked[2 * pair + 1]
+    low, high = picked[8 + 2 * pair], picked[8 + 2 * pair + 1]
+
+    def stack(ref):
+        a, b = ref[0, first], ref[0, second]
+        return jnp.concatenate(
+            [r[:, h * 128 : (h + 1) * 128] for h in range(4) for r in (a, b)], axis=0
+        )
+
+    q = stack(q_ref)
+    do = stack(do_ref)
     q_t = q.T
     do_t = do.T
-    q_pos = qpos_ref[0, 0]
-
-    def rows(c):
-        return pl.ds(pl.multiple_of(c * CHUNK, CHUNK), CHUNK)
-
-    def scores_of(c, top):
-        s = jnp.dot(kv_ref[0, rows(c), :128], q_t, preferred_element_type=F32)
-        k_pos = kpos_ref[0, rows(c), :]
-        k_pos = jnp.concatenate([k_pos, k_pos], axis=1)
-        s = jnp.where(k_pos <= q_pos, s, -1e30)
-        score[rows(c), :] = s
-        return jnp.maximum(top, jnp.max(s.reshape(CHUNK // 8, 8, 256), axis=0))
-
-    top = lax.fori_loop(0, chunks, scores_of, jnp.full((8, 256), -1e30, F32), unroll=True)
-    top = jnp.max(top, axis=0, keepdims=True)
-
-    def exps_of(c, total):
-        e = jnp.exp2((score[rows(c), :] - top) * to_two)
-        score[rows(c), :] = e
-        return total + jnp.sum(e.reshape(CHUNK // 8, 8, 256), axis=0)
-
-    total = lax.fori_loop(0, chunks, exps_of, jnp.zeros((8, 256), F32), unroll=True)
-    inverse = 1.0 / jnp.sum(total, axis=0, keepdims=True)
-
-    def attended_of(c, out):
-        p = (score[rows(c), :] * inverse).astype(BF)
-        prob[rows(c), :] = p
-        return out + jnp.dot(value_t[:, rows(c)], p, preferred_element_type=F32)
-
-    out_t = lax.fori_loop(0, chunks, attended_of, jnp.zeros((128, 256), F32), unroll=True)
-    out_t = out_t.astype(BF)
-    delta = jnp.sum(out_t.astype(F32) * do_t.astype(F32), axis=0, keepdims=True)
-
-    def grads_of(c, dq_t):
-        dp = jnp.dot(kv_ref[0, rows(c), 128:], do_t, preferred_element_type=F32)
-        ds = (score[rows(c), :] * inverse * (dp - delta)).astype(BF)
-        acc_k[rows(c), :] += jnp.dot(ds, q, preferred_element_type=F32)
-        acc_v[rows(c), :] += jnp.dot(prob[rows(c), :], do, preferred_element_type=F32)
-        return dq_t + jnp.dot(key_t[:, rows(c)], ds, preferred_element_type=F32)
-
-    dq_t = lax.fori_loop(0, chunks, grads_of, jnp.zeros((128, 256), F32), unroll=True)
-    out = out_t.T
-    dq = (dq_t * scale).astype(BF).T
-    for h in range(4):
-        att_ref[0, 0, :, h * 128 : (h + 1) * 128] = out[h * 64 : (h + 1) * 64]
-        dq_ref[0, 0, :, h * 128 : (h + 1) * 128] = dq[h * 64 : (h + 1) * 64]
-
-    @pl.when(block == 3)
+    lane = lax.broadcasted_iota(jnp.int32, (1, 256), 1)
+    q_pos = lane % 32 + 32 * jnp.where(lane % 64 < 32, low, high)
+
+    def run(count):
+        key_at = lax.broadcasted_iota(jnp.int32, (CHUNK, 256), 0)
+        top = jnp.full((8, 256), -1e30, F32)
+        for c in range(count):
+            rows = slice(c * CHUNK, (c + 1) * CHUNK)
+            s = jnp.dot(kv_s[rows, :128], q_t, preferred_element_type=F32)
+            s = jnp.where(key_at <= q_pos - c * CHUNK, s, -1e30)
+            score[rows, :] = s
+            top = jnp.maximum(top, jnp.max(s.reshape(CHUNK // 8, 8, 256), axis=0))
+        top = jnp.max(top, axis=0, keepdims=True)
+        total = jnp.zeros((8, 256), F32)
+        for c in range(count):
+            rows = slice(c * CHUNK, (c + 1) * CHUNK)
+            e = jnp.exp2((score[rows, :] - top) * to_two)
+            score[rows, :] = e
+            total = total + jnp.sum(e.reshape(CHUNK // 8, 8, 256), axis=0)
+        inverse = 1.0 / jnp.sum(total, axis=0, keepdims=True)
+        out_t = jnp.zeros((128, 256), F32)
+        for c in range(count):
+            rows = slice(c * CHUNK, (c + 1) * CHUNK)
+            p = (score[rows, :] * inverse).astype(BF)
+            prob[rows, :] = p
+            out_t = out_t + jnp.dot(value_t[:, rows], p, preferred_element_type=F32)
+        out_t = out_t.astype(BF)
+        delta = jnp.sum(out_t.astype(F32) * do_t.astype(F32), axis=0, keepdims=True)
+        dq_t = jnp.zeros((128, 256), F32)
+        for c in range(count):
+            rows = slice(c * CHUNK, (c + 1) * CHUNK)
+            dp = jnp.dot(kv_s[rows, 128:], do_t, preferred_element_type=F32)
+            ds = (score[rows, :] * inverse * (dp - delta)).astype(BF)
+            acc_k[rows, :] += jnp.dot(ds, q, preferred_element_type=F32)
+            acc_v[rows, :] += jnp.dot(prob[rows, :], do, preferred_element_type=F32)
+            dq_t = dq_t + jnp.dot(key_t[:, rows], ds, preferred_element_type=F32)
+        out = out_t.T
+        dq = (dq_t * scale).astype(BF).T
+        for h in range(4):
+            for k, span in enumerate((first, second)):
+                at = slice(h * 64 + k * 32, h * 64 + k * 32 + 32)
+                att_ref[0, span, :, h * 128 : (h + 1) * 128] = out[at]
+                dq_ref[0, span, :, h * 128 : (h + 1) * 128] = dq[at]
+
+    need = lax.shift_right_logical(high, 3) + 1
+    for count in range(1, chunks + 1):
+        pl.when(need == count)(functools.partial(run, count))
+
+    @pl.when(pair == 3)
     def _():
-        term_ref[0, :, :128] = (acc_k[...] * scale).astype(BF)
-        term_ref[0, :, 128:] = acc_v[...].astype(BF)
-
-
-def attend(qr, dr, kvr, q_pos, k_pos):
-    rows = pl.BlockSpec((1, 1, 64, 512), lambda s, b: (s, b, 0, 0))
+        for i in range(64):
+            rows = span_rows(key_span(i))
+            term_ref[0, i * 32 : (i + 1) * 32, :128] = (acc_k[rows, :] * scale).astype(BF)
+            term_ref[0, i * 32 : (i + 1) * 32, 128:] = acc_v[rows, :].astype(BF)
+
+
+def attend(spans, qr, dr, kvr):
+    rows = pl.BlockSpec((1, 8, 32, 512), lambda s, b: (s, 0, 0, 0))
     whole = pl.BlockSpec((1, KEYS, 256), lambda s, b: (s, 0, 0))
     return pl.pallas_call(
         attend_kernel,
         name="attend",
         grid=(2, 4),
         out_shape=(
-            jax.ShapeDtypeStruct((2, 4, 64, 512), BF),
-            jax.ShapeDtypeStruct((2, 4, 64, 512), BF),
+            jax.ShapeDtypeStruct((2, 8, 32, 512), BF),
+            jax.ShapeDtypeStruct((2, 8, 32, 512), BF),
             jax.ShapeDtypeStruct((2, KEYS, 256), BF),
         ),
-        in_specs=[
-            rows,
-            rows,
-            whole,
-            pl.BlockSpec((1, 1, 1, 256), lambda s, b: (s, b, 0, 0)),
-            pl.BlockSpec((1, KEYS, 128), lambda s, b: (s, 0, 0)),
-        ],
+        in_specs=[pl.BlockSpec(memory_space=pltpu.SMEM), rows, rows, whole],
         out_specs=(rows, rows, whole),
         scratch_shapes=[
             VM((KEYS, 256), F32),
+            VM((KEYS, 256), BF),
             VM((KEYS, 256), BF),
             VM((128, KEYS), BF),
             VM((128, KEYS), BF),
             VM((KEYS, 128), F32),
             VM((KEYS, 128), F32),
+            pltpu.SMEM((16,), jnp.int32),
         ],
         compiler_params=pltpu.CompilerParams(
-            dimension_semantics=("arbitrary", "arbitrary"), vmem_limit_bytes=48 * 2**20
+            dimension_semantics=("arbitrary", "arbitrary"), vmem_limit_bytes=60 * 1024 * 1024
         ),
         cost_estimate=pl.CostEstimate(
-            flops=6_500_000_000, bytes_accessed=12_000_000, transcendentals=4_200_000
+            flops=6_500_000_000, bytes_accessed=8_000_000, transcendentals=4_200_000
         ),
-    )(qr, dr, kvr, q_pos, k_pos)
+    )(spans, qr, dr, kvr)
+
+
+def finish_kernel(
+    att, dq, rows, weights, gain, att_to, dq_to, rows_to, keys_to, values_to, gain_to,
+    att_v, dq_v, rows_v, weights_v, gain_v, sems,
+):
+    here = Here()
+    loads = []
+    for k, (src, dst) in enumerate(
+        ((gain, gain_v), (att, att_v), (dq, dq_v), (rows, rows_v), (weights, weights_v))
+    ):
+        copy = pltpu.make_async_copy(src, dst, sems.at[k])
+        copy.start()
+        loads.append(copy)
+    loads[0].wait()
+    row = gain_v[pl.ds(here.y * 2 + here.xh, 1), :]
+    dp = here.xl * 2 + here.core
+    gain_to[...] = pltpu.roll(row, (128 - dp * 32) % 128, 1)[:, :32]
+    stores = []
+    for k, (load, src, dst) in enumerate(
+        (
+            (loads[1], att_v, att_to),
+            (loads[2], dq_v, dq_to),
+            (loads[3], rows_v, rows_to),
+            (loads[4], weights_v.at[0], keys_to),
+            (None, weights_v.at[1], values_to),
+        )
+    ):
+        if load is not None:
+            load.wait()
+        copy = pltpu.make_async_copy(src, dst, sems.at[5 + k])
+        copy.start()
+        stores.append(copy)
+    for copy in stores:
+        copy.wait()
+
+
+def finish(att, dq, rows, weights, gain):
+    any_ = pl.BlockSpec(memory_space=pl.ANY)
+    return pl.pallas_call(
+        finish_kernel,
+        name="finish",
+        out_shape=(
+            jax.ShapeDtypeStruct((2, 64, 2048), BF),
+            jax.ShapeDtypeStruct((2, 64, 2048), BF),
+            jax.ShapeDtypeStruct((128, 4096), BF),
+            jax.ShapeDtypeStruct((32, 512), F32),
+            jax.ShapeDtypeStruct((32, 512), F32),
+            jax.ShapeDtypeStruct((1, 32), F32),
+        ),
+        in_specs=[any_] * 5,
+        out_specs=(any_,) * 5 + (pl.BlockSpec(memory_space=VM),),
+        scratch_shapes=[
+            VM((2, 64, 2048), BF),
+            VM((2, 64, 2048), BF),
+            VM((128, 4096), BF),
+            VM((2, 32, 512), F32),
+            VM((8, 128), F32),
+            pltpu.SemaphoreType.DMA((10,)),
+        ],
+        compiler_params=pltpu.CompilerParams(vmem_limit_bytes=60 * 1024 * 1024),
+    )(att, dq, rows, weights, gain)
 
 
 PARTS = (
@@ -380,7 +477,7 @@
     (3, 0, 256, "zyx", True),
     (3, 256, 256, "yxz", True),
 )
-N_BACK = 2 * (2 * 3 + 4 + 2 + 1 + 3)
+N_BACK = 2 * (2 * 3 + 4 + 2 + 2 + 3)
 N_SUM = 9 * len(PARTS) + 8 + 1
 N_TAIL = N_BACK + N_SUM + 1
 
@@ -388,7 +485,7 @@
 def tail_kernel(
     att, dq, term_hbm, tokens_hbm, norm_hbm, rms_in, norm_gain, key_w, value_w, cos, sin,
     att_out, dq_out, rows_out, out, gain_out,
-    term, tokens, norm_t, kw, vw, got1, sum1, got2, part, got3, final, dkv_out,
+    term, tokens, norm_t, kw, vw, got1, sum1, got2, part, got3, final, whole, grad_rows,
     grads, got_grad, big, wide_grad, gain,
     r0, s0, r1, s1, r2, s2, r3, s3, r4, s4, r5, full, gain_got, gain_sent,
     send_sems, recv_sems, local_sems, load_sems,
@@ -436,6 +533,29 @@
                 )
     for copy in loads:
         copy.start()
+    loads[0].wait()
+    two = {}
+    for s in range(2):
+        for half in range(2):
+            f, g = flips[half]
+            one[s, half, 1].wait_recv()
+            sum1[s, half] = (
+                term[s, slots(g(ring[s])), 2 * half : 2 * half + 2].astype(F32)
+                + got1[s, half, 1].astype(F32)
+            ).astype(BF)
+            two[s, half] = net.start(sum1.at[s, half], got2.at[s, half], across(s, g(ring[s])))
+    three = {}
+    for half in range(2):
+        for s in range(2):
+            at = slice(2 * half, 2 * half + 2)
+            one[s, half, 0].wait_recv()
+            two[s, half].wait_recv()
+            part[s, :, at] = (
+                term[s, slots(ring[s]), at].astype(F32)
+                + got1[s, half, 0].astype(F32)
+                + got2[s, half].astype(F32)
+            ).astype(BF)
+            three[s, half] = net.start(part.at[s, 1 - xh, at], got3.at[s, at], here.at(x=x2))
     rest = []
     local = []
     for f in (flip1, flip3, flip2):
@@ -451,52 +571,26 @@
             copy.start()
             local.append(copy)
 
-    loads[0].wait()
-    two = {}
+    for half in range(2):
+        for s in range(2):
+            at = slice(2 * half, 2 * half + 2)
+            three[s, half].wait_recv()
+            final[s, at] = (part[s, xh, at].astype(F32) + got3[s, at].astype(F32)).astype(BF)
+    owners = []
     for s in range(2):
-        for half in range(2):
-            f, g = flips[half]
-            one[s, half, 1].wait_recv()
-            sum1[s, half] = (
-                term[s, slots(g(ring[s])), 2 * half : 2 * half + 2].astype(F32)
-                + got1[s, half, 1].astype(F32)
-            ).astype(BF)
-            two[s, half] = net.start(sum1.at[s, half], got2.at[s, half], across(s, g(ring[s])))
-    three = []
-    for s in range(2):
-        for half in range(2):
-            one[s, half, 0].wait_recv()
-            two[s, half].wait_recv()
-            part[s, :, 2 * half : 2 * half + 2] = (
-                term[s, slots(ring[s]), 2 * half : 2 * half + 2].astype(F32)
-                + got1[s, half, 0].astype(F32)
-                + got2[s, half].astype(F32)
-            ).astype(BF)
-        three.append(net.start(part.at[s, 1 - xh], got3.at[s], here.at(x=x2)))
-    four = []
-    for s in range(2):
-        three[s].wait_recv()
-        final[s] = (part[s, xh].astype(F32) + got3[s].astype(F32)).astype(BF)
-        for f in (flip1, flip3, flip2):
+        for f in (flip2, flip1, flip3):
             to = f(head[s])
-            four.append(net.start(final.at[s, to], dkv_out.at[s, :, cols(head[s], 256)], along(s, to)))
-        copy = pltpu.make_async_copy(
-            final.at[s, head[s]], dkv_out.at[s, :, cols(head[s], 256)], local_sems.at[len(local)]
-        )
-        copy.start()
-        local.append(copy)
-    for copy in four:
+            owners.append(net.start(final.at[s, to], whole.at[s, head[s]], along(s, to)))
+        whole[s, head[s]] = final[s, head[s]]
+    for copy in owners:
         copy.wait_recv()
-    for copy in local[4:]:
-        copy.wait()
 
     both_cos = jnp.concatenate([cos[...], cos[...]], axis=0)
     both_sin = jnp.concatenate([sin[...], sin[...]], axis=0)
     for h in range(KV_HEADS):
         at = slice(h * 128, (h + 1) * 128)
-        u = jnp.concatenate([dkv_out[s, :, h * 256 : h * 256 + 128] for s in range(2)], axis=0)
-        v = jnp.concatenate([dkv_out[s, :, h * 256 + 128 : (h + 1) * 256] for s in range(2)], axis=0)
-        u = u.astype(F32)
+        both = jnp.concatenate([whole[s, h] for s in range(2)], axis=0)
+        u, v = both[:, :128].astype(F32), both[:, 128:]
         grads[0, :, at] = (u * both_cos - pltpu.roll(u, 64, 1) * both_sin).astype(BF)
         grads[1, :, at] = v
     swap_grad = net.start(grads.at[1 - here.core], got_grad, here.at(core=1 - here.core))
@@ -504,7 +598,7 @@
     swap_grad.wait_recv()
     pair = jnp.concatenate([grads[here.core], got_grad[...]], axis=0)
 
-    @pl.loop(0, 16)
+    @pl.loop(0, 16, unroll=4)
     def _(i):
         at = pl.ds(pl.multiple_of(i * 256, 256), 256)
         n = jnp.concatenate([norm_t[0, at, :], norm_t[1, at, :]], axis=1)
@@ -537,7 +631,7 @@
         cube = rms**3 * mean
         for c in range(16):
             at = slice(c * 256, (c + 1) * 256)
-            rows_out[:, at] = (
+            grad_rows[:, at] = (
                 rms * norm_gain[:, at] * wide_grad[:, at] - tokens[:, at].astype(F32) * cube
             ).astype(BF)
 
@@ -664,6 +758,8 @@
                 )
         if step == 0:
             backward_rows()
+            keep_rows = pltpu.make_async_copy(grad_rows, rows_out, load_sems.at[5])
+            keep_rows.start()
         gain_step(step)
     for p, (u, lanes, f, f2, a0, a1, a2, leading) in enumerate(plans):
         waits[p, 4, 0].wait_recv()
@@ -681,8 +777,9 @@
     swap.wait_recv()
     for copy in rest:
         copy.wait_recv()
-    for copy in local[:4]:
+    for copy in local:
         copy.wait()
+    keep_rows.wait()
     net.finish()
 
 
@@ -701,7 +798,7 @@
             jax.ShapeDtypeStruct((8, 128), F32),
         ),
         in_specs=[any_] * 5 + [vm] * 2 + [any_] * 2 + [vm] * 2,
-        out_specs=(vm,) * 5,
+        out_specs=(any_,) * 3 + (vm,) * 2,
         scratch_shapes=[
             VM((2, 8, 4, 64, 256), BF),
             VM((128, 4096), BF),
@@ -714,7 +811,8 @@
             VM((2, 2, 4, 64, 256), BF),
             VM((2, 4, 64, 256), BF),
             VM((2, 4, 64, 256), BF),
-            VM((2, 64, 1024), BF),
+            VM((2, 4, 64, 256), BF),
+            VM((128, 4096), BF),
             VM((2, 128, 512), BF),
             VM((128, 512), BF),
             VM((4, 4, 4, 4, *end), BF),
@@ -736,11 +834,11 @@
             VM((8, 8, 128), F32),
             pltpu.SemaphoreType.DMA((N_TAIL,)),
             pltpu.SemaphoreType.DMA((N_TAIL,)),
+            pltpu.SemaphoreType.DMA((4,)),
             pltpu.SemaphoreType.DMA((6,)),
-            pltpu.SemaphoreType.DMA((5,)),
         ],
         compiler_params=pltpu.CompilerParams(
-            collective_id=2, has_side_effects=True, vmem_limit_bytes=60 * 2**20
+            collective_id=2, has_side_effects=True, vmem_limit_bytes=60 * 1024 * 1024
         ),
     )(att, dq, term, tokens, norm_t, rms, norm_gain, key_w, value_w, cos, sin)
 
@@ -757,39 +855,35 @@
     seqs, rows, width = tokens.shape
     count = seqs * rows
     ctx = lax.axis_index("ctx")
-    z, y, xh = ctx // 8, (ctx // 2) % 4, ctx % 2
-    offsets = jnp.arange(rows // 2, dtype=jnp.int32)
-    token_pos = (span_order[:, None] * (rows // 2) + offsets[None, :]).reshape(-1)
-    own_pos = lax.dynamic_slice_in_dim(token_pos, ctx * rows, rows, 0)
+    span_len = rows // 2
+    own_spans = lax.dynamic_slice_in_dim(span_order, ctx * 2, 2, 0)
+    own_pos = (own_spans[:, None] * span_len + jnp.arange(span_len, dtype=jnp.int32)).reshape(-1)
     cosine, sine = rotation(own_pos, HEAD_DIM)
     sine = jnp.concatenate([-sine[:, : HEAD_DIM // 2], sine[:, HEAD_DIM // 2 :]], axis=1)
-
-    placed = token_pos.reshape(4, 4, 2, rows)
-    q_pos = jnp.stack([placed[:, y, xh], placed[z, :, xh]])
-    q_pos = jnp.tile(q_pos, (1, 1, 4))[:, :, None, :]
-    k_pos = jnp.stack(
-        [placed.transpose(1, 2, 0, 3).reshape(-1), placed.transpose(0, 2, 1, 3).reshape(-1)]
-    )
-    k_pos = jnp.broadcast_to(k_pos[:, :, None], (*k_pos.shape, 128))
 
     flat = tokens.reshape(count, width)
     gain_row = norm_gain.reshape(1, width)
     qr, dr, kvr, norm_t, rms = front(
         queries, d_attended, flat, gain_row, key_weight, value_weight, cosine, sine
     )
-    att, dq, term = attend(qr, dr, kvr.reshape(seqs, -1, 256), q_pos, k_pos)
-    attended, grad_queries, grad_rows, weights, gain = tail(
-        att, dq, term.reshape(seqs, 8, 4, rows, 256), flat, norm_t, rms, gain_row,
+    att, dq, term = attend(
+        span_order, qr.reshape(2, 8, 32, 512), dr.reshape(2, 8, 32, 512), kvr.reshape(2, KEYS, 256)
+    )
+    done = tail(
+        att.reshape(2, 4, rows, 512), dq.reshape(2, 4, rows, 512),
+        term.reshape(2, 8, 4, rows, 256), flat, norm_t, rms, gain_row,
         key_weight, value_weight, cosine, sine,
     )
-    weights = weights.reshape(2, 32, 512)
-    gain = lax.dynamic_slice(gain, (ctx % 8, lax.axis_index("dp") * 32), (1, 32))
+    attended, grad_queries, grad_rows, weights, gain = done
+    attended, grad_queries, grad_rows, grad_keys, grad_values, gain = finish(
+        attended, grad_queries, grad_rows, weights.reshape(2, 32, 512), gain
+    )
     return (
         attended,
         grad_queries,
         grad_rows.reshape(seqs, rows, width),
-        weights[0],
-        weights[1],
+        grad_keys,
+        grad_values,
         gain.reshape(32),
     )
 

time: 148 us -> 125 us (0.84)
  local copies, waits for them, and re-layouts: 15.6 us -> 0.08 us
  Pallas kernels: 129 us -> 122 us
    unnamed x15 -> x0, local copies, waits for them, and re-layouts: 9.7 us -> none
    pallas_call x1, Pallas kernels: 69.7 us -> 63.9 us  [tail(): pl.pallas_call(tail_kernel, name='tail', out_shape=(jax.ShapeDtypeStruct(...]
    pallas_call x1, Pallas kernels: 25.2 us -> 20.7 us  [attend(): pl.pallas_call(attend_kernel, name='attend', grid=(2, 4), out_shape=(jax....]
    pallas_call x0 -> x1, Pallas kernels: none -> 3.15 us  [finish(): pl.pallas_call(finish_kernel, name='finish', out_shape=(jax.ShapeDtypeStr...]
    broadcast_in_dim x1 -> x0, local copies, waits for them, and re-layouts: 2.3 us -> none  [body(): k_pos = jnp.broadcast_to(k_pos[:, :, None], (*k_pos.shape, 128))]
    slice x1 -> x0, local copies, waits for them, and re-layouts: 1.53 us -> none  [body(): weights[1]]
where the time goes in v3:
time: 125 us
  Pallas kernels  122 us (98%)
  other arithmetic  2.49 us (2%)
    pallas_call x1, Pallas kernels, tail(): pl.pallas_call(tail_kernel, name='tail', out_shape=(jax.ShapeDtypeStruct(...  63.9 us
    pallas_call x1, Pallas kernels, front(): pl.pallas_call(front_kernel, name='front', out_shape=(jax.ShapeDtypeStruc...  34 us
    pallas_call x1, Pallas kernels, attend(): pl.pallas_call(attend_kernel, name='attend', grid=(2, 4), out_shape=(jax....  20.7 us
    pallas_call x1, Pallas kernels, finish(): pl.pallas_call(finish_kernel, name='finish', out_shape=(jax.ShapeDtypeStr...  3.15 us

profile of v3, /device:TPU:1, one launch (start us, length us, event | category | flops | bytes accessed | tf_op | source)
XLA Modules:
  0.0 125.2 jit_solution(9455627276839750593)
XLA Ops:
  0.6 0.7 dynamic-slice_multiply_fusion
  1.4 0.1 add_convert_fusion
  1.4 0.1 convert_element_type.11
  1.5 0.1 broadcast_multiply_fusion
  1.6 0.8 fusion
  2.4 0.1 slice_negate_fusion
  2.5 0.7 pad_maximum_fusion.1.sin
  3.2 34.0 %front.1 = (bf16[2,4,64,512]{3,2,1,0:T(8,128)(2,1)}, bf16[2,4,64,512]{3,2,1,0:T(8,128)(2,1)}, bf16[2,8,4,64,256]{4,3,2,1,0:T(8,128)(2,1)}, bf16[2,4096,128]{2,1,0:T(8,128)(2,1)}, f32[128,128]{1,0:T(8,128)}) custom-call(bf16[2,64,2048]{2,1,0:T(8,128)(2,1)} %q.1, bf16[2,64,2048]{2,1,0:T(8,128)(2,1)} %do.1, bf16[128,4096]{1,0:T(8,128)(2,1)} %bitcast.11, ...), custom_call_target="tpu_custom_call" | custom-call | tf_op jit(solution)/shard_map/front/pallas_call | solution.py:233
  37.3 20.7 %attend.1 = (bf16[2,8,32,512]{3,2,1,0:T(8,128)(2,1)}, bf16[2,8,32,512]{3,2,1,0:T(8,128)(2,1)}, bf16[2,2048,256]{2,1,0:T(8,128)(2,1)}) custom-call(s32[64]{0:T(128)} %spans.1, bf16[2,8,32,512]{3,2,1,0:T(8,128)(2,1)} %bitcast.21, bf16[2,8,32,512]{3,2,1,0:T(8,128)(2,1)} %bitcast.22, bf16[2,2048,256]{2,1,0:T(8,128)(2,1)} %bitcast.19), custom_call_target="tpu_custom_call" | custom-call | flops 6499999744 | bytes 8000000 | tf_op jit(solution)/shard_map/attend/pallas_call | solution.py:378
  58.0 63.9 %tail.1 = (bf16[2,64,2048]{2,1,0:T(8,128)(2,1)}, bf16[2,64,2048]{2,1,0:T(8,128)(2,1)}, bf16[128,4096]{1,0:T(8,128)(2,1)}, f32[2,2,16,512]{3,2,1,0:T(8,128)}, f32[8,128]{1,0:T(8,128)}) custom-call(bf16[2,4,64,512]{3,2,1,0:T(8,128)(2,1)} %bitcast.14, bf16[2,4,64,512]{3,2,1,0:T(8,128)(2,1)} %bitcast.15, bf16[2,8,4,64,256]{4,3,2,1,0:T(8,128)(2,1)} %bitcast.13, ...), custom_call_target="tpu_custom_call" | custom-call | tf_op jit(solution)/shard_map/tail/pallas_call | solution.py:790
  121.9 3.1 %finish.1 = (bf16[2,64,2048]{2,1,0:T(8,128)(2,1)}, bf16[2,64,2048]{2,1,0:T(8,128)(2,1)}, bf16[128,4096]{1,0:T(8,128)(2,1)}, f32[32,512]{1,0:T(8,128)}, f32[32,512]{1,0:T(8,128)}, /*index=5*/f32[1,32]{1,0:T(1,128)}) custom-call(bf16[2,64,2048]{2,1,0:T(8,128)(2,1)} %get-tuple-element.33.att, bf16[2,64,2048]{2,1,0:T(8,128)(2,1)} %get-tuple-element.34.dq, ...), custom_call_target="tpu_custom_call" | custom-call | tf_op jit(solution)/shard_map/finish/pallas_call | solution.py:445
  (1 shorter events, 0.0 us)

commit v4 on v0

v4 whole, which is shorter than its diff:
```python
import functools
import math

import jax
import jax.numpy as jnp
from jax import lax
from jax.experimental import pallas as pl
from jax.experimental.pallas import tpu as pltpu
from jax.sharding import PartitionSpec as P

KV_HEADS = 4
HEAD_DIM = 128
ROPE_BASE = 500000.0
EPSILON = 1e-05
BF = jnp.bfloat16
F32 = jnp.float32
VM = pltpu.VMEM
MESH = pl.DeviceIdType.MESH


def flip1(a):
    return a + 1 - 2 * (a % 2)


def flip3(a):
    return 3 - a


def flip2(a):
    return (a + 2) % 4


class Here:
    def __init__(self):
        ctx = lax.axis_index("ctx")
        dp = lax.axis_index("dp")
        self.z = ctx // 8
        self.y = (ctx // 2) % 4
        self.xh = ctx % 2
        self.xl = dp // 2
        self.core = dp % 2
        self.x = self.xh * 2 + self.xl

    def at(self, z=None, y=None, x=None, core=None):
        z = self.z if z is None else z
        y = self.y if y is None else y
        core = self.core if core is None else core
        if x is None:
            xh, xl = self.xh, self.xl
        else:
            xh, xl = x // 2, x % 2
        return {"ctx": z * 8 + y * 2 + xh, "dp": xl * 2 + core}


class Net:
    def __init__(self, send_sems, recv_sems):
        self.send_sems = send_sems
        self.recv_sems = recv_sems
        self.made = []

    def start(self, src, dst, device):
        k = len(self.made)
        copy = pltpu.make_async_remote_copy(
            src_ref=src,
            dst_ref=dst,
            send_sem=self.send_sems.at[k],
            recv_sem=self.recv_sems.at[k],
            device_id=device,
            device_id_type=MESH,
        )
        copy.start()
        self.made.append(copy)
        return copy

    def finish(self):
        for copy in self.made:
            copy.wait_send()


def greet(devices):
    barrier = pltpu.get_barrier_semaphore()
    for device in devices:
        pl.semaphore_signal(barrier, inc=1, device_id=device, device_id_type=MESH)
    pl.semaphore_wait(barrier, len(devices))


def cols(index, width):
    return pl.ds(pl.multiple_of(index * width, width), width)


KEYS = 2048
CHUNK = 256
PIECES = 8
PARTS = (
    (0, 0, 128, "zyx", True),
    (1, 0, 128, "yxz", True),
    (2, 0, 256, "xzy", True),
    (0, 128, 384, "zyx", False),
    (1, 128, 384, "yxz", False),
    (2, 256, 256, "xzy", False),
    (3, 0, 256, "zyx", True),
    (3, 256, 256, "yxz", True),
)
N_COPIES = 47 + 46 + 1 + 9 * len(PARTS) + 10 + 1
SHAPES = dict(
    kw=((4096, 512), BF),
    vw=((4096, 512), BF),
    normed=((128, 4096), BF),
    acc=((2, 128, 512), F32),
    kv=((2, 64, 1024), BF),
    norm_t=((2, 4096, 128), BF),
    qr=((2, 4, 64, 512), BF),
    dr=((2, 4, 64, 512), BF),
    kvr=((2, 8, 4, 64, 256), BF),
    key_pos=((2, KEYS, 128), jnp.int32),
    score=((KEYS, 256), F32),
    prob=((KEYS, 256), BF),
    key_t=((128, KEYS), BF),
    value_t=((128, KEYS), BF),
    acc_k=((KEYS, 128), F32),
    acc_v=((KEYS, 128), F32),
    att=((2, 4, 64, 512), BF),
    dq=((2, 4, 64, 512), BF),
    term=((2, 8, 4, 64, 256), BF),
    got1=((2, 2, 2, 2, 2, 64, 256), BF),
    sum1=((2, 2, 2, 2, 64, 256), BF),
    got2=((2, 2, 2, 2, 64, 256), BF),
    part=((2, 4, 64, 256), BF),
    got3=((2, 4, 64, 256), BF),
    final=((2, 4, 64, 256), BF),
    whole=((2, 4, 64, 256), BF),
    grads=((2, 128, 512), BF),
    got_grad=((128, 512), BF),
    big=((4, 4, 4, 4, 16, 512), BF),
    wide_grad=((128, 4096), F32),
    grad_rows=((128, 4096), BF),
    gain=((4, 8, 128), F32),
    r0=((4, 2, 4, 4, 16, 512), BF),
    s0=((4, 4, 4, 16, 512), BF),
    r1=((4, 4, 4, 16, 512), BF),
    s1=((4, 4, 4, 16, 512), BF),
    r2=((4, 3, 4, 16, 512), BF),
    s3=((4, 4, 16, 512), BF),
    r4=((4, 3, 16, 512), BF),
    full=((2, 2, 16, 512), F32),
    gain_got=((10, 8, 128), F32),
    gain_sum=((3, 8, 128), F32),
)


class Box:
    pass


def layer_kernel(
    spans, q, do, tokens, norm_gain, key_w, value_w, cos, sin,
    att_out, dq_out, rows_out, out, gain_out, *scratch,
):
    b = Box()
    for name, ref in zip(SHAPES, scratch):
        setattr(b, name, ref)
    send_sems, recv_sems, local_sems, weight_sems = scratch[len(SHAPES) :]
    here = Here()
    place = {"z": here.z, "y": here.y, "x": here.x}
    z, y, xh = here.z, here.y, here.xh
    x2 = flip2(here.x)
    twin = here.at(core=1 - here.core)
    turns = (flip1, flip3, flip2)
    piece = 4096 // PIECES
    loads = []
    for c in range(PIECES):
        for w, (src, dst) in enumerate(((key_w, b.kw), (value_w, b.vw))):
            at = pl.ds(c * piece, piece)
            copy = pltpu.make_async_copy(src.at[at], dst.at[at], weight_sems.at[2 * c + w])
            copy.start()
            loads.append(copy)
    greet([here.at(**{a: f(place[a])}) for a in "zyx" for f in turns] + [twin])
    net = Net(send_sems, recv_sems)

    def along(s, value):
        return here.at(z=value) if s == 0 else here.at(y=value)

    def across(s, value):
        return here.at(y=value) if s == 0 else here.at(z=value)

    head = [z, y]
    ring = [y, z]
    mine = [ring[s] * 2 + xh for s in range(2)]
    local = []

    def keep(src, dst):
        copy = pltpu.make_async_copy(src, dst, local_sems.at[len(local)])
        copy.start()
        local.append(copy)
        return copy

    rows_in = [[], []]

    def send_rows(s, src, dst):
        for f in turns:
            to = f(head[s])
            rows_in[s].append(
                net.start(src.at[s, :, cols(to, 512)], dst.at[s, head[s]], along(s, to))
            )
        rows_in[s].append(keep(src.at[s, :, cols(head[s], 512)], dst.at[s, head[s]]))

    def arrived(copy):
        if any(copy is c for c in local):
            copy.wait()
        else:
            copy.wait_recv()

    for s in range(2):
        send_rows(s, q, b.qr)
    squares = jnp.zeros((128, 128), F32)
    for c in range(32):
        t = tokens[:, c * 128 : (c + 1) * 128].astype(F32)
        squares = squares + t * t
    rms = lax.rsqrt(jnp.sum(squares, axis=1, keepdims=True) / 4096.0 + EPSILON)
    for c in range(PIECES):
        at = slice(c * piece, (c + 1) * piece)
        b.normed[:, at] = (tokens[:, at].astype(F32) * rms * norm_gain[:, at]).astype(BF)
    for c in range(PIECES):
        at = slice(c * piece, (c + 1) * piece)
        n = b.normed[:, at]
        for w, ref in enumerate((b.kw, b.vw)):
            loads[2 * c + w].wait()
            product = jnp.dot(n, ref[at, :], preferred_element_type=F32)
            if c == 0:
                b.acc[w] = product
            else:
                b.acc[w] += product

    def widen(half):
        both = jnp.concatenate([half, half], axis=1)
        return jnp.concatenate([both, both], axis=0)

    lane = lax.broadcasted_iota(jnp.int32, (128, 128), 1)
    both_cos = widen(cos[...])
    both_sin = widen(sin[...])
    both_sin = jnp.where(lane < 64, -both_sin, both_sin)
    for h in range(KV_HEADS):
        at = slice(h * 128, (h + 1) * 128)
        u = b.acc[0, :, at]
        k = (u * both_cos + pltpu.roll(u, 64, 1) * both_sin).astype(BF)
        v = b.acc[1, :, at].astype(BF)
        for s in range(2):
            b.kv[s, :, h * 256 : h * 256 + 128] = k[s * 64 : (s + 1) * 64]
            b.kv[s, :, h * 256 + 128 : (h + 1) * 256] = v[s * 64 : (s + 1) * 64]

    kv_in = [[], []]
    for s in range(2):
        for f in (flip2, flip1, flip3):
            to = f(head[s])
            kv_in[s].append(
                net.start(b.kv.at[s, :, cols(to, 256)], b.kvr.at[s, mine[s], head[s]], along(s, to))
            )
        kv_in[s].append(keep(b.kv.at[s, :, cols(head[s], 256)], b.kvr.at[s, mine[s], head[s]]))
    send_rows(0, do, b.dr)
    for c in range(32):
        at = slice(c * 128, (c + 1) * 128)
        b.norm_t[0, at, :] = b.normed[:, at].T

    first = {}
    last = [[], []]
    swapped = {}

    def spread(s, of, half):
        f = (flip1, flip3)[half]
        block = b.kvr.at[s, ring[s] * 2 + (xh if of == 0 else 1 - xh), 2 * half : 2 * half + 2]
        first[s, of, half] = net.start(block, block, across(s, f(ring[s])))

    def spread_on(s, of):
        for half, f, g in ((0, flip1, flip3), (1, flip3, flip1)):
            first[s, of, half].wait_recv()
            for value in (ring[s], f(ring[s])):
                slot = value * 2 + (xh if of == 0 else 1 - xh)
                block = b.kvr.at[s, slot, 2 * half : 2 * half + 2]
                last[s].append(net.start(block, block, across(s, g(ring[s]))))

    def gather_own(s):
        for copy in kv_in[s]:
            arrived(copy)
        for half in range(2):
            block = b.kvr.at[s, mine[s], 2 * half : 2 * half + 2]
            swapped[s, half] = net.start(block, block, here.at(x=x2))
        for half in range(2):
            spread(s, 0, half)

    def gather_swapped(s):
        for half in range(2):
            swapped[s, half].wait_recv()
            spread(s, 1, half)

    gather_own(0)
    gather_own(1)
    norm_in = net.start(b.norm_t.at[0], b.norm_t.at[1], twin)
    offset = lax.broadcasted_iota(jnp.int32, (32, 128), 0)
    for i in range(64):
        m, w, n, half = i // 16, (i // 8) % 2, (i // 2) % 4, i % 2
        for s in range(2):
            zz, yy = (n, m) if s == 0 else (m, n)
            span = spans[((zz * 4 + yy) * 2 + w) * 2 + half]
            b.key_pos[s, i * 32 : (i + 1) * 32, :] = offset + span * 32
    spread_on(0, 0)
    send_rows(1, do, b.dr)
    gather_swapped(0)
    spread_on(0, 1)
    spread_on(1, 0)

    scale = HEAD_DIM ** (-0.5)
    to_two = scale * math.log2(math.e)
    slots_of = [slice(c * CHUNK, (c + 1) * CHUNK) for c in range(KEYS // CHUNK)]
    returned = []

    def keys_of(s, c):
        return b.kvr[s, c, :, :, :128].reshape(CHUNK, 128)

    def values_of(s, c):
        return b.kvr[s, c, :, :, 128:].reshape(CHUNK, 128)

    def ready(s):
        for copy in last[s]:
            copy.wait_recv()
        for copy in rows_in[s]:
            arrived(copy)
        for c, rows in enumerate(slots_of):
            b.key_t[:, rows] = keys_of(s, c).T
            b.value_t[:, rows] = values_of(s, c).T

    def stack(ref, s, block):
        both = ref[s, block]
        return jnp.concatenate([both[:, h * 128 : (h + 1) * 128] for h in range(4)], axis=0)

    def attention(s, order):
        f = (flip1, flip3, flip2, lambda a: a)[order]
        block = f(head[s])
        queries = stack(b.qr, s, block)
        grads = stack(b.dr, s, block)
        q_t = queries.T
        do_t = grads.T
        start = (block * 4 + y) * 4 + xh * 2 if s == 0 else (z * 4 + block) * 4 + xh * 2
        column = lax.broadcasted_iota(jnp.int32, (1, 256), 1)
        q_pos = column % 32 + 32 * jnp.where(column % 64 < 32, spans[start], spans[start + 1])
        top = jnp.full((8, 256), -1e30, F32)
        for c, rows in enumerate(slots_of):
            t = jnp.dot(keys_of(s, c), q_t, preferred_element_type=F32)
            k_pos = b.key_pos[s, rows, :]
            k_pos = jnp.concatenate([k_pos, k_pos], axis=1)
            t = jnp.where(k_pos <= q_pos, t, -1e30)
            b.score[rows, :] = t
            top = jnp.maximum(top, jnp.max(t.reshape(CHUNK // 8, 8, 256), axis=0))
        top = jnp.max(top, axis=0, keepdims=True)
        total = jnp.zeros((8, 256), F32)
        for rows in slots_of:
            e = jnp.exp2((b.score[rows, :] - top) * to_two)
            b.score[rows, :] = e
            total = total + jnp.sum(e.reshape(CHUNK // 8, 8, 256), axis=0)
        inverse = 1.0 / jnp.sum(total, axis=0, keepdims=True)
        out_t = jnp.zeros((128, 256), F32)
        for rows in slots_of:
            p = (b.score[rows, :] * inverse).astype(BF)
            b.prob[rows, :] = p
            out_t = out_t + jnp.dot(b.value_t[:, rows], p, preferred_element_type=F32)
        out_t = out_t.astype(BF)
        delta = jnp.sum(out_t.astype(F32) * do_t.astype(F32), axis=0, keepdims=True)
        dq_t = jnp.zeros((128, 256), F32)
        for c, rows in enumerate(slots_of):
            dp = jnp.dot(values_of(s, c), do_t, preferred_element_type=F32)
            ds = (b.score[rows, :] * inverse * (dp - delta)).astype(BF)
            k_term = jnp.dot(ds, queries, preferred_element_type=F32)
            v_term = jnp.dot(b.prob[rows, :], grads, preferred_element_type=F32)
            if order > 0:
                k_term = k_term + b.acc_k[rows, :]
                v_term = v_term + b.acc_v[rows, :]
            if order < 3:
                b.acc_k[rows, :] = k_term
                b.acc_v[rows, :] = v_term
            else:
                b.term[s, c, :, :, :128] = (k_term * scale).astype(BF).reshape(4, 64, 128)
                b.term[s, c, :, :, 128:] = v_term.astype(BF).reshape(4, 64, 128)
            dq_t = dq_t + jnp.dot(b.key_t[:, rows], ds, preferred_element_type=F32)
        attended = out_t.T
        dq = (dq_t * scale).astype(BF).T
        for h in range(4):
            at = slice(h * 64, (h + 1) * 64)
            b.att[s, block, :, h * 128 : (h + 1) * 128] = attended[at]
            b.dq[s, block, :, h * 128 : (h + 1) * 128] = dq[at]
        for src, dst in ((b.att, att_out), (b.dq, dq_out)):
            dst = dst.at[s, :, cols(head[s], 512)]
            if order < 3:
                returned.append(net.start(src.at[s, block], dst, along(s, block)))
            else:
                returned.append(keep(src.at[s, block], dst))

    flips = ((flip3, flip1), (flip1, flip3))
    one, two, three, owners = {}, {}, {}, [[], []]

    def half_of(half):
        return slice(2 * half, 2 * half + 2)

    def side(k):
        return 1 - xh if k == 0 else xh

    def sum_one(s, k):
        for j in (1, 0):
            for half in range(2):
                f, g = flips[half]
                target = f(ring[s])
                slot = target if j == 0 else g(target)
                one[s, half, j, k] = net.start(
                    b.term.at[s, slot * 2 + side(k), half_of(half)],
                    b.got1.at[s, half, j, k],
                    across(s, target),
                )

    def sum_two(s, k):
        for half in range(2):
            f, g = flips[half]
            one[s, half, 1, k].wait_recv()
            b.sum1[s, half, k] = (
                b.term[s, g(ring[s]) * 2 + side(k), half_of(half)].astype(F32)
                + b.got1[s, half, 1, k].astype(F32)
            ).astype(BF)
            two[s, half, k] = net.start(
                b.sum1.at[s, half, k], b.got2.at[s, half, k], across(s, g(ring[s]))
            )

    def summed(s, half, k):
        one[s, half, 0, k].wait_recv()
        two[s, half, k].wait_recv()
        return (
            b.term[s, ring[s] * 2 + side(k), half_of(half)].astype(F32)
            + b.got1[s, half, 0, k].astype(F32)
            + b.got2[s, half, k].astype(F32)
        )

    def sum_three(s):
        for half in range(2):
            at = half_of(half)
            b.part[s, at] = summed(s, half, 0).astype(BF)
            three[s, half] = net.start(b.part.at[s, at], b.got3.at[s, at], here.at(x=x2))

    def sum_four(s):
        for half in range(2):
            at = half_of(half)
            total = summed(s, half, 1)
            three[s, half].wait_recv()
            b.final[s, at] = (total + b.got3[s, at].astype(F32)).astype(BF)
        for f in (flip2, flip1, flip3):
            to = f(head[s])
            owners[s].append(
                net.start(b.final.at[s, to], b.whole.at[s, head[s]], along(s, to))
            )
        b.whole[s, head[s]] = b.final[s, head[s]]

    def rotate_rows(s):
        for copy in owners[s]:
            copy.wait_recv()
        rows = slice(s * 64, (s + 1) * 64)
        for h in range(KV_HEADS):
            at = slice(h * 128, (h + 1) * 128)
            u = b.whole[s, h, :, :128].astype(F32)
            b.grads[0, rows, at] = (
                u * both_cos[:64] - pltpu.roll(u, 64, 1) * both_sin[:64]
            ).astype(BF)
            b.grads[1, rows, at] = b.whole[s, h, :, 128:]

    ready(0)
    attention(0, 0)
    gather_swapped(1)
    attention(0, 1)
    spread_on(1, 1)
    attention(0, 2)
    attention(0, 3)
    sum_one(0, 0)
    sum_one(0, 1)
    ready(1)
    attention(1, 0)
    sum_two(0, 0)
    sum_two(0, 1)
    attention(1, 1)
    sum_three(0)
    attention(1, 2)
    sum_four(0)
    attention(1, 3)
    sum_one(1, 0)
    rotate_rows(0)
    sum_two(1, 0)
    sum_one(1, 1)
    sum_three(1)
    sum_two(1, 1)
    sum_four(1)
    rotate_rows(1)

    swap_grad = net.start(b.grads.at[1 - here.core], b.got_grad, twin)
    norm_in.wait_recv()
    swap_grad.wait_recv()
    pair = jnp.concatenate([b.grads[here.core], b.got_grad[...]], axis=0)

    @pl.loop(0, 16, unroll=4)
    def _(i):
        at = pl.ds(pl.multiple_of(i * 256, 256), 256)
        n = jnp.concatenate([b.norm_t[0, at, :], b.norm_t[1, at, :]], axis=1)
        w = jnp.dot(n, pair, preferred_element_type=F32).astype(BF)
        for x in range(4):
            for u in range(4):
                row = x * 64 + u * 16
                b.big[u, i // 4, i % 4, x] = w[row : row + 16]

    def backward_rows():
        key_grad, value_grad = b.grads[0], b.grads[1]
        nt = (((1,), (1,)), ((), ()))
        inner = jnp.zeros((128, 128), F32)
        for c in range(16):
            at = slice(c * 256, (c + 1) * 256)
            ng = lax.dot_general(key_grad, b.kw[at, :], nt, preferred_element_type=F32)
            ng = ng + lax.dot_general(value_grad, b.vw[at, :], nt, preferred_element_type=F32)
            t = tokens[:, at].astype(F32)
            b.wide_grad[:, at] = ng
            across_rows = jnp.sum(ng * t * rms, axis=0, keepdims=True)
            weighted = ng * norm_gain[:, at] * t
            inner = inner + weighted[:, :128] + weighted[:, 128:]
            for k in range(2):
                row = c * 2 + k
                b.gain[row // 8, row % 8 : row % 8 + 1, :] = across_rows[:, k * 128 : (k + 1) * 128]
        mean = jnp.sum(inner, axis=1, keepdims=True) / 4096.0
        cube = rms**3 * mean
        for c in range(16):
            at = slice(c * 256, (c + 1) * 256)
            b.grad_rows[:, at] = (
                rms * norm_gain[:, at] * b.wide_grad[:, at] - tokens[:, at].astype(F32) * cube
            ).astype(BF)

    def device(axis, value):
        return here.at(**{axis: value})

    plans = []
    for u, lo, width, order, up in PARTS:
        f, f2 = (flip1, flip3) if up else (flip3, flip1)
        a0, a1, a2 = order
        left = [a for a in "zyx" if a != a0]
        plans.append((u, pl.ds(lo, width), f, f2, a0, a1, a2, left.index(a1) == 0))

    def slab(u, axis, value, lanes):
        if axis == "z":
            return b.big.at[u, value, :, :, :, lanes]
        if axis == "y":
            return b.big.at[u, :, value, :, :, lanes]
        return b.big.at[u, :, :, value, :, lanes]

    def slab1(u, value, lanes, leading):
        return b.s1.at[u, value, :, :, lanes] if leading else b.s1.at[u, :, value, :, lanes]

    def wide(ref):
        return ref[...].astype(F32)

    gains = []

    def gain_step(step):
        if step == 0:
            tiles = [b.gain.at[f(z)] for f in turns]
            own = None
        else:
            own = b.gain[z] if step == 1 else b.gain_sum[step - 2]
            for k in range(3):
                gains[k].wait_recv()
                own = own + b.gain_got[3 * (step - 1) + k]
            del gains[:]
            b.gain_sum[step - 1] = own
            tiles = [b.gain_sum.at[step - 1]] * 3
        if step < 3:
            axis = "zyx"[step]
            for k, f in enumerate(turns):
                gains.append(
                    net.start(tiles[k], b.gain_got.at[3 * step + k], device(axis, f(place[axis])))
                )
        else:
            gains.append(net.start(tiles[0], b.gain_got.at[9], twin))

    waits = {}
    for j in (1, 0):
        for p, (u, lanes, f, f2, a0, a1, a2, leading) in enumerate(plans):
            m0 = place[a0]
            slot = flip2(m0) if j == 1 else f(m0)
            waits[p, 0, j] = net.start(
                slab(u, a0, slot, lanes), b.r0.at[u, j, :, :, :, lanes], device(a0, f(m0))
            )
    backward_rows()
    keep_rows = keep(b.grad_rows, rows_out)
    gain_step(0)
    for p, (u, lanes, f, f2, a0, a1, a2, leading) in enumerate(plans):
        m0 = place[a0]
        waits[p, 0, 1].wait_recv()
        b.s0[u, :, :, :, lanes] = (
            wide(slab(u, a0, f2(m0), lanes)) + b.r0[u, 1, :, :, :, lanes].astype(F32)
        ).astype(BF)
        waits[p, 1] = net.start(
            b.s0.at[u, :, :, :, lanes], b.r1.at[u, :, :, :, lanes], device(a0, f2(m0))
        )
    gain_step(1)
    for p, (u, lanes, f, f2, a0, a1, a2, leading) in enumerate(plans):
        m0, m1 = place[a0], place[a1]
        waits[p, 0, 0].wait_recv()
        waits[p, 1].wait_recv()
        b.s1[u, :, :, :, lanes] = (
            wide(slab(u, a0, m0, lanes))
            + b.r0[u, 0, :, :, :, lanes].astype(F32)
            + b.r1[u, :, :, :, lanes].astype(F32)
        ).astype(BF)
        for k, turn in enumerate(turns):
            waits[p, 2, k] = net.start(
                slab1(u, turn(m1), lanes, leading),
                b.r2.at[u, k, :, :, lanes],
                device(a1, turn(m1)),
            )
    gain_step(2)
    for p, (u, lanes, f, f2, a0, a1, a2, leading) in enumerate(plans):
        m1, m2 = place[a1], place[a2]
        total = wide(slab1(u, m1, lanes, leading))
        for k in range(3):
            waits[p, 2, k].wait_recv()
            total = total + b.r2[u, k, :, :, lanes].astype(F32)
        b.s3[u, :, :, lanes] = total.astype(BF)
        for k, turn in enumerate(turns):
            waits[p, 3, k] = net.start(
                b.s3.at[u, turn(m2), :, lanes], b.r4.at[u, k, :, lanes], device(a2, turn(m2))
            )
    gain_step(3)
    for p, (u, lanes, f, f2, a0, a1, a2, leading) in enumerate(plans):
        total = b.s3[u, place[a2], :, lanes].astype(F32)
        for k in range(3):
            waits[p, 3, k].wait_recv()
            total = total + b.r4[u, k, :, lanes].astype(F32)
        b.full[u // 2, u % 2, :, lanes] = total
    swap = net.start(b.full.at[1 - here.core], out.at[here.core], twin)
    out[here.core] = b.full[here.core]
    gains[0].wait_recv()
    gain_out[...] = b.gain_sum[2] + b.gain_got[9]
    swap.wait_recv()
    for copy in returned:
        arrived(copy)
    keep_rows.wait()
    net.finish()


def layer(spans, q, do, tokens, norm_gain, key_w, value_w, cos, sin):
    vm = pl.BlockSpec(memory_space=VM)
    any_ = pl.BlockSpec(memory_space=pl.ANY)
    return pl.pallas_call(
        layer_kernel,
        name="layer",
        out_shape=(
            jax.ShapeDtypeStruct((2, 64, 2048), BF),
            jax.ShapeDtypeStruct((2, 64, 2048), BF),
            jax.ShapeDtypeStruct((128, 4096), BF),
            jax.ShapeDtypeStruct((2, 2, 16, 512), F32),
            jax.ShapeDtypeStruct((8, 128), F32),
        ),
        in_specs=[pl.BlockSpec(memory_space=pltpu.SMEM), any_, any_, vm, vm, any_, any_, vm, vm],
        out_specs=(any_,) * 3 + (vm,) * 2,
        scratch_shapes=[VM(*shape) for shape in SHAPES.values()]
        + [
            pltpu.SemaphoreType.DMA((N_COPIES,)),
            pltpu.SemaphoreType.DMA((N_COPIES,)),
            pltpu.SemaphoreType.DMA((12,)),
            pltpu.SemaphoreType.DMA((2 * PIECES,)),
        ],
        compiler_params=pltpu.CompilerParams(
            collective_id=1, has_side_effects=True, vmem_limit_bytes=60 * 1024 * 1024
        ),
    )(spans, q, do, tokens, norm_gain, key_w, value_w, cos, sin)


def finish_kernel(
    att, dq, rows, weights, gain, att_to, dq_to, rows_to, keys_to, values_to, gain_to,
    att_v, dq_v, rows_v, weights_v, gain_v, sems,
):
    here = Here()
    loads = []
    for k, (src, dst) in enumerate(
        ((gain, gain_v), (att, att_v), (dq, dq_v), (rows, rows_v), (weights, weights_v))
    ):
        copy = pltpu.make_async_copy(src, dst, sems.at[k])
        copy.start()
        loads.append(copy)
    loads[0].wait()
    row = gain_v[pl.ds(here.y * 2 + here.xh, 1), :]
    dp = here.xl * 2 + here.core
    gain_to[...] = pltpu.roll(row, (128 - dp * 32) % 128, 1)[:, :32]
    stores = []
    for k, (load, src, dst) in enumerate(
        (
            (loads[1], att_v, att_to),
            (loads[2], dq_v, dq_to),
            (loads[3], rows_v, rows_to),
            (loads[4], weights_v.at[0], keys_to),
            (None, weights_v.at[1], values_to),
        )
    ):
        if load is not None:
            load.wait()
        copy = pltpu.make_async_copy(src, dst, sems.at[5 + k])
        copy.start()
        stores.append(copy)
    for copy in stores:
        copy.wait()


def finish(att, dq, rows, weights, gain):
    any_ = pl.BlockSpec(memory_space=pl.ANY)
    return pl.pallas_call(
        finish_kernel,
        name="finish",
        out_shape=(
            jax.ShapeDtypeStruct((2, 64, 2048), BF),
            jax.ShapeDtypeStruct((2, 64, 2048), BF),
            jax.ShapeDtypeStruct((128, 4096), BF),
            jax.ShapeDtypeStruct((32, 512), F32),
            jax.ShapeDtypeStruct((32, 512), F32),
            jax.ShapeDtypeStruct((1, 32), F32),
        ),
        in_specs=[any_] * 5,
        out_specs=(any_,) * 5 + (pl.BlockSpec(memory_space=VM),),
        scratch_shapes=[
            VM((2, 64, 2048), BF),
            VM((2, 64, 2048), BF),
            VM((128, 4096), BF),
            VM((2, 32, 512), F32),
            VM((8, 128), F32),
            pltpu.SemaphoreType.DMA((10,)),
        ],
        compiler_params=pltpu.CompilerParams(vmem_limit_bytes=60 * 1024 * 1024),
    )(att, dq, rows, weights, gain)


def body(tokens, queries, d_attended, span_order, norm_gain, key_weight, value_weight):
    seqs, rows, width = tokens.shape
    count = seqs * rows
    half_dim = HEAD_DIM // 2
    span_len = rows // 2
    own_spans = lax.dynamic_slice_in_dim(span_order, lax.axis_index("ctx") * 2, 2, 0)
    own_pos = (own_spans[:, None] * span_len + jnp.arange(span_len, dtype=jnp.int32)).reshape(-1)
    frequency = ROPE_BASE ** (-2.0 * jnp.arange(half_dim, dtype=F32) / HEAD_DIM)
    angles = own_pos.astype(F32)[:, None] * frequency[None, :]
    attended, grad_queries, grad_rows, weights, gain = layer(
        span_order, queries, d_attended, tokens.reshape(count, width), norm_gain.reshape(1, width),
        key_weight, value_weight, jnp.cos(angles), jnp.sin(angles),
    )
    attended, grad_queries, grad_rows, grad_keys, grad_values, gain = finish(
        attended, grad_queries, grad_rows, weights.reshape(2, 32, 512), gain
    )
    return (
        attended,
        grad_queries,
        grad_rows.reshape(seqs, rows, width),
        grad_keys,
        grad_values,
        gain.reshape(32),
    )


def solution(mesh):
    placed = (P("dp", "ctx", None), P("dp", "ctx", None), P("dp", "ctx", None), P(), P(), P(), P())
    return jax.shard_map(
        body,
        mesh=mesh,
        in_specs=placed,
        out_specs=(
            P("dp", "ctx", None),
            P("dp", "ctx", None),
            P("dp", "ctx", None),
            P(("ctx", "dp"), None),
            P(("ctx", "dp"), None),
            P(("ctx", "dp")),
        ),
        check_vma=False,
    )
```

time: 634 us -> 118 us (0.19); the launches traced: 627 us -> 118 us
  waiting for transfers between devices: 304 us -> 0 us
  Pallas kernels: 0 us -> 116 us
  blocking collectives: 102 us -> 0 us
  matrix products: 97.4 us -> 0 us
  local copies, waits for them, and re-layouts: 64.4 us -> 0.08 us
  other arithmetic: 43.8 us -> 1.65 us
  between operations: 16 us -> 0.83 us
    unnamed x3 -> x0, waiting for transfers between devices: 201 us -> none
    pallas_call x0 -> x2, Pallas kernels: none -> 116 us  [the longest x1 113 us: layer(): pl.pallas_call(layer_kernel, name='layer', out_shape=(jax.ShapeDtypeStruc...]
    all_gather x1 -> x0, waiting for transfers between devices: 103 us -> none  [side_by_side(): out, at, done = (lax.all_gather(both, axis, axis=dim, tiled=True), 0, [])]
    all_to_all x1 -> x0, blocking collectives: 102 us -> none  [sent_and_summed(): lax.all_to_all(blocks, axis, split_axis=0, concat_axis=0, tiled=True)]
    dot_general x46 -> x0, matrix products: 69.4 us -> none  [the longest x8 21.6 us: attend_group(): jnp.einsum('gts,sd->tgd', probability_b, value_group, preferred_element_t...]
    sub x8 -> x0, matrix products: 27.9 us -> none  [attend_group(): exponent = jnp.exp(scores - row_max)]
    unnamed x210 -> x0, local copies, waits for them, and re-layouts: 24.5 us -> none
    convert_element_type x16 -> x1, other arithmetic: 19.3 us -> 0.07 us  [body(): angles = own_pos.astype(F32)[:, None] * frequency[None, :]]
  transfers between devices with their start and end apart: 2 -> 0, of which waited for: 2 -> 0; matrix products, arithmetic and copies ran while one was open for 2% -> 0% of each run, Pallas kernels for 0% -> 0%
where the time goes in v4:
time: 118 us
  Pallas kernels  116 us (98%)
  other arithmetic  1.65 us (1%)
    pallas_call x1, Pallas kernels, layer(): pl.pallas_call(layer_kernel, name='layer', out_shape=(jax.ShapeDtypeStruc...  113 us
    pallas_call x1, Pallas kernels, finish(): pl.pallas_call(finish_kernel, name='finish', out_shape=(jax.ShapeDtypeStr...  3.15 us

profile of v4, /device:TPU:1, one launch (start us, length us, event | category | flops | bytes accessed | tf_op | source)
XLA Modules:
  0.0 118.2 jit_solution(13844693466970891344)
XLA Ops:
  0.6 0.7 dynamic-slice_multiply_fusion
  1.4 0.1 add_convert_fusion
  1.4 0.1 convert_element_type.11
  1.5 0.8 multiply_sine_fusion
  2.4 112.5 %layer.1 = (bf16[2,64,2048]{2,1,0:T(8,128)(2,1)}, bf16[2,64,2048]{2,1,0:T(8,128)(2,1)}, bf16[128,4096]{1,0:T(8,128)(2,1)}, f32[2,2,16,512]{3,2,1,0:T(8,128)}, f32[8,128]{1,0:T(8,128)}) custom-call(s32[64]{0:T(128)} %spans.1, bf16[2,64,2048]{2,1,0:T(8,128)(2,1)} %q.1, bf16[2,64,2048]{2,1,0:T(8,128)(2,1)} %do.1, bf16[128,4096]{1,0:T(8,128)(2,1)} %bitcast.5, ...), custom_call_target="tpu_custom_call" | custom-call | tf_op jit(solution)/shard_map/layer/pallas_call | solution.py:650
  114.9 3.1 %finish.1 = (bf16[2,64,2048]{2,1,0:T(8,128)(2,1)}, bf16[2,64,2048]{2,1,0:T(8,128)(2,1)}, bf16[128,4096]{1,0:T(8,128)(2,1)}, f32[32,512]{1,0:T(8,128)}, f32[32,512]{1,0:T(8,128)}, /*index=5*/f32[1,32]{1,0:T(1,128)}) custom-call(bf16[2,64,2048]{2,1,0:T(8,128)(2,1)} %get-tuple-element.17.att, bf16[2,64,2048]{2,1,0:T(8,128)(2,1)} %get-tuple-element.18.dq, ...), custom_call_target="tpu_custom_call" | custom-call | tf_op jit(solution)/shard_map/finish/pallas_call | solution.py:712
  (1 shorter events, 0.0 us)

commit v5 on v4

--- a/solution.py
+++ b/solution.py
@@ -103,6 +103,7 @@
 )
 N_COPIES = 47 + 46 + 1 + 9 * len(PARTS) + 10 + 1
 SHAPES = dict(
+    tokens=((128, 4096), BF),
     kw=((4096, 512), BF),
     vw=((4096, 512), BF),
     normed=((128, 4096), BF),
@@ -113,12 +114,15 @@
     dr=((2, 4, 64, 512), BF),
     kvr=((2, 8, 4, 64, 256), BF),
     key_pos=((2, KEYS, 128), jnp.int32),
-    score=((KEYS, 256), F32),
-    prob=((KEYS, 256), BF),
+    score=((4, KEYS, 256), F32),
+    prob=((4, KEYS, 256), BF),
+    query_s=((4, 256, 128), BF),
+    grad_s=((4, 256, 128), BF),
+    grad_t=((4, 128, 256), BF),
+    stats=((4, 2, 8, 256), F32),
+    dq_t=((4, 128, 256), F32),
     key_t=((128, KEYS), BF),
     value_t=((128, KEYS), BF),
-    acc_k=((KEYS, 128), F32),
-    acc_v=((KEYS, 128), F32),
     att=((2, 4, 64, 512), BF),
     dq=((2, 4, 64, 512), BF),
     term=((2, 8, 4, 64, 256), BF),
@@ -153,13 +157,16 @@
 
 
 def layer_kernel(
-    spans, q, do, tokens, norm_gain, key_w, value_w, cos, sin,
+    spans, q, do, tokens_in, norm_gain, key_w, value_w, cos, sin,
     att_out, dq_out, rows_out, out, gain_out, *scratch,
 ):
     b = Box()
     for name, ref in zip(SHAPES, scratch):
         setattr(b, name, ref)
     send_sems, recv_sems, local_sems, weight_sems = scratch[len(SHAPES) :]
+    tokens = b.tokens
+    token_load = pltpu.make_async_copy(tokens_in, tokens, weight_sems.at[2 * PIECES])
+    token_load.start()
     here = Here()
     place = {"z": here.z, "y": here.y, "x": here.x}
     z, y, xh = here.z, here.y, here.xh
@@ -210,8 +217,8 @@
         else:
             copy.wait_recv()
 
-    for s in range(2):
-        send_rows(s, q, b.qr)
+    send_rows(0, q, b.qr)
+    token_load.wait()
     squares = jnp.zeros((128, 128), F32)
     for c in range(32):
         t = tokens[:, c * 128 : (c + 1) * 128].astype(F32)
@@ -256,7 +263,6 @@
                 net.start(b.kv.at[s, :, cols(to, 256)], b.kvr.at[s, mine[s], head[s]], along(s, to))
             )
         kv_in[s].append(keep(b.kv.at[s, :, cols(head[s], 256)], b.kvr.at[s, mine[s], head[s]]))
-    send_rows(0, do, b.dr)
     for c in range(32):
         at = slice(c * 128, (c + 1) * 128)
         b.norm_t[0, at, :] = b.normed[:, at].T
@@ -293,8 +299,7 @@
             spread(s, 1, half)
 
     gather_own(0)
-    gather_own(1)
-    norm_in = net.start(b.norm_t.at[0], b.norm_t.at[1], twin)
+    send_rows(0, do, b.dr)
     offset = lax.broadcasted_iota(jnp.int32, (32, 128), 0)
     for i in range(64):
         m, w, n, half = i // 16, (i // 8) % 2, (i // 2) % 4, i % 2
@@ -303,10 +308,12 @@
             span = spans[((zz * 4 + yy) * 2 + w) * 2 + half]
             b.key_pos[s, i * 32 : (i + 1) * 32, :] = offset + span * 32
     spread_on(0, 0)
-    send_rows(1, do, b.dr)
+    gather_own(1)
     gather_swapped(0)
     spread_on(0, 1)
-    spread_on(1, 0)
+    send_rows(1, q, b.qr)
+    send_rows(1, do, b.dr)
+    norm_in = net.start(b.norm_t.at[0], b.norm_t.at[1], twin)
 
     scale = HEAD_DIM ** (-0.5)
     to_two = scale * math.log2(math.e)
@@ -332,13 +339,30 @@
         both = ref[s, block]
         return jnp.concatenate([both[:, h * 128 : (h + 1) * 128] for h in range(4)], axis=0)
 
+    def side(k):
+        return 1 - xh if k == 0 else xh
+
+    def block_of(s, order):
+        return (flip1, flip3, flip2, lambda a: a)[order](head[s])
+
+    def give_back(s, order, src, dst):
+        block = block_of(s, order)
+        dst = dst.at[s, :, cols(head[s], 512)]
+        if order < 3:
+            returned.append(net.start(src.at[s, block], dst, along(s, block)))
+        else:
+            returned.append(keep(src.at[s, block], dst))
+
     def attention(s, order):
-        f = (flip1, flip3, flip2, lambda a: a)[order]
-        block = f(head[s])
+        block = block_of(s, order)
+        score, prob = b.score.at[order], b.prob.at[order]
         queries = stack(b.qr, s, block)
         grads = stack(b.dr, s, block)
         q_t = queries.T
         do_t = grads.T
+        b.query_s[order] = queries
+        b.grad_s[order] = grads
+        b.grad_t[order] = do_t
         start = (block * 4 + y) * 4 + xh * 2 if s == 0 else (z * 4 + block) * 4 + xh * 2
         column = lax.broadcasted_iota(jnp.int32, (1, 256), 1)
         q_pos = column % 32 + 32 * jnp.where(column % 64 < 32, spans[start], spans[start + 1])
@@ -348,59 +372,65 @@
             k_pos = b.key_pos[s, rows, :]
             k_pos = jnp.concatenate([k_pos, k_pos], axis=1)
             t = jnp.where(k_pos <= q_pos, t, -1e30)
-            b.score[rows, :] = t
+            score[rows, :] = t
             top = jnp.maximum(top, jnp.max(t.reshape(CHUNK // 8, 8, 256), axis=0))
         top = jnp.max(top, axis=0, keepdims=True)
         total = jnp.zeros((8, 256), F32)
         for rows in slots_of:
-            e = jnp.exp2((b.score[rows, :] - top) * to_two)
-            b.score[rows, :] = e
+            e = jnp.exp2((score[rows, :] - top) * to_two)
+            score[rows, :] = e
             total = total + jnp.sum(e.reshape(CHUNK // 8, 8, 256), axis=0)
         inverse = 1.0 / jnp.sum(total, axis=0, keepdims=True)
         out_t = jnp.zeros((128, 256), F32)
         for rows in slots_of:
-            p = (b.score[rows, :] * inverse).astype(BF)
-            b.prob[rows, :] = p
+            p = (score[rows, :] * inverse).astype(BF)
+            prob[rows, :] = p
             out_t = out_t + jnp.dot(b.value_t[:, rows], p, preferred_element_type=F32)
         out_t = out_t.astype(BF)
         delta = jnp.sum(out_t.astype(F32) * do_t.astype(F32), axis=0, keepdims=True)
-        dq_t = jnp.zeros((128, 256), F32)
-        for c, rows in enumerate(slots_of):
-            dp = jnp.dot(values_of(s, c), do_t, preferred_element_type=F32)
-            ds = (b.score[rows, :] * inverse * (dp - delta)).astype(BF)
-            k_term = jnp.dot(ds, queries, preferred_element_type=F32)
-            v_term = jnp.dot(b.prob[rows, :], grads, preferred_element_type=F32)
-            if order > 0:
-                k_term = k_term + b.acc_k[rows, :]
-                v_term = v_term + b.acc_v[rows, :]
-            if order < 3:
-                b.acc_k[rows, :] = k_term
-                b.acc_v[rows, :] = v_term
-            else:
-                b.term[s, c, :, :, :128] = (k_term * scale).astype(BF).reshape(4, 64, 128)
-                b.term[s, c, :, :, 128:] = v_term.astype(BF).reshape(4, 64, 128)
-            dq_t = dq_t + jnp.dot(b.key_t[:, rows], ds, preferred_element_type=F32)
+        b.stats[order, 0] = jnp.broadcast_to(inverse, (8, 256))
+        b.stats[order, 1] = jnp.broadcast_to(delta, (8, 256))
         attended = out_t.T
-        dq = (dq_t * scale).astype(BF).T
         for h in range(4):
-            at = slice(h * 64, (h + 1) * 64)
-            b.att[s, block, :, h * 128 : (h + 1) * 128] = attended[at]
-            b.dq[s, block, :, h * 128 : (h + 1) * 128] = dq[at]
-        for src, dst in ((b.att, att_out), (b.dq, dq_out)):
-            dst = dst.at[s, :, cols(head[s], 512)]
-            if order < 3:
-                returned.append(net.start(src.at[s, block], dst, along(s, block)))
-            else:
-                returned.append(keep(src.at[s, block], dst))
+            b.att[s, block, :, h * 128 : (h + 1) * 128] = attended[h * 64 : (h + 1) * 64]
+        give_back(s, order, b.att, att_out)
+
+    def gradients(s, k):
+        for c in range(4):
+            slot = c * 2 + side(k)
+            rows = pl.ds(pl.multiple_of(slot * CHUNK, CHUNK), CHUNK)
+            values = values_of(s, slot)
+            keys = b.key_t[:, rows]
+            k_term = jnp.zeros((CHUNK, 128), F32)
+            v_term = jnp.zeros((CHUNK, 128), F32)
+            for order in range(4):
+                inverse, delta = b.stats[order, 0, :1], b.stats[order, 1, :1]
+                dp = jnp.dot(values, b.grad_t[order], preferred_element_type=F32)
+                ds = (b.score[order, rows, :] * inverse * (dp - delta)).astype(BF)
+                k_term = k_term + jnp.dot(ds, b.query_s[order], preferred_element_type=F32)
+                v_term = v_term + jnp.dot(
+                    b.prob[order, rows, :], b.grad_s[order], preferred_element_type=F32
+                )
+                dq = jnp.dot(keys, ds, preferred_element_type=F32)
+                if k == 0 and c == 0:
+                    b.dq_t[order] = dq
+                else:
+                    b.dq_t[order] += dq
+            b.term[s, slot, :, :, :128] = (k_term * scale).astype(BF).reshape(4, 64, 128)
+            b.term[s, slot, :, :, 128:] = v_term.astype(BF).reshape(4, 64, 128)
+
+    def give_query_grads(s):
+        for order in range(4):
+            dq = (b.dq_t[order] * scale).astype(BF).T
+            for h in range(4):
+                b.dq[s, block_of(s, order), :, h * 128 : (h + 1) * 128] = dq[h * 64 : (h + 1) * 64]
+            give_back(s, order, b.dq, dq_out)
 
     flips = ((flip3, flip1), (flip1, flip3))
     one, two, three, owners = {}, {}, {}, [[], []]
 
     def half_of(half):
         return slice(2 * half, 2 * half + 2)
-
-    def side(k):
-        return 1 - xh if k == 0 else xh
 
     def sum_one(s, k):
         for j in (1, 0):
@@ -466,28 +496,35 @@
             ).astype(BF)
             b.grads[1, rows, at] = b.whole[s, h, :, 128:]
 
+    spread_on(1, 0)
     ready(0)
     attention(0, 0)
     gather_swapped(1)
     attention(0, 1)
+    attention(0, 2)
     spread_on(1, 1)
-    attention(0, 2)
     attention(0, 3)
+    gradients(0, 0)
     sum_one(0, 0)
+    gradients(0, 1)
     sum_one(0, 1)
+    give_query_grads(0)
     ready(1)
     attention(1, 0)
+    attention(1, 1)
     sum_two(0, 0)
+    attention(1, 2)
     sum_two(0, 1)
-    attention(1, 1)
+    attention(1, 3)
     sum_three(0)
-    attention(1, 2)
+    gradients(1, 0)
+    sum_one(1, 0)
     sum_four(0)
-    attention(1, 3)
-    sum_one(1, 0)
-    rotate_rows(0)
+    gradients(1, 1)
     sum_two(1, 0)
     sum_one(1, 1)
+    give_query_grads(1)
+    rotate_rows(0)
     sum_three(1)
     sum_two(1, 1)
     sum_four(1)
@@ -657,14 +694,14 @@
             jax.ShapeDtypeStruct((2, 2, 16, 512), F32),
             jax.ShapeDtypeStruct((8, 128), F32),
         ),
-        in_specs=[pl.BlockSpec(memory_space=pltpu.SMEM), any_, any_, vm, vm, any_, any_, vm, vm],
+        in_specs=[pl.BlockSpec(memory_space=pltpu.SMEM), any_, any_, any_, vm, any_, any_, vm, vm],
         out_specs=(any_,) * 3 + (vm,) * 2,
         scratch_shapes=[VM(*shape) for shape in SHAPES.values()]
         + [
             pltpu.SemaphoreType.DMA((N_COPIES,)),
             pltpu.SemaphoreType.DMA((N_COPIES,)),
             pltpu.SemaphoreType.DMA((12,)),
-            pltpu.SemaphoreType.DMA((2 * PIECES,)),
+            pltpu.SemaphoreType.DMA((2 * PIECES + 1,)),
         ],
         compiler_params=pltpu.CompilerParams(
             collective_id=1, has_side_effects=True, vmem_limit_bytes=60 * 1024 * 1024

time: 118 us -> 113 us (0.958)
  Pallas kernels: 116 us -> 110 us
    pallas_call x1, Pallas kernels: 113 us -> 107 us  [layer(): pl.pallas_call(layer_kernel, name='layer', out_shape=(jax.ShapeDtypeStruc...]
where the time goes in v5:
time: 113 us; the launch traced here: 112 us
  Pallas kernels  110 us (97%)
  other arithmetic  1.65 us (1%)
    pallas_call x1, Pallas kernels, layer(): pl.pallas_call(layer_kernel, name='layer', out_shape=(jax.ShapeDtypeStruc...  107 us
    pallas_call x1, Pallas kernels, finish(): pl.pallas_call(finish_kernel, name='finish', out_shape=(jax.ShapeDtypeStr...  3.15 us

profile of v5, /device:TPU:1, one launch (start us, length us, event | category | flops | bytes accessed | tf_op | source)
XLA Modules:
  0.0 112.4 jit_solution(5626514847157844420)
XLA Ops:
  0.6 0.7 dynamic-slice_multiply_fusion
  1.4 0.1 add_convert_fusion
  1.4 0.1 convert_element_type.11
  1.5 0.8 multiply_sine_fusion
  2.4 106.7 %layer.1 = (bf16[2,64,2048]{2,1,0:T(8,128)(2,1)}, bf16[2,64,2048]{2,1,0:T(8,128)(2,1)}, bf16[128,4096]{1,0:T(8,128)(2,1)}, f32[2,2,16,512]{3,2,1,0:T(8,128)}, f32[8,128]{1,0:T(8,128)}) custom-call(s32[64]{0:T(128)} %spans.1, bf16[2,64,2048]{2,1,0:T(8,128)(2,1)} %q.1, bf16[2,64,2048]{2,1,0:T(8,128)(2,1)} %do.1, bf16[128,4096]{1,0:T(8,128)(2,1)} %bitcast.5, ...), custom_call_target="tpu_custom_call" | custom-call | tf_op jit(solution)/shard_map/layer/pallas_call | solution.py:687
  109.1 3.1 %finish.1 = (bf16[2,64,2048]{2,1,0:T(8,128)(2,1)}, bf16[2,64,2048]{2,1,0:T(8,128)(2,1)}, bf16[128,4096]{1,0:T(8,128)(2,1)}, f32[32,512]{1,0:T(8,128)}, f32[32,512]{1,0:T(8,128)}, /*index=5*/f32[1,32]{1,0:T(1,128)}) custom-call(bf16[2,64,2048]{2,1,0:T(8,128)(2,1)} %get-tuple-element.17.att, bf16[2,64,2048]{2,1,0:T(8,128)(2,1)} %get-tuple-element.18.dq, ...), custom_call_target="tpu_custom_call" | custom-call | tf_op jit(solution)/shard_map/finish/pallas_call | solution.py:749
  (1 shorter events, 0.0 us)

commit v6 on v5

--- a/solution.py
+++ b/solution.py
@@ -101,7 +101,7 @@
     (3, 0, 256, "zyx", True),
     (3, 256, 256, "yxz", True),
 )
-N_COPIES = 47 + 46 + 1 + 9 * len(PARTS) + 10 + 1
+N_COPIES = 41 + 34 + 1 + 9 * len(PARTS) + 10 + 1
 SHAPES = dict(
     tokens=((128, 4096), BF),
     kw=((4096, 512), BF),
@@ -126,9 +126,7 @@
     att=((2, 4, 64, 512), BF),
     dq=((2, 4, 64, 512), BF),
     term=((2, 8, 4, 64, 256), BF),
-    got1=((2, 2, 2, 2, 2, 64, 256), BF),
-    sum1=((2, 2, 2, 2, 64, 256), BF),
-    got2=((2, 2, 2, 2, 64, 256), BF),
+    got1=((2, 3, 2, 4, 64, 256), BF),
     part=((2, 4, 64, 256), BF),
     got3=((2, 4, 64, 256), BF),
     final=((2, 4, 64, 256), BF),
@@ -184,14 +182,19 @@
     greet([here.at(**{a: f(place[a])}) for a in "zyx" for f in turns] + [twin])
     net = Net(send_sems, recv_sems)
 
+    seq = [here.core, 1 - here.core]
+
+    def either(s, a, b):
+        return a * (1 - seq[s]) + b * seq[s]
+
     def along(s, value):
-        return here.at(z=value) if s == 0 else here.at(y=value)
+        return here.at(z=either(s, value, z), y=either(s, y, value))
 
     def across(s, value):
-        return here.at(y=value) if s == 0 else here.at(z=value)
-
-    head = [z, y]
-    ring = [y, z]
+        return here.at(z=either(s, z, value), y=either(s, value, y))
+
+    head = [either(s, z, y) for s in range(2)]
+    ring = [either(s, y, z) for s in range(2)]
     mine = [ring[s] * 2 + xh for s in range(2)]
     local = []
 
@@ -207,9 +210,9 @@
         for f in turns:
             to = f(head[s])
             rows_in[s].append(
-                net.start(src.at[s, :, cols(to, 512)], dst.at[s, head[s]], along(s, to))
+                net.start(src.at[seq[s], :, cols(to, 512)], dst.at[s, head[s]], along(s, to))
             )
-        rows_in[s].append(keep(src.at[s, :, cols(head[s], 512)], dst.at[s, head[s]]))
+        rows_in[s].append(keep(src.at[seq[s], :, cols(head[s], 512)], dst.at[s, head[s]]))
 
     def arrived(copy):
         if any(copy is c for c in local):
@@ -260,43 +263,39 @@
         for f in (flip2, flip1, flip3):
             to = f(head[s])
             kv_in[s].append(
-                net.start(b.kv.at[s, :, cols(to, 256)], b.kvr.at[s, mine[s], head[s]], along(s, to))
+                net.start(
+                    b.kv.at[seq[s], :, cols(to, 256)], b.kvr.at[s, mine[s], head[s]], along(s, to)
+                )
             )
-        kv_in[s].append(keep(b.kv.at[s, :, cols(head[s], 256)], b.kvr.at[s, mine[s], head[s]]))
+        own = b.kv.at[seq[s], :, cols(head[s], 256)]
+        kv_in[s].append(keep(own, b.kvr.at[s, mine[s], head[s]]))
     for c in range(32):
         at = slice(c * 128, (c + 1) * 128)
         b.norm_t[0, at, :] = b.normed[:, at].T
 
-    first = {}
     last = [[], []]
     swapped = {}
 
-    def spread(s, of, half):
-        f = (flip1, flip3)[half]
-        block = b.kvr.at[s, ring[s] * 2 + (xh if of == 0 else 1 - xh), 2 * half : 2 * half + 2]
-        first[s, of, half] = net.start(block, block, across(s, f(ring[s])))
-
-    def spread_on(s, of):
-        for half, f, g in ((0, flip1, flip3), (1, flip3, flip1)):
-            first[s, of, half].wait_recv()
-            for value in (ring[s], f(ring[s])):
-                slot = value * 2 + (xh if of == 0 else 1 - xh)
-                block = b.kvr.at[s, slot, 2 * half : 2 * half + 2]
-                last[s].append(net.start(block, block, across(s, g(ring[s]))))
+    def half_of(half):
+        return slice(2 * half, 2 * half + 2)
+
+    def spread(s, of, rows):
+        block = b.kvr.at[s, ring[s] * 2 + (xh if of == 0 else 1 - xh), rows]
+        for f in (flip2, flip1, flip3):
+            last[s].append(net.start(block, block, across(s, f(ring[s]))))
 
     def gather_own(s):
         for copy in kv_in[s]:
             arrived(copy)
         for half in range(2):
-            block = b.kvr.at[s, mine[s], 2 * half : 2 * half + 2]
+            block = b.kvr.at[s, mine[s], half_of(half)]
             swapped[s, half] = net.start(block, block, here.at(x=x2))
-        for half in range(2):
-            spread(s, 0, half)
+        spread(s, 0, slice(0, 4))
 
     def gather_swapped(s):
         for half in range(2):
             swapped[s, half].wait_recv()
-            spread(s, 1, half)
+            spread(s, 1, half_of(half))
 
     gather_own(0)
     send_rows(0, do, b.dr)
@@ -304,13 +303,11 @@
     for i in range(64):
         m, w, n, half = i // 16, (i // 8) % 2, (i // 2) % 4, i % 2
         for s in range(2):
-            zz, yy = (n, m) if s == 0 else (m, n)
-            span = spans[((zz * 4 + yy) * 2 + w) * 2 + half]
+            at_z, at_y = ((n * 4 + m) * 2 + w) * 2 + half, ((m * 4 + n) * 2 + w) * 2 + half
+            span = spans[either(s, at_z, at_y)]
             b.key_pos[s, i * 32 : (i + 1) * 32, :] = offset + span * 32
-    spread_on(0, 0)
+    gather_swapped(0)
     gather_own(1)
-    gather_swapped(0)
-    spread_on(0, 1)
     send_rows(1, q, b.qr)
     send_rows(1, do, b.dr)
     norm_in = net.start(b.norm_t.at[0], b.norm_t.at[1], twin)
@@ -347,7 +344,7 @@
 
     def give_back(s, order, src, dst):
         block = block_of(s, order)
-        dst = dst.at[s, :, cols(head[s], 512)]
+        dst = dst.at[seq[s], :, cols(head[s], 512)]
         if order < 3:
             returned.append(net.start(src.at[s, block], dst, along(s, block)))
         else:
@@ -363,7 +360,7 @@
         b.query_s[order] = queries
         b.grad_s[order] = grads
         b.grad_t[order] = do_t
-        start = (block * 4 + y) * 4 + xh * 2 if s == 0 else (z * 4 + block) * 4 + xh * 2
+        start = either(s, (block * 4 + y) * 4, (z * 4 + block) * 4) + xh * 2
         column = lax.broadcasted_iota(jnp.int32, (1, 256), 1)
         q_pos = column % 32 + 32 * jnp.where(column % 64 < 32, spans[start], spans[start + 1])
         top = jnp.full((8, 256), -1e30, F32)
@@ -426,57 +423,30 @@
                 b.dq[s, block_of(s, order), :, h * 128 : (h + 1) * 128] = dq[h * 64 : (h + 1) * 64]
             give_back(s, order, b.dq, dq_out)
 
-    flips = ((flip3, flip1), (flip1, flip3))
-    one, two, three, owners = {}, {}, {}, [[], []]
-
-    def half_of(half):
-        return slice(2 * half, 2 * half + 2)
+    one, three, owners = {}, {}, [[], []]
 
     def sum_one(s, k):
-        for j in (1, 0):
-            for half in range(2):
-                f, g = flips[half]
-                target = f(ring[s])
-                slot = target if j == 0 else g(target)
-                one[s, half, j, k] = net.start(
-                    b.term.at[s, slot * 2 + side(k), half_of(half)],
-                    b.got1.at[s, half, j, k],
-                    across(s, target),
-                )
-
-    def sum_two(s, k):
-        for half in range(2):
-            f, g = flips[half]
-            one[s, half, 1, k].wait_recv()
-            b.sum1[s, half, k] = (
-                b.term[s, g(ring[s]) * 2 + side(k), half_of(half)].astype(F32)
-                + b.got1[s, half, 1, k].astype(F32)
-            ).astype(BF)
-            two[s, half, k] = net.start(
-                b.sum1.at[s, half, k], b.got2.at[s, half, k], across(s, g(ring[s]))
+        for i, f in enumerate((flip2, flip1, flip3)):
+            target = f(ring[s])
+            one[s, i, k] = net.start(
+                b.term.at[s, target * 2 + side(k)], b.got1.at[s, i, k], across(s, target)
             )
 
-    def summed(s, half, k):
-        one[s, half, 0, k].wait_recv()
-        two[s, half, k].wait_recv()
-        return (
-            b.term[s, ring[s] * 2 + side(k), half_of(half)].astype(F32)
-            + b.got1[s, half, 0, k].astype(F32)
-            + b.got2[s, half, k].astype(F32)
-        )
+    def summed(s, k):
+        total = b.term[s, ring[s] * 2 + side(k)].astype(F32)
+        for i in range(3):
+            one[s, i, k].wait_recv()
+            total = total + b.got1[s, i, k].astype(F32)
+        return total
 
     def sum_three(s):
-        for half in range(2):
-            at = half_of(half)
-            b.part[s, at] = summed(s, half, 0).astype(BF)
-            three[s, half] = net.start(b.part.at[s, at], b.got3.at[s, at], here.at(x=x2))
+        b.part[s] = summed(s, 0).astype(BF)
+        three[s] = net.start(b.part.at[s], b.got3.at[s], here.at(x=x2))
 
     def sum_four(s):
-        for half in range(2):
-            at = half_of(half)
-            total = summed(s, half, 1)
-            three[s, half].wait_recv()
-            b.final[s, at] = (total + b.got3[s, at].astype(F32)).astype(BF)
+        total = summed(s, 1)
+        three[s].wait_recv()
+        b.final[s] = (total + b.got3[s].astype(F32)).astype(BF)
         for f in (flip2, flip1, flip3):
             to = f(head[s])
             owners[s].append(
@@ -487,7 +457,7 @@
     def rotate_rows(s):
         for copy in owners[s]:
             copy.wait_recv()
-        rows = slice(s * 64, (s + 1) * 64)
+        rows = pl.ds(pl.multiple_of(seq[s] * 64, 64), 64)
         for h in range(KV_HEADS):
             at = slice(h * 128, (h + 1) * 128)
             u = b.whole[s, h, :, :128].astype(F32)
@@ -496,13 +466,11 @@
             ).astype(BF)
             b.grads[1, rows, at] = b.whole[s, h, :, 128:]
 
-    spread_on(1, 0)
     ready(0)
     attention(0, 0)
     gather_swapped(1)
     attention(0, 1)
     attention(0, 2)
-    spread_on(1, 1)
     attention(0, 3)
     gradients(0, 0)
     sum_one(0, 0)
@@ -512,21 +480,17 @@
     ready(1)
     attention(1, 0)
     attention(1, 1)
-    sum_two(0, 0)
     attention(1, 2)
-    sum_two(0, 1)
+    sum_three(0)
     attention(1, 3)
-    sum_three(0)
     gradients(1, 0)
     sum_one(1, 0)
     sum_four(0)
     gradients(1, 1)
-    sum_two(1, 0)
     sum_one(1, 1)
+    sum_three(1)
     give_query_grads(1)
     rotate_rows(0)
-    sum_three(1)
-    sum_two(1, 1)
     sum_four(1)
     rotate_rows(1)
 

time: 113 us -> 105 us (0.929)
  Pallas kernels: 110 us -> 102 us
    pallas_call x1, Pallas kernels: 107 us -> 98.8 us  [layer(): pl.pallas_call(layer_kernel, name='layer', out_shape=(jax.ShapeDtypeStruc...]
where the time goes in v6:
time: 105 us
  Pallas kernels  102 us (97%)
  other arithmetic  1.65 us (2%)
    pallas_call x1, Pallas kernels, layer(): pl.pallas_call(layer_kernel, name='layer', out_shape=(jax.ShapeDtypeStruc...  98.8 us
    pallas_call x1, Pallas kernels, finish(): pl.pallas_call(finish_kernel, name='finish', out_shape=(jax.ShapeDtypeStr...  3.15 us

profile of v6, /device:TPU:1, one launch (start us, length us, event | category | flops | bytes accessed | tf_op | source)
XLA Modules:
  0.0 104.5 jit_solution(14754854981245656296)
XLA Ops:
  0.6 0.7 dynamic-slice_multiply_fusion
  1.4 0.1 add_convert_fusion
  1.4 0.1 convert_element_type.11
  1.5 0.8 multiply_sine_fusion
  2.4 98.8 %layer.1 = (bf16[2,64,2048]{2,1,0:T(8,128)(2,1)}, bf16[2,64,2048]{2,1,0:T(8,128)(2,1)}, bf16[128,4096]{1,0:T(8,128)(2,1)}, f32[2,2,16,512]{3,2,1,0:T(8,128)}, f32[8,128]{1,0:T(8,128)}) custom-call(s32[64]{0:T(128)} %spans.1, bf16[2,64,2048]{2,1,0:T(8,128)(2,1)} %q.1, bf16[2,64,2048]{2,1,0:T(8,128)(2,1)} %do.1, bf16[128,4096]{1,0:T(8,128)(2,1)} %bitcast.5, ...), custom_call_target="tpu_custom_call" | custom-call | tf_op jit(solution)/shard_map/layer/pallas_call | solution.py:651
  101.2 3.1 %finish.1 = (bf16[2,64,2048]{2,1,0:T(8,128)(2,1)}, bf16[2,64,2048]{2,1,0:T(8,128)(2,1)}, bf16[128,4096]{1,0:T(8,128)(2,1)}, f32[32,512]{1,0:T(8,128)}, f32[32,512]{1,0:T(8,128)}, /*index=5*/f32[1,32]{1,0:T(1,128)}) custom-call(bf16[2,64,2048]{2,1,0:T(8,128)(2,1)} %get-tuple-element.17.att, bf16[2,64,2048]{2,1,0:T(8,128)(2,1)} %get-tuple-element.18.dq, ...), custom_call_target="tpu_custom_call" | custom-call | tf_op jit(solution)/shard_map/finish/pallas_call | solution.py:713
  (1 shorter events, 0.0 us)

commit v7 on v6

--- a/solution.py
+++ b/solution.py
@@ -298,7 +298,6 @@
             spread(s, 1, half_of(half))
 
     gather_own(0)
-    send_rows(0, do, b.dr)
     offset = lax.broadcasted_iota(jnp.int32, (32, 128), 0)
     for i in range(64):
         m, w, n, half = i // 16, (i // 8) % 2, (i // 2) % 4, i % 2
@@ -307,10 +306,8 @@
             span = spans[either(s, at_z, at_y)]
             b.key_pos[s, i * 32 : (i + 1) * 32, :] = offset + span * 32
     gather_swapped(0)
+    send_rows(0, do, b.dr)
     gather_own(1)
-    send_rows(1, q, b.qr)
-    send_rows(1, do, b.dr)
-    norm_in = net.start(b.norm_t.at[0], b.norm_t.at[1], twin)
 
     scale = HEAD_DIM ** (-0.5)
     to_two = scale * math.log2(math.e)
@@ -467,6 +464,9 @@
             b.grads[1, rows, at] = b.whole[s, h, :, 128:]
 
     ready(0)
+    send_rows(1, q, b.qr)
+    send_rows(1, do, b.dr)
+    norm_in = net.start(b.norm_t.at[0], b.norm_t.at[1], twin)
     attention(0, 0)
     gather_swapped(1)
     attention(0, 1)

time: 105 us -> 107 us (1.019)
  Pallas kernels: 102 us -> 104 us
    pallas_call x1, Pallas kernels: 98.8 us -> 101 us  [layer(): pl.pallas_call(layer_kernel, name='layer', out_shape=(jax.ShapeDtypeStruc...]
where the time goes in v7:
time: 107 us
  Pallas kernels  104 us (97%)
  other arithmetic  1.65 us (2%)
    pallas_call x1, Pallas kernels, layer(): pl.pallas_call(layer_kernel, name='layer', out_shape=(jax.ShapeDtypeStruc...  101 us
    pallas_call x1, Pallas kernels, finish(): pl.pallas_call(finish_kernel, name='finish', out_shape=(jax.ShapeDtypeStr...  3.15 us

profile of v7, /device:TPU:1, one launch (start us, length us, event | category | flops | bytes accessed | tf_op | source)
XLA Modules:
  0.0 106.5 jit_solution(4643601664879887746)
XLA Ops:
  0.6 0.7 dynamic-slice_multiply_fusion
  1.4 0.1 add_convert_fusion
  1.4 0.1 convert_element_type.11
  1.5 0.8 multiply_sine_fusion
  2.4 100.8 %layer.1 = (bf16[2,64,2048]{2,1,0:T(8,128)(2,1)}, bf16[2,64,2048]{2,1,0:T(8,128)(2,1)}, bf16[128,4096]{1,0:T(8,128)(2,1)}, f32[2,2,16,512]{3,2,1,0:T(8,128)}, f32[8,128]{1,0:T(8,128)}) custom-call(s32[64]{0:T(128)} %spans.1, bf16[2,64,2048]{2,1,0:T(8,128)(2,1)} %q.1, bf16[2,64,2048]{2,1,0:T(8,128)(2,1)} %do.1, bf16[128,4096]{1,0:T(8,128)(2,1)} %bitcast.5, ...), custom_call_target="tpu_custom_call" | custom-call | tf_op jit(solution)/shard_map/layer/pallas_call | solution.py:651
  103.2 3.1 %finish.1 = (bf16[2,64,2048]{2,1,0:T(8,128)(2,1)}, bf16[2,64,2048]{2,1,0:T(8,128)(2,1)}, bf16[128,4096]{1,0:T(8,128)(2,1)}, f32[32,512]{1,0:T(8,128)}, f32[32,512]{1,0:T(8,128)}, /*index=5*/f32[1,32]{1,0:T(1,128)}) custom-call(bf16[2,64,2048]{2,1,0:T(8,128)(2,1)} %get-tuple-element.17.att, bf16[2,64,2048]{2,1,0:T(8,128)(2,1)} %get-tuple-element.18.dq, ...), custom_call_target="tpu_custom_call" | custom-call | tf_op jit(solution)/shard_map/finish/pallas_call | solution.py:713
  (1 shorter events, 0.0 us)
